TPU v7x, 32 devices: a whole 2x2x4 slice. The times are simulated.
32 devices in a mesh: head: 8 (over z, x), client: 4 (over y, core).
Axes of the slice: x: 2, y: 2, z: 4, core: 2. Of those that a mesh axis runs over, the one named last changes fastest.
Arguments:
- client_ids: int32 [32], replicated, may hold values from 0 to 127, as said below
- client_table: bfloat16 [128, 256], replicated, may hold values from -6 to 6
- in_weight: bfloat16 [256, 4096], P(None, 'client'), may hold values from -0.375 to 0.375
- in_bias: float32 [4096], P('client'), may hold values from -3 to 3
- head_weight: bfloat16 [4096, 131072], P('client', 'head'), may hold values from -0.09375 to 0.09375
- tokens: int32 [32, 256], P(('head', 'client')), may hold values from 0 to 255
- labels: int32 [32, 256], P(('head', 'client')), may hold values from 0 to 255
- byte_table: bfloat16 [256, 4096], P(None, 'client'), may hold values from -5.5 to 6.7
- out_table: bfloat16 [256, 4096], P(None, 'client'), may hold values from -5.625 to 5.625
Outputs:
- head_grad: bfloat16 [4096, 131072], P('client', 'head')
- in_grad: float32 [256, 4096], P(None, 'client')
- losses: float32 [32], P(('head', 'client'))
Inputs may be any that keep to these rules, and one draw needn't show every extreme that they name: `client_ids`: distinct population indices.
All inputs are finite; a program needn't handle non-finite values.
Results may differ from a plain program's by a relative error of at most 0.0085.
Values may be sent and summed in bfloat16 or wider, within the bound.
No kernel may reach another device: no remote copies, remote signals or barrier semaphores. Data moves between devices by JAX's collectives and lax.ppermute only.
A program may use at most 128 MiB of HBM per device.

v0:
```python
import jax
import jax.numpy as jnp
from jax import lax
from jax.sharding import PartitionSpec as P

EPSILON = 1e-06
learn_rate = 0.1


def client_loss(factor_a, factor_b, inputs, label_row, out_table):
    depth = factor_a.shape[0]
    rank_size = factor_a.shape[1]
    normed_in = inputs * lax.rsqrt(jnp.mean(inputs * inputs, -1, keepdims=True) + EPSILON)
    low_rank = jnp.dot(normed_in, factor_a, precision=lax.Precision.HIGHEST)
    adapted = inputs + jnp.dot(low_rank, factor_b, precision=lax.Precision.HIGHEST) / jnp.sqrt(
        jnp.float32(depth * rank_size)
    )
    normed = (adapted * lax.rsqrt(jnp.mean(adapted * adapted, -1, keepdims=True) + EPSILON)).astype(
        jnp.bfloat16
    )
    logits = lax.dot_general(
        normed, out_table, (((1,), (1,)), ((), ())), preferred_element_type=jnp.float32
    )
    logits = logits * (4.0 / jnp.sqrt(jnp.float32(depth)))
    log_total = jax.nn.logsumexp(logits, -1)
    vocab_ids = lax.broadcasted_iota(jnp.int32, logits.shape, 1)
    picked = jnp.sum(jnp.where(vocab_ids == label_row[:, None], logits, 0.0), -1)
    return jnp.sum(log_total - picked)


def train_client(factor_row, token_row, label_row, byte_table, out_table):
    depth = byte_table.shape[1]
    split_at = factor_row.shape[0] // 2
    rank_size = split_at // depth
    start_a = factor_row[:split_at].reshape(depth, rank_size).astype(jnp.float32)
    start_b = factor_row[split_at:].reshape(rank_size, depth).astype(jnp.float32)
    onehot = (
        token_row[:, None]
        == lax.broadcasted_iota(jnp.int32, (token_row.shape[0], byte_table.shape[0]), 1)
    ).astype(jnp.bfloat16)
    inputs = jnp.dot(onehot, byte_table, preferred_element_type=jnp.float32)
    loss_grad = jax.value_and_grad(client_loss, argnums=(0, 1))
    first_loss, (grad_a, grad_b) = loss_grad(start_a, start_b, inputs, label_row, out_table)
    middle_a = start_a - learn_rate * grad_a
    middle_b = start_b - learn_rate * grad_b
    second_loss, (grad_a, grad_b) = loss_grad(middle_a, middle_b, inputs, label_row, out_table)
    final_a = middle_a - learn_rate * grad_a
    final_b = middle_b - learn_rate * grad_b
    deltas = jnp.concatenate(
        [(final_a - start_a).reshape(-1), (final_b - start_b).reshape(-1)]
    ).astype(jnp.bfloat16)
    return (deltas, first_loss / token_row.shape[0])


def local(
    client_ids, client_table, in_weight, in_bias, head_weight, tokens, labels, byte_table, out_table
):
    head_count = lax.axis_size("head")
    group_count = lax.axis_size("client")
    per_device = tokens.shape[0]
    byte_full, out_full = (
        lax.all_gather(byte_table, "client", axis=1, tiled=True),
        lax.all_gather(out_table, "client", axis=1, tiled=True),
    )
    ordered = client_ids.reshape(head_count, group_count, per_device).transpose(1, 0, 2).reshape(-1)
    chosen = client_table[ordered]
    preact = jnp.dot(chosen, in_weight, preferred_element_type=jnp.float32) + in_bias
    hidden = jnp.maximum(preact, 0.0).astype(jnp.bfloat16)
    hidden_rows = hidden
    summed = lax.psum_scatter(
        jnp.dot(hidden_rows, head_weight, preferred_element_type=jnp.float32),
        "client",
        scatter_dimension=0,
        tiled=True,
    )
    owned = lax.all_to_all(
        summed.astype(jnp.bfloat16), "head", split_axis=0, concat_axis=1, tiled=True
    )

    def run_client(record):
        return train_client(record[0], record[1], record[2], byte_full, out_full)

    deltas, losses = lax.map(run_client, (owned, tokens, labels))
    returned = lax.all_to_all(deltas, "head", split_axis=1, concat_axis=0, tiled=True)
    received = lax.all_gather(returned, "client", axis=0, tiled=True)
    hidden_rows = hidden
    grad_sum = lax.dot_general(
        hidden_rows, received, (((0,), (0,)), ((), ())), preferred_element_type=jnp.float32
    )
    partial_value = lax.dot_general(
        received, head_weight, (((1,), (1,)), ((), ())), preferred_element_type=jnp.float32
    )
    hidden_back = partial_value
    grad_sum, hidden_back = (grad_sum, hidden_back)
    hidden_back = lax.psum(hidden_back, "head")
    masked = jnp.where(preact > 0, hidden_back, 0.0)
    in_grad = lax.dot_general(
        chosen.astype(jnp.float32),
        masked,
        (((0,), (0,)), ((), ())),
        precision=lax.Precision.HIGHEST,
    )
    return (grad_sum.astype(jnp.bfloat16), in_grad, losses)


def solution(mesh):
    placed = (
        P(),
        P(),
        P(None, "client"),
        P("client"),
        P("client", "head"),
        P(("head", "client"), None),
        P(("head", "client"), None),
        P(None, "client"),
        P(None, "client"),
    )
    return jax.shard_map(
        local,
        mesh=mesh,
        in_specs=placed,
        out_specs=(P("client", "head"), P(None, "client"), P(("head", "client"))),
        check_vma=False,
    )
```

profile of v0, /device:TPU:0, one launch (start us, length us, event | category | flops | bytes accessed | tf_op | source)
XLA Modules:
  0.0 274.2 jit_solution(7337150185194927193)
XLA Ops:
  7.2 0.0 reduce-scatter.2.cloned.1.call-start
  7.2 0.8 reshape.166
  8.0 0.1 copy.22
  8.1 0.1 reshape.167
  8.2 1.5 gather_fusion
  9.7 0.9 convolution_add_fusion
  10.5 14.9 %fusion.59 = f32[32,16384]{1,0:T(8,128)} fusion(bf16[1024,16384]{1,0:T(8,128)(2,1)} %param.13, f32[32,1024]{1,0:T(8,128)S(1)} %convolution_add_fusion), kind=kOutput, calls=%fused_computation.91 | convolution fusion | flops 1073807360 | bytes 35782656 | tf_op jit(solution)/shard_map/dot_general | solution.py:71
  25.4 0.0 reduce-scatter.2.cloned.1.call-update
  25.4 0.0 all-gather.5.cloned.1.call-start
  25.5 0.7 all-gather.5.cloned.1.call-update
  26.2 0.0 all-gather.7.cloned.1.call-start
  26.2 0.7 all-gather.7.cloned.1.call-update
  26.9 32.6 %reduce-scatter.2.cloned.1.call-done = f32[8,16384]{1,0:T(8,128)} async-done(((f32[32,16384]{1,0:T(8,128)}), f32[8,16384]{1,0:T(8,128)}) %reduce-scatter.2.cloned.1.call-update) | async-done | bytes 524304 | tf_op jit(solution)/shard_map/reduce_scatter | solution.py:70
  59.5 1.1 convert_bitcast_fusion
  60.6 0.5 broadcast.217
  61.1 0.8 reduce.4
  61.9 0.9 reshape.181
  62.8 5.5 %all-to-all-start = ((bf16[8,2,8192]{2,1,0:T(2,128)(2,1)}), bf16[8,2,8192]{2,1,0:T(2,128)(2,1)S(1)}, u32[]{:S(2)}, u32[]{:S(2)}) async-start(bf16[8,2,8192]{2,1,0:T(2,128)(2,1)} %reshape.181), calls=%async_computation.1 | async-start | bytes 524288 | tf_op jit(solution)/shard_map/all_to_all | solution.py:76
  68.3 0.0 all-gather.9.cloned.1.call-start
  68.3 15.3 %all-gather.5.cloned.1.call-done = bf16[256,4096]{1,0:T(8,128)(2,1)} async-done(((bf16[256,1024]{1,0:T(8,128)(2,1)}), bf16[256,4096]{1,0:T(8,128)(2,1)}) %all-gather.5.cloned.1.call-update) | async-done | bytes 2097168 | tf_op jit(solution)/shard_map/all_gather | solution.py:62
  83.7 4.4 %multiply_reduce_fusion.2 = (f32[256]{0:T(256)S(1)}, f32[256,4096]{1,0:T(8,128)}) fusion(bf16[256,4096]{1,0:T(8,128)(2,1)} %all-gather.5.cloned.1.call-done, s32[256]{0:T(256)S(1)} %bitcast.43), kind=kOutput, calls=%fused_computation.34 | convolution fusion | flops 539033344 | bytes 6293504 | tf_op jit(solution)/shard_map/while/body/eval_jaxpr/dot_general | solution.py:41
  88.0 0.5 reshape.182
  88.5 1.2 slice_reduce_fusion
  89.7 0.8 reshape.168
  90.4 0.1 reshape.169
  90.5 0.3 copy.24
  90.9 4.8 %fusion.18 = f32[256,16]{0,1:T(8,128)S(1)} fusion(bf16[4096,16]{1,0:T(8,128)(2,1)S(1)} %reshape.168, f32[256,4096]{1,0:T(8,128)} %get-tuple-element.34, f32[256]{0:T(256)S(1)} %add_rsqrt_fusion), kind=kOutput, calls=%fused_computation.39 | convolution fusion | flops 202375168 | bytes 4342784 | tf_op jit(solution)/shard_map/while/body/eval_jaxpr/jvp()/dot_general | solution.py:14
  95.7 0.0 copy-done.2
  95.7 4.3 %multiply_reduce_fusion.1 = (f32[256]{0:T(256)S(1)}, f32[256,4096]{1,0:T(8,128)}) fusion(f32[256,4096]{1,0:T(8,128)S(1)} %copy-done.2, f32[256,16]{0,1:T(8,128)S(1)} %fusion.18, bf16[16,4096]{1,0:T(8,128)(2,1)S(1)} %reshape.169), kind=kOutput, calls=%fused_computation.33 | convolution fusion | flops 205520640 | bytes 8537088 | tf_op jit(solution)/shard_map/while/body/eval_jaxpr/jvp()/dot_general | solution.py:15
  100.0 7.8 %all-gather.7.cloned.1.call-done = bf16[256,4096]{1,0:T(8,128)(2,1)} async-done(((bf16[256,1024]{1,0:T(8,128)(2,1)}), bf16[256,4096]{1,0:T(8,128)(2,1)}) %all-gather.7.cloned.1.call-update) | async-done | bytes 2097168 | tf_op jit(solution)/shard_map/all_gather | solution.py:63
  107.8 3.8 %fusion.78 = (f32[256]{0:T(256)S(1)}, f32[256,256]{0,1:T(8,128)S(1)}) fusion(bf16[256,4096]{1,0:T(8,128)(2,1)} %all-gather.7.cloned.1.call-done, f32[256,4096]{1,0:T(8,128)} %get-tuple-element.36, f32[256]{0:T(256)S(1)} %fusion.60), kind=kOutput, calls=%fused_computation.118 | convolution fusion | flops 539098880 | bytes 6555648 | tf_op jit(solution)/shard_map/while/body/eval_jaxpr/jvp()/dot_general | solution.py:21
  111.7 0.1 select_reduce_fusion
  111.8 0.6 subtract_reduce_fusion
  112.4 0.1 copy-done.5
  112.5 0.9 fusion.10
  113.5 2.8 %fusion.76 = f32[256,16]{0,1:T(8,128)S(1)} fusion(bf16[16,4096]{1,0:T(8,128)(2,1)S(1)} %reshape.169, bf16[256,4096]{1,0:T(8,128)(2,1)S(1)} %get-tuple-element.40, f32[256,4096]{1,0:T(8,128)S(1)} %copy-done.4, f32[256]{0:T(256)S(1)} %multiply_multiply_fusion.1, f32[256]{0:T(256)S(1)} %fusion.60), kind=kOutput, calls=%fused_computation.117 | convolution fusion | flops 207618048 | bytes 6440960 | tf_op jit(solution)/shard_map/while/body/eval_jaxpr/transpose(jvp())/dot_general | solution.py:15
  116.3 0.0 copy-start.3
  116.3 3.1 %fusion.6 = f32[16,4096]{1,0:T(8,128)S(1)} fusion(f32[256,16]{0,1:T(8,128)S(1)} %fusion.18, bf16[16,4096]{1,0:T(8,128)(2,1)S(1)} %reshape.169, bf16[256,4096]{1,0:T(8,128)(2,1)S(1)} %get-tuple-element.40, f32[256,4096]{1,0:T(8,128)S(1)} %copy-done.4, f32[256]{0:T(256)S(1)} %multiply_multiply_fusion.1, f32[256]{0:T(256)S(1)} %fusion.60), kind=kOutput, calls=%fused_computation.21 | convolution fusion | flops 207814656 | bytes 6703104 | tf_op jit(solution)/shard_map/while/body/eval_jaxpr/transpose(jvp())/dot_general | solution.py:15
  119.5 2.5 fusion.7
  122.0 3.4 %fusion.15 = f32[256,16]{0,1:T(8,128)S(1)} fusion(f32[4096,16]{0,1:T(8,128)S(1)} %fusion.7, f32[256,4096]{1,0:T(8,128)S(1)} %copy-done.3, f32[256]{0:T(256)S(1)} %add_rsqrt_fusion), kind=kOutput, calls=%fused_computation.36 | convolution fusion | flops 202375168 | bytes 4473856 | tf_op jit(solution)/shard_map/while/body/eval_jaxpr/jvp()/dot_general | solution.py:14
  125.4 4.1 %multiply_reduce_fusion = (f32[256]{0:T(256)S(1)}, f32[256,4096]{1,0:T(8,128)S(1)}) fusion(f32[256,4096]{1,0:T(8,128)S(1)} %copy-done.3, f32[256,16]{0,1:T(8,128)S(1)} %fusion.15, f32[16,4096]{1,0:T(8,128)S(1)} %fusion.6), kind=kOutput, calls=%fused_computation.31 | convolution fusion | flops 205520640 | bytes 8668160 | tf_op jit(solution)/shard_map/while/body/eval_jaxpr/jvp()/dot_general | solution.py:15
  129.5 0.9 fusion.79
  130.4 0.1 fusion.41
  130.5 0.9 fusion.11
  131.4 4.4 %fusion.73 = f32[256,16]{0,1:T(8,128)S(1)} fusion(f32[16,4096]{1,0:T(8,128)S(1)} %fusion.6, bf16[256,4096]{1,0:T(8,128)(2,1)S(1)} %get-tuple-element.46, f32[256,4096]{1,0:T(8,128)S(1)} %get-tuple-element.42, f32[256]{0:T(256)S(1)} %multiply_multiply_fusion, f32[256]{0:T(256)S(1)} %fusion.61), kind=kOutput, calls=%fused_computation.116 | convolution fusion | flops 207618048 | bytes 6572032 | tf_op jit(solution)/shard_map/while/body/eval_jaxpr/transpose(jvp())/dot_general | solution.py:15
  135.8 2.9 %fusion.9 = bf16[16,4096]{1,0:T(8,128)(2,1)S(1)} fusion(f32[16,4096]{1,0:T(8,128)S(1)} %fusion.6, f32[256,16]{0,1:T(8,128)S(1)} %fusion.15, bf16[16,4096]{1,0:T(8,128)(2,1)S(1)} %reshape.169, bf16[256,4096]{1,0:T(8,128)(2,1)S(1)} %get-tuple-element.46, f32[256,4096]{1,0:T(8,128)S(1)} %get-tuple-element.42, f32[256]{0:T(256)S(1)} %multiply_multiply_fusion, ...), kind=kOutput, calls=%fused_computation.25 | convolution fusion | flops 207945728 | bytes 6834176 | tf_op jit(solution)/shard_map/while/body/eval_jaxpr/transpose(jvp())/dot_general | solution.py:15
  138.8 2.5 fusion.8
  141.3 0.5 copy.25
  141.8 1.2 concatenate.17
  143.0 0.2 concatenate.18
  143.1 0.1 pad_maximum_fusion
  143.3 0.4 copy.29
  143.7 2.2 reduce.5
  145.9 0.2 reshape.183
  146.1 14.8 %all_to_all.26 = bf16[8,2,8192]{2,1,0:T(2,128)(2,1)S(1)} all-to-all(bf16[8,2,8192]{2,1,0:T(2,128)(2,1)S(1)} %reshape.183), channel_id=1, replica_groups=mesh['head'=8,'client'=4] {'head'}, dimensions={0} | all-to-all | bytes 524288 | tf_op jit(solution)/shard_map/all_to_all | solution.py:84
  160.9 0.3 reshape.184
  161.1 1.0 copy.27
  162.2 0.0 all-reduce.2.cloned.1.call-start
  162.8 14.3 %all-gather.9.cloned.1.call-done = bf16[1,32,16384]{2,1,0:T(8,128)(2,1)} async-done(((bf16[1,8,16384]{2,1,0:T(8,128)(2,1)}), bf16[1,32,16384]{2,1,0:T(8,128)(2,1)}) %all-gather.9.cloned.1.call-update) | async-done | bytes 1048592 | tf_op jit(solution)/shard_map/all_gather | solution.py:85
  177.1 16.1 %fusion.30 = f32[32,1024]{1,0:T(8,128)} fusion(bf16[1024,16384]{1,0:T(8,128)(2,1)} %param.13, bf16[1,32,16384]{2,1,0:T(8,128)(2,1)} %all-gather.9.cloned.1.call-done), kind=kOutput, calls=%fused_computation.52 | convolution fusion | flops 1073741824 | bytes 34734080 | tf_op jit(solution)/shard_map/dot_general | solution.py:90
  193.2 0.0 all-reduce.2.cloned.1.call-update
  193.2 14.9 %convolution_convert_fusion = bf16[1024,16384]{1,0:T(8,128)(2,1)} fusion(bf16[1,32,16384]{2,1,0:T(8,128)(2,1)S(1)} %copy-done.6, f32[32,1024]{1,0:T(8,128)S(1)} %convolution_add_fusion), kind=kOutput, calls=%fused_computation.1 | convolution fusion | flops 1090584576 | bytes 34734080 | tf_op jit(solution)/shard_map/dot_general | solution.py:87
  208.1 55.7 %all-reduce.2.cloned.1.call-done = f32[32,1024]{1,0:T(8,128)} async-done(((f32[32,1024]{1,0:T(8,128)}), f32[32,1024]{1,0:T(8,128)}) %all-reduce.2.cloned.1.call-update) | async-done | bytes 131088 | tf_op jit(solution)/shard_map/psum | solution.py:95
  263.8 2.5 fusion.42
  (27 shorter events, 0.1 us)
Async XLA Ops:
  7.2 2.5 copy-start
  7.2 52.3 %reduce-scatter.2.cloned.1.call-start = ((), (), s32[]{:S(2)}) async-start(), calls=%async_computation.3 | async-start | bytes 2621440 | tf_op jit(solution)/shard_map/reduce_scatter | solution.py:70
  25.4 58.2 %copy-start.7 = (s32[1,256]{1,0:T(1,128)S(1)}, s32[1,256]{1,0:T(1,128)}, u32[]{:S(2)}) copy-start(s32[1,256]{1,0:T(1,128)} %param.14) | copy-start | bytes 3076
  25.4 58.2 %all-gather.5.cloned.1.call-start = ((), (), s32[]{:S(2)}) async-start(), calls=%async_computation.4 | async-start | bytes 2621440 | tf_op jit(solution)/shard_map/all_gather | solution.py:62
  26.2 81.6 %all-gather.7.cloned.1.call-start = ((), (), s32[]{:S(2)}) async-start(), calls=%async_computation.5 | async-start | bytes 2621440 | tf_op jit(solution)/shard_map/all_gather | solution.py:63
  62.8 25.2 %all-to-all-start = ((bf16[8,2,8192]{2,1,0:T(2,128)(2,1)}), bf16[8,2,8192]{2,1,0:T(2,128)(2,1)S(1)}, u32[]{:S(2)}, u32[]{:S(2)}) async-start(bf16[8,2,8192]{2,1,0:T(2,128)(2,1)} %reshape.181), calls=%async_computation.1 | async-start | bytes 524288 | tf_op jit(solution)/shard_map/all_to_all | solution.py:76
  68.3 108.8 %all-gather.9.cloned.1.call-start = ((), (), s32[]{:S(2)}) async-start(), calls=%async_computation.7 | async-start | bytes 1310720 | tf_op jit(solution)/shard_map/all_gather | solution.py:85
  90.9 4.9 %copy-start.2 = (f32[256,4096]{1,0:T(8,128)S(1)}, f32[256,4096]{1,0:T(8,128)}, u32[]{:S(2)}) copy-start(f32[256,4096]{1,0:T(8,128)} %get-tuple-element.34) | copy-start | bytes 12582916
  100.0 11.7 %copy-start.8 = (s32[1,256]{1,0:T(1,128)S(1)}, s32[1,256]{1,0:T(1,128)}, u32[]{:S(2)}) copy-start(s32[1,256]{1,0:T(1,128)} %param.15) | copy-start | bytes 3076
  107.8 4.6 %copy-start.4 = (f32[256,4096]{1,0:T(8,128)S(1)}, f32[256,4096]{1,0:T(8,128)}, u32[]{:S(2)}) copy-start(f32[256,4096]{1,0:T(8,128)} %get-tuple-element.36) | copy-start | bytes 12582916
  107.8 4.7 %copy-start.5 = (bf16[256,4096]{1,0:T(8,128)(2,1)S(1)}, bf16[256,4096]{1,0:T(8,128)(2,1)}, u32[]{:S(2)}) copy-start(bf16[256,4096]{1,0:T(8,128)(2,1)} %all-gather.7.cloned.1.call-done) | copy-start | bytes 6291460
  116.3 3.2 %copy-start.3 = (f32[256,4096]{1,0:T(8,128)S(1)}, f32[256,4096]{1,0:T(8,128)}, u32[]{:S(2)}) copy-start(f32[256,4096]{1,0:T(8,128)} %get-tuple-element.34) | copy-start | bytes 12582916
  162.2 101.7 %all-reduce.2.cloned.1.call-start = ((), (), s32[]{:S(2)}) async-start(), calls=%async_computation.6 | async-start | bytes 262144 | tf_op jit(solution)/shard_map/psum | solution.py:95
  177.1 16.1 %copy-start.6 = (bf16[1,32,16384]{2,1,0:T(8,128)(2,1)S(1)}, bf16[1,32,16384]{2,1,0:T(8,128)(2,1)}, u32[]{:S(2)}) copy-start(bf16[1,32,16384]{2,1,0:T(8,128)(2,1)} %all-gather.9.cloned.1.call-done) | copy-start | bytes 3145732
  193.2 73.1 %copy-start.1 = (bf16[256,1024]{1,0:T(8,128)(2,1)S(1)}, bf16[256,1024]{1,0:T(8,128)(2,1)}, u32[]{:S(2)}) copy-start(bf16[256,1024]{1,0:T(8,128)(2,1)} %param.11) | copy-start | bytes 1572868
Sparse Core Ops, SparseCore 0:
  25.6 33.9 reduce-scatter.1
  61.1 22.5 all-gather.4
  85.2 22.5 all-gather.6
  162.3 14.7 all-gather.8
  193.3 70.4 all-reduce.1
where the time goes:
time: 278 us; the launch traced here: 274 us
  waiting for transfers between devices  127 us (46%)
  matrix products  95.1 us (34%)
  between operations  15.9 us (6%)
  blocking collectives  14.8 us (5%)
  local copies, waits for them, and re-layouts  10.5 us (4%)
  starting transfers between devices  5.69 us (2%)
  other arithmetic  5.08 us (2%)
    psum x1, waiting for transfers between devices, local(): hidden_back = lax.psum(hidden_back, 'head')  55.7 us
    reduce_scatter x1, waiting for transfers between devices, local(): lax.psum_scatter(jnp.dot(hidden_rows, head_weight, preferred_element_type...  32.6 us
    dot_general x6, matrix products, client_loss(): jnp.dot(low_rank, factor_b, precision=lax.Precision.HIGHEST)  21.7 us
    dot_general x1, matrix products, local(): lax.dot_general(received, head_weight, (((1,), (1,)), ((), ())), preferre...  16.1 us
    all_gather x1, waiting for transfers between devices, local(): lax.all_gather(byte_table, 'client', axis=1, tiled=True)  15.3 us
    dot_general x1, matrix products, local(): lax.dot_general(hidden_rows, received, (((0,), (0,)), ((), ())), preferre...  14.9 us
    dot_general x1, matrix products, local(): jnp.dot(hidden_rows, head_weight, preferred_element_type=jnp.float32)  14.9 us
    all_to_all x1, blocking collectives, local(): lax.all_to_all(deltas, 'head', split_axis=1, concat_axis=0, tiled=True)  14.8 us
  transfers between devices with their start and end apart: 6, of which 5 were waited for; matrix products, arithmetic and copies ran while one was open for 13% of the time, Pallas kernels for 0%

commit v1 on v0

v1 whole, which is shorter than its diff:
```python
import functools

import jax
import jax.numpy as jnp
from jax import lax
from jax.experimental import pallas as pl
from jax.experimental.pallas import tpu as pltpu
from jax.sharding import PartitionSpec as P

EPSILON = 1e-06
learn_rate = 0.1
F32 = jnp.float32
BF16 = jnp.bfloat16
LANES = 128
HIGH = lax.Precision.HIGHEST


def dot(a, b, contract, precision=None):
    return lax.dot_general(a, b, ((contract[0], contract[1]), ((), ())), precision=precision, preferred_element_type=F32)


NN = ((1,), (0,))
NT = ((1,), (1,))
TN = ((0,), (0,))


def bits_of(count):
    return count.bit_length() - 1


def offset_of(position, count):
    bits = bits_of(count)
    return sum(((position >> (bits - 1 - bit)) & 1) << bit for bit in range(bits))


def small(a, b):
    return sum(a[:, k : k + 1] * b[k : k + 1, :] for k in range(a.shape[1]))


def span(index, width):
    return pl.ds(pl.multiple_of(index * width, LANES), width)


def forward_kernel(head_count, group_count, width, place, ids, table, in_w, in_b, w, keep, send, hidden_t, preact_out, chosen_t, held, hidden, sems):
    slots = held.shape[0]
    rows = keep.shape[0] * 2
    blocks = w.shape[1] // width

    def copy(index):
        return pltpu.make_async_copy(w.at[:, span(index, width)], held.at[index % slots], sems.at[index % slots])

    @pl.loop(0, slots)
    def _(index):
        copy(index).start()

    row = lax.broadcasted_iota(jnp.int32, (rows, rows), 0)
    column = lax.broadcasted_iota(jnp.int32, (rows, rows), 1)
    position = row // head_count
    bits = bits_of(group_count)
    offset = jnp.zeros_like(position)
    for bit in range(bits):
        offset = offset + (((position >> (bits - 1 - bit)) & 1) << bit)
    slot = (row % head_count) * group_count + jnp.bitwise_xor(offset, place[0])
    picked = jnp.sum(jnp.where(column == slot, ids[...], 0), axis=1, keepdims=True)
    people = table.shape[0]
    onehot = (lax.broadcasted_iota(jnp.int32, (rows, people), 1) == picked).astype(F32).astype(BF16)
    chosen = dot(onehot, table[...], NN)
    preact = dot(chosen.astype(BF16), in_w[...], NN) + in_b[...]
    value = jnp.maximum(preact, 0.0)
    hidden[...] = value.astype(BF16)
    hidden_t[...] = value.T.astype(BF16)
    chosen_t[...] = chosen.T.astype(BF16)
    preact_out[...] = preact

    @pl.loop(0, blocks)
    def _(index):
        copy(index).wait()
        part = dot(hidden[...], held[index % slots], NN)
        keep[:, span(index, width)] = part[: rows // 2]
        send[:, span(index, width)] = part[rows // 2 :].astype(BF16)

        @pl.when(index + slots < blocks)
        def _():
            copy(index + slots).start()


def forward(place, ids, table, in_w, in_b, w, head_count, group_count):
    rows = ids.shape[1]
    depth, columns = w.shape
    width = min(1024, columns)
    whole = pl.BlockSpec(memory_space=pltpu.VMEM)
    shapes = [
        ((rows // 2, columns), F32),
        ((rows // 2, columns), BF16),
        ((depth, rows), BF16),
        ((rows, depth), F32),
        ((table.shape[1], rows), BF16),
    ]
    slots = min(6, columns // width)
    return pl.pallas_call(
        functools.partial(forward_kernel, head_count, group_count, width),
        in_specs=[pl.BlockSpec(memory_space=pltpu.SMEM)] + [whole] * 4 + [pl.BlockSpec(memory_space=pltpu.HBM)],
        out_specs=[whole] * len(shapes),
        out_shape=[jax.ShapeDtypeStruct(*shape) for shape in shapes],
        scratch_shapes=[pltpu.VMEM((slots, depth, width), BF16), pltpu.VMEM((rows, depth), BF16), pltpu.SemaphoreType.DMA((slots,))],
        compiler_params=pltpu.CompilerParams(vmem_limit_bytes=40 * 1024 * 1024),
        cost_estimate=pl.CostEstimate(flops=32 * rows * depth * columns, bytes_accessed=2 * depth * columns, transcendentals=0),
        name="factors",
    )(place, ids, table, in_w, in_b, w)


def prepare_kernel(group_count, step, place, tokens, *refs):
    byte_parts, out_parts = refs[:group_count], refs[group_count : 2 * group_count]
    byte_full, out_full, byte_mixed, logit_gram, grams, normed_gram, inverse, squares = refs[2 * group_count :]
    vocab, width = byte_parts[0].shape
    depth = byte_full.shape[1]
    inner = width // step
    pair = min(2, step)
    gap = lax.broadcasted_iota(jnp.int32, (width, inner), 0) - step * lax.broadcasted_iota(jnp.int32, (width, inner), 1)
    byte_gram = jnp.zeros((vocab, vocab), F32)
    cross = jnp.zeros((vocab, vocab), F32)
    own_gram = jnp.zeros((vocab, vocab), F32)
    for position in range(group_count):
        start = jnp.bitwise_xor(place[0], offset_of(position, group_count))
        byte_part, out_part = byte_parts[position][...], out_parts[position][...]
        byte_full[:, pl.ds(pl.multiple_of(start * width, LANES), width)] = byte_part
        out_full[:, pl.ds(pl.multiple_of(start * width, LANES), width)] = out_part
        byte_gram += dot(byte_part, byte_part, NT)
        cross += dot(out_part, byte_part, NT)
        own_gram += dot(out_part, out_part, NT)
    for first in range(0, step, pair):
        mixer = jnp.concatenate([jnp.where(gap == first + k, 1.0, 0.0) for k in range(pair)], axis=1).astype(BF16)
        for position in range(group_count):
            start = jnp.bitwise_xor(place[0], offset_of(position, group_count))
            mixed = dot(byte_parts[position][...], mixer, NN).astype(BF16)
            for k in range(pair):
                at = pl.multiple_of((first + k) * (depth // step) + start * inner, LANES)
                byte_mixed[:, pl.ds(at, inner)] = mixed[:, k * inner : (k + 1) * inner]
    count = tokens.shape[1]
    onehot = (lax.broadcasted_iota(jnp.int32, (vocab, count), 0) == tokens[...]).astype(F32)
    logit = dot(cross, onehot, NN, HIGH)
    logit_gram[...] = logit
    half = dot(byte_gram, onehot, NN, HIGH)
    total = jnp.sum(onehot * half, axis=0, keepdims=True)
    both = dot(onehot, half, TN, HIGH)
    scale = lax.rsqrt(total / depth + EPSILON)
    eye = lax.broadcasted_iota(jnp.int32, (count, count), 0) == lax.broadcasted_iota(jnp.int32, (count, count), 1)
    down = jnp.sum(jnp.where(eye, scale, 0.0), axis=1, keepdims=True)
    grams[:vocab, :vocab] = own_gram
    grams[:vocab, vocab:] = logit
    grams[vocab:, :vocab] = logit.T
    grams[vocab:, vocab:] = both
    normed_gram[...] = both * scale * down
    inverse[...] = scale
    squares[...] = total


def prepare(place, tokens, byte_parts, out_parts, step):
    group_count = len(byte_parts)
    vocab, width = byte_parts[0].shape
    count = tokens.shape[1]
    depth = width * group_count
    whole = pl.BlockSpec(memory_space=pltpu.VMEM)
    shapes = [
        ((vocab, depth), BF16),
        ((vocab, depth), BF16),
        ((vocab, depth), BF16),
        ((vocab, count), F32),
        ((vocab + count, vocab + count), F32),
        ((count, count), F32),
        ((1, count), F32),
        ((1, count), F32),
    ]
    return pl.pallas_call(
        functools.partial(prepare_kernel, group_count, step),
        in_specs=[pl.BlockSpec(memory_space=pltpu.SMEM)] + [whole] * (1 + 2 * group_count),
        out_specs=[whole] * len(shapes),
        out_shape=[jax.ShapeDtypeStruct(*shape) for shape in shapes],
        compiler_params=pltpu.CompilerParams(vmem_limit_bytes=16 * 1024 * 1024),
        cost_estimate=pl.CostEstimate(flops=2**31, bytes_accessed=2**23, transcendentals=0),
        name="prepare",
    )(place, tokens, *byte_parts, *out_parts)


def train_kernel(
    rank,
    owned,
    tokens,
    labels,
    byte_full,
    out_full,
    byte_mixed,
    logit_gram,
    grams,
    normed_gram,
    inverse,
    squares,
    deltas,
    loss_out,
    work,
):
    vocab, depth = byte_full.shape
    count = tokens.shape[1]
    step = LANES // rank
    rows = depth * rank // LANES
    inner = depth // step
    chunks = depth // LANES
    onehot = (lax.broadcasted_iota(jnp.int32, (vocab, count), 0) == tokens[...]).astype(F32)
    label = (lax.broadcasted_iota(jnp.int32, (vocab, count), 0) == labels[...]).astype(F32)
    scale = inverse[...]
    a_t = owned[:rows, :].astype(F32).T.astype(BF16)
    table_a = jnp.zeros((rank, vocab), F32)
    for j in range(step):
        table_a += dot(a_t[j * rank : (j + 1) * rank, :], byte_mixed[:, j * inner : (j + 1) * inner], NT)
    work[...] = owned[rows:, :].astype(F32)
    b = jnp.concatenate([work[pl.ds(k, rank, stride=chunks), :] for k in range(chunks)], axis=1).astype(BF16)
    out_b = dot(b, out_full[...], NT)
    byte_b = dot(b, byte_full[...], NT)
    gram_b = dot(b, b, NT)
    low = dot(table_a, onehot, NN, HIGH) * scale
    in_b = dot(byte_b, onehot, NN, HIGH)
    s = 1.0 / (depth * rank) ** 0.5
    c = 4.0 / depth**0.5

    def one_step(low, both_b, gram_b):
        out_b, in_b = both_b[:, :vocab], both_b[:, vocab:]
        low_gram = small(gram_b, low)
        mean = (squares[...] + jnp.sum(low * (2.0 * s * in_b + (s * s) * low_gram), axis=0, keepdims=True)) / depth
        r = lax.rsqrt(jnp.maximum(mean, 0.0) + EPSILON)
        raw = logit_gram[...] + s * dot(out_b, low, TN, HIGH)
        logits = raw * (c * r)
        top = jnp.max(logits, axis=0, keepdims=True)
        grown = jnp.exp(logits - top)
        total = jnp.sum(grown, axis=0, keepdims=True)
        loss = jnp.log(total) + top - jnp.sum(label * logits, axis=0, keepdims=True)
        error = grown / total - label
        k = (c / depth) * (r * r * r) * jnp.sum(error * raw, axis=0, keepdims=True)
        error = error * (c * r)
        d_low = s * (dot(out_b, error, NN, HIGH) - k * (in_b + s * low_gram))
        kept = k * low
        on_both = rate * jnp.concatenate([-dot(low, error, NT, HIGH), kept], axis=1)
        return loss, d_low, on_both, (rate * s) * dot(kept, low, NT, HIGH)

    rate = learn_rate * s
    both_b = jnp.concatenate([out_b, in_b], axis=1)
    loss, d_low, on_both, more = one_step(low, both_b, gram_b)
    low_1 = low - learn_rate * dot(d_low, normed_gram[...], NN, HIGH)
    both_b1 = both_b + small(more, both_b) + dot(on_both, grams[...], NN, HIGH)
    gram_1 = gram_b + small(more, gram_b) + dot(on_both, both_b, NT, HIGH)
    gram_b1 = gram_1 + small(gram_1, more.T) + dot(both_b1, on_both, NT, HIGH)
    _, d_low1, on_both1, more1 = one_step(low_1, both_b1, gram_b1)
    total_b = more + more1 + small(more1, more)
    total_both = on_both + on_both1 + small(more1, on_both)
    total_out, total_in = total_both[:, :vocab], total_both[:, vocab:]
    on_byte = dot(total_in, onehot, NT, HIGH)
    on_a = dot((-learn_rate) * scale * (d_low + d_low1), onehot, NT, HIGH).astype(BF16)
    pieces = [dot(on_a, byte_mixed[:, j * inner : (j + 1) * inner], NN) for j in range(step)]
    deltas[:rows, :] = jnp.concatenate(pieces, axis=0).T.astype(BF16)
    delta_b = dot(total_b.astype(BF16), b, NN) + dot(total_out.astype(BF16), out_full[...], NN) + dot(on_byte.astype(BF16), byte_full[...], NN)
    for k in range(chunks):
        work[pl.ds(k, rank, stride=chunks), :] = delta_b[:, k * LANES : (k + 1) * LANES]
    deltas[rows:, :] = work[...].astype(BF16)
    loss_out[...] = jnp.broadcast_to(jnp.sum(loss, axis=1, keepdims=True) / count, loss_out.shape)


def train(rank, owned, tokens, labels, prepared):
    whole = pl.BlockSpec(memory_space=pltpu.VMEM)
    return pl.pallas_call(
        functools.partial(train_kernel, rank),
        in_specs=[whole] * (3 + len(prepared)),
        out_specs=[whole, whole],
        out_shape=[jax.ShapeDtypeStruct(owned.shape, BF16), jax.ShapeDtypeStruct((1, LANES), F32)],
        scratch_shapes=[pltpu.VMEM((owned.shape[0] // 2, LANES), F32)],
        compiler_params=pltpu.CompilerParams(vmem_limit_bytes=16 * 1024 * 1024),
        cost_estimate=pl.CostEstimate(flops=2**31, bytes_accessed=2**23, transcendentals=2**17),
        name="train",
    )(owned, tokens, labels, *prepared)


def stacked(parts):
    return jnp.concatenate([part[...].astype(F32) for part in parts], axis=0).astype(BF16)


def back_kernel(width, w, *refs):
    parts, out, held, sems = refs[:-3], refs[-3], refs[-2], refs[-1]
    slots = held.shape[0]
    blocks = w.shape[1] // width

    def copy(index):
        return pltpu.make_async_copy(w.at[:, span(index, width)], held.at[index % slots], sems.at[index % slots])

    @pl.loop(0, slots)
    def _(index):
        copy(index).start()

    out[...] = jnp.zeros_like(out)

    @pl.loop(0, blocks)
    def _(index):
        piece = stacked([part.at[:, span(index, width)] for part in parts])
        copy(index).wait()
        out[...] += dot(piece, held[index % slots], NT)

        @pl.when(index + slots < blocks)
        def _():
            copy(index + slots).start()


def back(w, parts):
    depth, columns = w.shape
    rows = sum(part.shape[0] for part in parts)
    width = min(1024, columns)
    slots = min(6, columns // width)
    whole = pl.BlockSpec(memory_space=pltpu.VMEM)
    return pl.pallas_call(
        functools.partial(back_kernel, width),
        in_specs=[pl.BlockSpec(memory_space=pltpu.HBM)] + [whole] * len(parts),
        out_specs=whole,
        out_shape=jax.ShapeDtypeStruct((rows, depth), F32),
        scratch_shapes=[pltpu.VMEM((slots, depth, width), BF16), pltpu.SemaphoreType.DMA((slots,))],
        compiler_params=pltpu.CompilerParams(vmem_limit_bytes=40 * 1024 * 1024),
        cost_estimate=pl.CostEstimate(flops=16 * rows * depth * columns, bytes_accessed=2 * depth * columns, transcendentals=0),
        name="hidden_back",
    )(w, *parts)


def grad_kernel(width, first, count, hidden_t, *refs):
    parts = refs[:-3] if first == 0 else refs[:-4]
    out, held, sems = refs[-3:]
    slots = held.shape[0]

    def copy(index):
        slot = index % slots
        return pltpu.make_async_copy(held.at[slot], out.at[:, span(first + index, width)], sems.at[slot])

    @pl.loop(0, count)
    def _(index):
        @pl.when(index >= slots)
        def _():
            copy(index - slots).wait()

        piece = stacked([part.at[:, span(first + index, width)] for part in parts])
        held[index % slots] = dot(hidden_t[...], piece, NN).astype(BF16)
        copy(index).start()

    @pl.loop(max(0, count - slots), count)
    def _(index):
        copy(index).wait()


def grad(hidden_t, parts, calls):
    depth, rows = hidden_t.shape
    columns = parts[0].shape[1]
    width = min(1024, columns // calls)
    count = columns // width // calls
    whole = pl.BlockSpec(memory_space=pltpu.VMEM)
    anywhere = pl.BlockSpec(memory_space=pltpu.HBM)
    out = None
    for call in range(calls):
        later = call > 0
        out = pl.pallas_call(
            functools.partial(grad_kernel, width, call * count, count),
            in_specs=[whole] * (1 + len(parts)) + [anywhere] * later,
            out_specs=anywhere,
            out_shape=jax.ShapeDtypeStruct((depth, columns), BF16),
            scratch_shapes=[pltpu.VMEM((min(4, count), depth, width), BF16), pltpu.SemaphoreType.DMA((min(4, count),))],
            input_output_aliases={1 + len(parts): 0} if later else {},
            compiler_params=pltpu.CompilerParams(vmem_limit_bytes=16 * 1024 * 1024),
            cost_estimate=pl.CostEstimate(flops=16 * rows * depth * columns // calls, bytes_accessed=2 * depth * columns // calls, transcendentals=0),
            name="head_grad",
        )(hidden_t, *parts, *([out] if later else []))
    return out


def input_kernel(chosen_t, preact, mine, other, out):
    value = jnp.where(preact[...] > 0, mine[...] + other[...].astype(F32), 0.0)
    high = value.astype(BF16)
    low = (value - high.astype(F32)).astype(BF16)
    out[...] = dot(chosen_t[...], high, NN) + dot(chosen_t[...], low, NN)


def input_grad(chosen_t, preact, mine, other):
    whole = pl.BlockSpec(memory_space=pltpu.VMEM)
    return pl.pallas_call(
        input_kernel,
        in_specs=[whole] * 4,
        out_specs=whole,
        out_shape=jax.ShapeDtypeStruct((chosen_t.shape[0], preact.shape[1]), F32),
        compiler_params=pltpu.CompilerParams(vmem_limit_bytes=8 * 1024 * 1024),
        name="in_grad",
    )(chosen_t, preact, mine, other)


def swap(value, axis, bit):
    size = lax.axis_size(axis)
    return lax.ppermute(value, axis, [(i, i ^ (1 << bit)) for i in range(size)])


def gathered(value, axis):
    parts = [value]
    for bit in reversed(range(bits_of(lax.axis_size(axis)))):
        parts = parts + [swap(part, axis, bit) for part in parts]
    return parts


def local(client_ids, client_table, in_weight, in_bias, head_weight, tokens, labels, byte_table, out_table):
    head_count = lax.axis_size("head")
    group_count = lax.axis_size("client")
    columns = head_weight.shape[1]
    depth = byte_table.shape[1] * group_count
    rank = columns * head_count // (2 * depth)
    slots = client_ids.shape[0]
    place = lax.axis_index("client").astype(jnp.int32).reshape(1)
    out_parts = gathered(out_table, "client")
    byte_parts = gathered(byte_table, "client")
    keep, send, hidden_t, preact, chosen_t = forward(
        place, client_ids.reshape(1, slots), client_table, in_weight, in_bias.reshape(1, -1), head_weight, head_count, group_count
    )
    prepared = prepare(place, tokens, byte_parts, out_parts, LANES // rank)
    total = keep + swap(send, "client", 0).astype(F32)
    for bit in range(1, bits_of(group_count)):
        half = total.shape[0] // 2
        total = total[:half] + swap(total[half:].astype(BF16), "client", bit).astype(F32)
    own = total.astype(BF16).reshape(head_count, columns // LANES, LANES)
    own, prepared = lax.optimization_barrier((own, prepared))
    owned = lax.all_to_all(own, "head", split_axis=0, concat_axis=0, tiled=True)
    deltas, losses = train(rank, owned.reshape(-1, LANES), tokens, labels, prepared)
    returned = lax.all_to_all(deltas.reshape(own.shape), "head", split_axis=0, concat_axis=0, tiled=True)
    parts = gathered(returned.reshape(head_count, columns), "client")
    hidden_back = back(head_weight, parts)
    head_grad = grad(hidden_t, parts, 4)
    bits = bits_of(head_count)
    for bit in range(bits - 1):
        hidden_back = hidden_back + swap(hidden_back.astype(BF16), "head", bit).astype(F32)
    other = swap(hidden_back.astype(BF16), "head", bits - 1)
    in_grad = input_grad(chosen_t, preact, hidden_back, other)
    return head_grad, in_grad, losses[0, :1]


def solution(mesh):
    placed = (
        P(),
        P(),
        P(None, "client"),
        P("client"),
        P("client", "head"),
        P(("head", "client"), None),
        P(("head", "client"), None),
        P(None, "client"),
        P(None, "client"),
    )
    return jax.shard_map(
        local,
        mesh=mesh,
        in_specs=placed,
        out_specs=(P("client", "head"), P(None, "client"), P(("head", "client"))),
        check_vma=False,
    )
```

time: 278 us -> 121 us (0.44); the launches traced: 274 us -> 120 us
  waiting for transfers between devices: 127 us -> 20.9 us
  matrix products: 95.1 us -> 0 us
  Pallas kernels: 0 us -> 56 us
  between operations: 15.9 us -> 0.83 us
  blocking collectives: 14.8 us -> 26.5 us
  local copies, waits for them, and re-layouts: 10.5 us -> 3.48 us
  starting transfers between devices: 5.69 us -> 12.3 us
  other arithmetic: 5.08 us -> 0.22 us
    dot_general x20 -> x0, matrix products: 95.1 us -> none  [the longest x6 21.7 us: client_loss(): jnp.dot(low_rank, factor_b, precision=lax.Precision.HIGHEST)]
    pallas_call x0 -> x9, Pallas kernels: none -> 56 us  [the longest x4 16.3 us: grad(): pl.pallas_call(functools.partial(grad_kernel, width, call * count, count)...]
    psum x1 -> x0, waiting for transfers between devices: 55.7 us -> none  [local(): hidden_back = lax.psum(hidden_back, 'head')]
    all_gather x3 -> x0, waiting for transfers between devices: 37.4 us -> none  [the longest x1 15.3 us: local(): lax.all_gather(byte_table, 'client', axis=1, tiled=True)]
    reduce_scatter x1 -> x0, waiting for transfers between devices: 32.6 us -> none  [local(): lax.psum_scatter(jnp.dot(hidden_rows, head_weight, preferred_element_type...]
    ppermute x0 -> x14, waiting for transfers between devices: none -> 20.9 us  [swap(): return lax.ppermute(value, axis, [(i, i ^ 1 << bit) for i in range(size)])]
    ppermute x0 -> x14, starting transfers between devices: none -> 12.3 us  [swap(): return lax.ppermute(value, axis, [(i, i ^ 1 << bit) for i in range(size)])]
    all_to_all x1 -> x2, blocking collectives: 14.8 us -> 26.5 us  [the longest x1 14.6 us: local(): owned = lax.all_to_all(own, 'head', split_axis=0, concat_axis=0, tiled=True)]
  transfers between devices with their start and end apart: 6 -> 14, of which waited for: 5 -> 5; matrix products, arithmetic and copies ran while one was open for 13% -> 0% of each run, Pallas kernels for 0% -> 23%
where the time goes in v1:
time: 121 us; the launch traced here: 120 us
  Pallas kernels  56 us (46%)
  blocking collectives  26.5 us (22%)
  waiting for transfers between devices  20.9 us (17%)
  starting transfers between devices  12.3 us (10%)
  local copies, waits for them, and re-layouts  3.48 us (3%)
    ppermute x14, waiting for transfers between devices, swap(): return lax.ppermute(value, axis, [(i, i ^ 1 << bit) for i in range(size)])  20.9 us
    pallas_call x4, Pallas kernels, grad(): pl.pallas_call(functools.partial(grad_kernel, width, call * count, count)...  16.3 us
    all_to_all x1, blocking collectives, local(): owned = lax.all_to_all(own, 'head', split_axis=0, concat_axis=0, tiled=True)  14.6 us
    pallas_call x1, Pallas kernels, back(): pl.pallas_call(functools.partial(back_kernel, width), in_specs=[pl.BlockS...  13.3 us
    ppermute x14, starting transfers between devices, swap(): return lax.ppermute(value, axis, [(i, i ^ 1 << bit) for i in range(size)])  12.3 us
    all_to_all x1, blocking collectives, local(): lax.all_to_all(deltas.reshape(own.shape), 'head', split_axis=0, concat_ax...  11.9 us
    pallas_call x1, Pallas kernels, forward(): pl.pallas_call(functools.partial(forward_kernel, head_count, group_count,...  11.6 us
    pallas_call x1, Pallas kernels, train(): pl.pallas_call(functools.partial(train_kernel, rank), in_specs=[whole] *...  7.75 us
  transfers between devices with their start and end apart: 14, of which 5 were waited for; matrix products, arithmetic and copies ran while one was open for 0% of the time, Pallas kernels for 23%

profile of v1, /device:TPU:0, one launch (start us, length us, event | category | flops | bytes accessed | tf_op | source)
XLA Modules:
  0.0 120.2 jit_solution(16711669796461722794)
XLA Ops:
  0.6 3.1 %collective-permute-start.2 = (bf16[256,1024]{1,0:T(8,128)(2,1)}, bf16[256,1024]{1,0:T(8,128)(2,1)S(1)}, u32[]{:S(2)}, u32[]{:S(2)}) collective-permute-start(bf16[256,1024]{1,0:T(8,128)(2,1)} %refs_0_.1), channel_id=1, source_target_pairs={{0,2},{1,3},{2,0},{3,1},{4,6},{5,7},{6,4},{7,5},{8,10},{9,11},{10,... | collective-permute-start | bytes 1572872 | tf_op jit(solution)/shard_map/ppermute | solution.py:396
  3.7 0.1 collective-permute-start.5
  3.8 0.0 copy-start.2
  3.8 1.0 copy-done.2
  4.8 0.0 copy-start.5
  4.8 0.8 copy-done.5
  5.7 0.0 copy-start.6
  5.7 0.7 copy-done.6
  6.3 0.0 copy-start.7
  6.3 0.7 copy-done.7
  7.0 0.0 copy-start.3
  7.0 0.0 copy-start.4
  7.0 0.0 copy-start
  7.0 0.0 copy-start.1
  7.0 11.6 %factors.1 = (f32[16,16384]{1,0:T(8,128)S(1)}, bf16[16,16384]{1,0:T(8,128)(2,1)S(1)}, bf16[1024,32]{1,0:T(8,128)(2,1)S(1)}, f32[32,1024]{1,0:T(8,128)S(1)}, bf16[256,32]{1,0:T(8,128)(2,1)S(1)}) custom-call(s32[1]{0:T(128)} %bitcast.place, s32[1,32]{1,0:T(1,128)S(1)} %bitcast.23, bf16[128,256]{1,0:T(8,128)(2,1)S(1)} %copy-done.5, ...), custom_call_target="tpu_custom_call" | custom-call | flops 17179869184 | bytes 33554432 | tf_op jit(solution)/shard_map/factors/pallas_call | solution.py:100
  18.6 0.1 collective-permute-start
  18.7 0.0 copy-done.3
  18.7 0.5 collective-permute-start.3
  19.2 0.0 copy-done.4
  19.2 0.1 collective-permute-start.6
  19.3 0.0 collective-permute-done.2.refs_1_
  19.3 0.4 collective-permute-start.4
  19.7 7.4 %collective-permute-done.5.refs_5_ = bf16[256,1024]{1,0:T(8,128)(2,1)S(1)} collective-permute-done((bf16[256,1024]{1,0:T(8,128)(2,1)}, bf16[256,1024]{1,0:T(8,128)(2,1)S(1)}, u32[]{:S(2)}, u32[]{:S(2)}) %collective-permute-start.5) | collective-permute-done | bytes 524320 | tf_op jit(solution)/shard_map/ppermute | solution.py:396
  27.1 0.0 collective-permute-start.7
  27.1 0.0 collective-permute-done
  27.1 0.1 convert_add_fusion
  27.2 1.8 %collective-permute-start.1 = (bf16[8,16384]{1,0:T(8,128)(2,1)S(1)}, bf16[8,16384]{1,0:T(8,128)(2,1)S(1)}, u32[]{:S(2)}, u32[]{:S(2)}) collective-permute-start(bf16[8,16384]{1,0:T(8,128)(2,1)S(1)} %slice.21), channel_id=1, source_target_pairs={{0,2},{1,3},{2,0},{3,1},{4,6},{5,7},{6,4},{7,5},{8,10},{9,11},{10,... | collective-permute-start | bytes 786440 | tf_op jit(solution)/shard_map/ppermute | solution.py:396
  29.0 7.0 %collective-permute-done.1 = bf16[8,16384]{1,0:T(8,128)(2,1)S(1)} collective-permute-done((bf16[8,16384]{1,0:T(8,128)(2,1)S(1)}, bf16[8,16384]{1,0:T(8,128)(2,1)S(1)}, u32[]{:S(2)}, u32[]{:S(2)}) %collective-permute-start.1) | collective-permute-done | bytes 262176 | tf_op jit(solution)/shard_map/ppermute | solution.py:396
  36.0 0.1 fusion.1
  36.1 0.0 collective-permute-done.3.refs_2_
  36.1 0.0 collective-permute-done.6.refs_6_
  36.1 0.0 collective-permute-done.4.refs_3_
  36.1 0.0 collective-permute-done.7.refs_7_
  36.1 0.0 copy-done
  36.1 5.6 %prepare.1 = (bf16[256,4096]{1,0:T(8,128)(2,1)S(1)}, bf16[256,4096]{1,0:T(8,128)(2,1)S(1)}, bf16[256,4096]{1,0:T(8,128)(2,1)S(1)}, f32[256,256]{1,0:T(8,128)S(1)...) custom-call(s32[1]{0:T(128)} %bitcast.place, ...), custom_call_target="tpu_custom_call" | custom-call | flops 2147483648 | bytes 8388608 | tf_op jit(solution)/shard_map/prepare/pallas_call | solution.py:174
  41.8 14.6 %all_to_all.10 = bf16[8,128,128]{2,1,0:T(8,128)(2,1)S(1)} all-to-all(bf16[8,128,128]{2,1,0:T(8,128)(2,1)S(1)} %copy.17), channel_id=1, replica_groups=mesh['head'=8,'client'=4] {'head'}, dimensions={0} | all-to-all | bytes 524288 | tf_op jit(solution)/shard_map/all_to_all | solution.py:426
  56.3 0.0 copy-done.1
  56.3 7.8 %train.1 = (bf16[1024,128]{1,0:T(8,128)(2,1)S(1)}, f32[1,128]{1,0:T(1,128)}) custom-call(bf16[1024,128]{1,0:T(8,128)(2,1)S(1)} %bitcast.20, s32[1,256]{1,0:T(1,128)S(1)} %copy-done, s32[1,256]{1,0:T(1,128)S(1)} %copy-done.1, bf16[256,4096]{1,0:T(8,128)(2,1)S(1)} %get-tuple-element.39.byte_full, bf16[256,4096]{1,0:T(8,128)(2,1)S(1)} %get-tuple-element.40.out_full, ...), custom_call_target="tpu_custom_call" | custom-call | flops 2147483648 | bytes 8388608 | tf_op jit(solution)/shard_map/train/pallas_call | solution.py:268
  64.1 11.9 %all_to_all.11 = bf16[8,128,128]{2,1,0:T(8,128)(2,1)S(1)} all-to-all(bf16[8,128,128]{2,1,0:T(8,128)(2,1)S(1)} %bitcast.21), channel_id=1, replica_groups=mesh['head'=8,'client'=4] {'head'}, dimensions={0} | all-to-all | bytes 524288 | tf_op jit(solution)/shard_map/all_to_all | solution.py:428
  76.0 0.2 copy.20
  76.2 1.6 %collective-permute-start.8 = (bf16[8,16384]{1,0:T(8,128)(2,1)S(1)}, bf16[8,16384]{1,0:T(8,128)(2,1)S(1)}, u32[]{:S(2)}, u32[]{:S(2)}) collective-permute-start(bf16[8,16384]{1,0:T(8,128)(2,1)S(1)} %bitcast.13), channel_id=1, source_target_pairs={{0,2},{1,3},{2,0},{3,1},{4,6},{5,7},{6,4},{7,5},{8,10},{9,11},{10,... | collective-permute-start | bytes 786440 | tf_op jit(solution)/shard_map/ppermute | solution.py:396
  77.8 0.0 collective-permute-start.9
  77.8 4.8 %collective-permute-done.8.refs_1_ = bf16[8,16384]{1,0:T(8,128)(2,1)S(1)} collective-permute-done((bf16[8,16384]{1,0:T(8,128)(2,1)S(1)}, bf16[8,16384]{1,0:T(8,128)(2,1)S(1)}, u32[]{:S(2)}, u32[]{:S(2)}) %collective-permute-start.8) | collective-permute-done | bytes 262176 | tf_op jit(solution)/shard_map/ppermute | solution.py:396
  82.6 0.0 collective-permute-start.10
  82.6 0.0 collective-permute-done.9.refs_2_
  82.6 1.5 %collective-permute-done.10.refs_3_ = bf16[8,16384]{1,0:T(8,128)(2,1)S(1)} collective-permute-done((bf16[8,16384]{1,0:T(8,128)(2,1)S(1)}, bf16[8,16384]{1,0:T(8,128)(2,1)S(1)}, u32[]{:S(2)}, u32[]{:S(2)}) %collective-permute-start.10) | collective-permute-done | bytes 262176 | tf_op jit(solution)/shard_map/ppermute | solution.py:396
  84.2 13.3 %hidden_back.1 = f32[32,1024]{1,0:T(8,128)S(1)} custom-call(bf16[1024,16384]{1,0:T(8,128)(2,1)} %w.3, bf16[8,16384]{1,0:T(8,128)(2,1)S(1)} %bitcast.15, bf16[8,16384]{1,0:T(8,128)(2,1)S(1)} %collective-permute-done.8.refs_1_, bf16[8,16384]{1,0:T(8,128)(2,1)S(1)} %collective-permute-done.9.refs_2_, bf16[8,16384]{1,0:T(8,128)(2,1)S(1)} %collective-permute-done.10.refs_3_), custom_call_target="tpu_custom_call" | custom-call | flops 8589934592 | bytes 33554432 | tf_op jit(solution)/shard_map/hidden_back/pallas_call | solution.py:315
  97.5 1.5 %collective-permute-start.11 = (bf16[32,1024]{1,0:T(8,128)(2,1)S(1)}, bf16[32,1024]{1,0:T(8,128)(2,1)S(1)}, u32[]{:S(2)}, u32[]{:S(2)}) collective-permute-start(bf16[32,1024]{1,0:T(8,128)(2,1)S(1)} %convert_element_type.28), channel_id=1, source_target_pairs={{0,4},{4,0},{8,12},{12,8},{16,20},{20,16},{24,28},{28,24},{1,5},{5... | collective-permute-start | bytes 196616 | tf_op jit(solution)/shard_map/ppermute | solution.py:396
  99.0 4.1 %head_grad.4.refs_4_ = bf16[1024,16384]{1,0:T(8,128)(2,1)} custom-call(bf16[1024,32]{1,0:T(8,128)(2,1)S(1)} %get-tuple-element.27.hidden_t, bf16[8,16384]{1,0:T(8,128)(2,1)S(1)} %bitcast.16, bf16[8,16384]{1,0:T(8,128)(2,1)S(1)} %collective-permute-done.8.refs_1_, bf16[8,16384]{1,0:T(8,128)(2,1)S(1)} %collective-permute-done.9.refs_2_, ...), custom_call_target="tpu_custom_call" | custom-call | flops 2147483648 | bytes 8388608 | tf_op jit(solution)/shard_map/head_grad/pallas_call | solution.py:361
  103.1 4.1 %head_grad.5.refs_4_ = bf16[1024,16384]{1,0:T(8,128)(2,1)} custom-call(bf16[1024,32]{1,0:T(8,128)(2,1)S(1)} %get-tuple-element.27.hidden_t, bf16[8,16384]{1,0:T(8,128)(2,1)S(1)} %bitcast.17, bf16[8,16384]{1,0:T(8,128)(2,1)S(1)} %collective-permute-done.8.refs_1_, ...), custom_call_target="tpu_custom_call", output_to_operand_aliasing={{}: (5, {})} | custom-call | flops 2147483648 | bytes 8388608 | tf_op jit(solution)/shard_map/head_grad/pallas_call | solution.py:361
  107.2 0.0 collective-permute-done.11
  107.2 0.1 collective-permute-start.12
  107.3 4.1 %head_grad.6.refs_4_ = bf16[1024,16384]{1,0:T(8,128)(2,1)} custom-call(bf16[1024,32]{1,0:T(8,128)(2,1)S(1)} %get-tuple-element.27.hidden_t, bf16[8,16384]{1,0:T(8,128)(2,1)S(1)} %bitcast.18, bf16[8,16384]{1,0:T(8,128)(2,1)S(1)} %collective-permute-done.8.refs_1_, ...), custom_call_target="tpu_custom_call", output_to_operand_aliasing={{}: (5, {})} | custom-call | flops 2147483648 | bytes 8388608 | tf_op jit(solution)/shard_map/head_grad/pallas_call | solution.py:361
  111.4 0.1 collective-permute-done.12
  111.6 3.1 %collective-permute-start.13 = (bf16[32,1024]{1,0:T(8,128)(2,1)S(1)}, bf16[32,1024]{1,0:T(8,128)(2,1)S(1)}, u32[]{:S(2)}, u32[]{:S(2)}) collective-permute-start(bf16[32,1024]{1,0:T(8,128)(2,1)S(1)} %get-tuple-element.51), channel_id=1, source_target_pairs={{0,16},{4,20},{8,24},{12,28},{16,0},{20,4},{24,8},{28,12},{1,17},{... | collective-permute-start | bytes 196616 | tf_op jit(solution)/shard_map/ppermute | solution.py:396
  114.7 4.1 %head_grad.7 = bf16[1024,16384]{1,0:T(8,128)(2,1)} custom-call(bf16[1024,32]{1,0:T(8,128)(2,1)S(1)} %get-tuple-element.27.hidden_t, bf16[8,16384]{1,0:T(8,128)(2,1)S(1)} %bitcast.19, bf16[8,16384]{1,0:T(8,128)(2,1)S(1)} %collective-permute-done.8.refs_1_, bf16[8,16384]{1,0:T(8,128)(2,1)S(1)} %collective-permute-done.9.refs_2_, ...), custom_call_target="tpu_custom_call", output_to_operand_aliasing={{}: (5, {})} | custom-call | flops 2147483648 | bytes 8388608 | tf_op jit(solution)/shard_map/head_grad/pallas_call | solution.py:361
  118.8 0.0 collective-permute-done.13.other
  118.8 1.4 %in_grad.1 = f32[256,1024]{1,0:T(8,128)} custom-call(bf16[256,32]{1,0:T(8,128)(2,1)S(1)} %get-tuple-element.48.chosen_t, f32[32,1024]{1,0:T(8,128)S(1)} %get-tuple-element.49.preact, f32[32,1024]{1,0:T(8,128)S(1)} %get-tuple-element.52.mine, bf16[32,1024]{1,0:T(8,128)(2,1)S(1)} %collective-permute-done.13.other), custom_call_target="tpu_custom_call" | custom-call | tf_op jit(solution)/shard_map/in_grad/pallas_call | solution.py:384
  (5 shorter events, 0.1 us)
Async XLA Ops:
  0.6 18.6 %collective-permute-start.2 = (bf16[256,1024]{1,0:T(8,128)(2,1)}, bf16[256,1024]{1,0:T(8,128)(2,1)S(1)}, u32[]{:S(2)}, u32[]{:S(2)}) collective-permute-start(bf16[256,1024]{1,0:T(8,128)(2,1)} %refs_0_.1), channel_id=1, source_target_pairs={{0,2},{1,3},{2,0},{3,1},{4,6},{5,7},{6,4},{7,5},{8,10},{9,11},{10,... | collective-permute-start | bytes 1572872 | tf_op jit(solution)/shard_map/ppermute | solution.py:396
  3.7 23.4 %collective-permute-start.5 = (bf16[256,1024]{1,0:T(8,128)(2,1)}, bf16[256,1024]{1,0:T(8,128)(2,1)S(1)}, u32[]{:S(2)}, u32[]{:S(2)}) collective-permute-start(bf16[256,1024]{1,0:T(8,128)(2,1)} %refs_4_.1), channel_id=1, source_target_pairs={{0,2},{1,3},{2,0},{3,1},{4,6},{5,7},{6,4},{7,5},{8,10},{9,11},{10,... | collective-permute-start | bytes 1572872 | tf_op jit(solution)/shard_map/ppermute | solution.py:396
  3.8 1.0 copy-start.2
  4.8 0.8 copy-start.5
  5.7 0.7 copy-start.6
  6.3 0.7 copy-start.7
  7.0 11.7 %copy-start.3 = (bf16[256,1024]{1,0:T(8,128)(2,1)S(1)}, bf16[256,1024]{1,0:T(8,128)(2,1)}, u32[]{:S(2)}) copy-start(bf16[256,1024]{1,0:T(8,128)(2,1)} %refs_0_.1) | copy-start | bytes 1572868
  7.0 12.2 %copy-start.4 = (bf16[256,1024]{1,0:T(8,128)(2,1)S(1)}, bf16[256,1024]{1,0:T(8,128)(2,1)}, u32[]{:S(2)}) copy-start(bf16[256,1024]{1,0:T(8,128)(2,1)} %refs_4_.1) | copy-start | bytes 1572868
  7.0 29.1 %copy-start = (s32[1,256]{1,0:T(1,128)S(1)}, s32[1,256]{1,0:T(1,128)}, u32[]{:S(2)}) copy-start(s32[1,256]{1,0:T(1,128)} %tokens.3) | copy-start | bytes 3076
  7.0 49.3 %copy-start.1 = (s32[1,256]{1,0:T(1,128)S(1)}, s32[1,256]{1,0:T(1,128)}, u32[]{:S(2)}) copy-start(s32[1,256]{1,0:T(1,128)} %labels.1) | copy-start | bytes 3076
  18.6 8.5 %collective-permute-start = (bf16[16,16384]{1,0:T(8,128)(2,1)S(1)}, bf16[16,16384]{1,0:T(8,128)(2,1)S(1)}, u32[]{:S(2)}, u32[]{:S(2)}) collective-permute-start(bf16[16,16384]{1,0:T(8,128)(2,1)S(1)} %get-tuple-element.29), channel_id=1, source_target_pairs={{0,1},{1,0},{2,3},{3,2},{4,5},{5,4},{6,7},{7,6},{8,9},{9,8},{10,11... | collective-permute-start | bytes 1572872 | tf_op jit(solution)/shard_map/ppermute | solution.py:396
  18.7 17.4 %collective-permute-start.3 = (bf16[256,1024]{1,0:T(8,128)(2,1)S(1)}, bf16[256,1024]{1,0:T(8,128)(2,1)S(1)}, u32[]{:S(2)}, u32[]{:S(2)}) collective-permute-start(bf16[256,1024]{1,0:T(8,128)(2,1)S(1)} %copy-done.3), channel_id=1, source_target_pairs={{0,1},{1,0},{2,3},{3,2},{4,5},{5,4},{6,7},{7,6},{8,9},{9,8},{10,11... | collective-permute-start | bytes 1572872 | tf_op jit(solution)/shard_map/ppermute | solution.py:396
  19.2 16.9 %collective-permute-start.6 = (bf16[256,1024]{1,0:T(8,128)(2,1)S(1)}, bf16[256,1024]{1,0:T(8,128)(2,1)S(1)}, u32[]{:S(2)}, u32[]{:S(2)}) collective-permute-start(bf16[256,1024]{1,0:T(8,128)(2,1)S(1)} %copy-done.4), channel_id=1, source_target_pairs={{0,1},{1,0},{2,3},{3,2},{4,5},{5,4},{6,7},{7,6},{8,9},{9,8},{10,11... | collective-permute-start | bytes 1572872 | tf_op jit(solution)/shard_map/ppermute | solution.py:396
  19.3 16.8 %collective-permute-start.4 = (bf16[256,1024]{1,0:T(8,128)(2,1)S(1)}, bf16[256,1024]{1,0:T(8,128)(2,1)S(1)}, u32[]{:S(2)}, u32[]{:S(2)}) collective-permute-start(bf16[256,1024]{1,0:T(8,128)(2,1)S(1)} %collective-permute-done.2.refs_1_), channel_id=1, source_target_pairs={{0,1},{1,0},{2,3},{3,2},{4,5},{5,4},{6,7},{7,6},{8,9},{9,8},{10,11... | collective-permute-start | bytes 1572872 | tf_op jit(solution)/shard_map/ppermute | solution.py:396
  27.1 9.0 %collective-permute-start.7 = (bf16[256,1024]{1,0:T(8,128)(2,1)S(1)}, bf16[256,1024]{1,0:T(8,128)(2,1)S(1)}, u32[]{:S(2)}, u32[]{:S(2)}) collective-permute-start(bf16[256,1024]{1,0:T(8,128)(2,1)S(1)} %collective-permute-done.5.refs_5_), channel_id=1, source_target_pairs={{0,1},{1,0},{2,3},{3,2},{4,5},{5,4},{6,7},{7,6},{8,9},{9,8},{10,11... | collective-permute-start | bytes 1572872 | tf_op jit(solution)/shard_map/ppermute | solution.py:396
  27.2 8.8 %collective-permute-start.1 = (bf16[8,16384]{1,0:T(8,128)(2,1)S(1)}, bf16[8,16384]{1,0:T(8,128)(2,1)S(1)}, u32[]{:S(2)}, u32[]{:S(2)}) collective-permute-start(bf16[8,16384]{1,0:T(8,128)(2,1)S(1)} %slice.21), channel_id=1, source_target_pairs={{0,2},{1,3},{2,0},{3,1},{4,6},{5,7},{6,4},{7,5},{8,10},{9,11},{10,... | collective-permute-start | bytes 786440 | tf_op jit(solution)/shard_map/ppermute | solution.py:396
  76.2 6.4 %collective-permute-start.8 = (bf16[8,16384]{1,0:T(8,128)(2,1)S(1)}, bf16[8,16384]{1,0:T(8,128)(2,1)S(1)}, u32[]{:S(2)}, u32[]{:S(2)}) collective-permute-start(bf16[8,16384]{1,0:T(8,128)(2,1)S(1)} %bitcast.13), channel_id=1, source_target_pairs={{0,2},{1,3},{2,0},{3,1},{4,6},{5,7},{6,4},{7,5},{8,10},{9,11},{10,... | collective-permute-start | bytes 786440 | tf_op jit(solution)/shard_map/ppermute | solution.py:396
  77.8 4.8 %collective-permute-start.9 = (bf16[8,16384]{1,0:T(8,128)(2,1)S(1)}, bf16[8,16384]{1,0:T(8,128)(2,1)S(1)}, u32[]{:S(2)}, u32[]{:S(2)}) collective-permute-start(bf16[8,16384]{1,0:T(8,128)(2,1)S(1)} %bitcast.14), channel_id=1, source_target_pairs={{0,1},{1,0},{2,3},{3,2},{4,5},{5,4},{6,7},{7,6},{8,9},{9,8},{10,11... | collective-permute-start | bytes 786440 | tf_op jit(solution)/shard_map/ppermute | solution.py:396
  82.6 1.5 %collective-permute-start.10 = (bf16[8,16384]{1,0:T(8,128)(2,1)S(1)}, bf16[8,16384]{1,0:T(8,128)(2,1)S(1)}, u32[]{:S(2)}, u32[]{:S(2)}) collective-permute-start(bf16[8,16384]{1,0:T(8,128)(2,1)S(1)} %collective-permute-done.8.refs_1_), channel_id=1, source_target_pairs={{0,1},{1,0},{2,3},{3,2},{4,5},{5,4},{6,7},{7,6},{8,9},{9,8},{10,11... | collective-permute-start | bytes 786440 | tf_op jit(solution)/shard_map/ppermute | solution.py:396
  97.5 9.7 %collective-permute-start.11 = (bf16[32,1024]{1,0:T(8,128)(2,1)S(1)}, bf16[32,1024]{1,0:T(8,128)(2,1)S(1)}, u32[]{:S(2)}, u32[]{:S(2)}) collective-permute-start(bf16[32,1024]{1,0:T(8,128)(2,1)S(1)} %convert_element_type.28), channel_id=1, source_target_pairs={{0,4},{4,0},{8,12},{12,8},{16,20},{20,16},{24,28},{28,24},{1,5},{5... | collective-permute-start | bytes 196616 | tf_op jit(solution)/shard_map/ppermute | solution.py:396
  107.2 4.3 %collective-permute-start.12 = (bf16[32,1024]{1,0:T(8,128)(2,1)S(1)}, bf16[32,1024]{1,0:T(8,128)(2,1)S(1)}, u32[]{:S(2)}, u32[]{:S(2)}) collective-permute-start(bf16[32,1024]{1,0:T(8,128)(2,1)S(1)} %fusion.2), channel_id=1, source_target_pairs={{0,8},{4,12},{8,0},{12,4},{16,24},{20,28},{24,16},{28,20},{1,9},{5... | collective-permute-start | bytes 196616 | tf_op jit(solution)/shard_map/ppermute | solution.py:396
  111.6 7.2 %collective-permute-start.13 = (bf16[32,1024]{1,0:T(8,128)(2,1)S(1)}, bf16[32,1024]{1,0:T(8,128)(2,1)S(1)}, u32[]{:S(2)}, u32[]{:S(2)}) collective-permute-start(bf16[32,1024]{1,0:T(8,128)(2,1)S(1)} %get-tuple-element.51), channel_id=1, source_target_pairs={{0,16},{4,20},{8,24},{12,28},{16,0},{20,4},{24,8},{28,12},{1,17},{... | collective-permute-start | bytes 196616 | tf_op jit(solution)/shard_map/ppermute | solution.py:396

commit v2 on v1

--- a/solution.py
+++ b/solution.py
@@ -7,16 +7,27 @@
 from jax.experimental.pallas import tpu as pltpu
 from jax.sharding import PartitionSpec as P
 
+
 EPSILON = 1e-06
 learn_rate = 0.1
 F32 = jnp.float32
 BF16 = jnp.bfloat16
 LANES = 128
-HIGH = lax.Precision.HIGHEST
-
-
-def dot(a, b, contract, precision=None):
-    return lax.dot_general(a, b, ((contract[0], contract[1]), ((), ())), precision=precision, preferred_element_type=F32)
+
+
+def dot(a, b, contract):
+    return lax.dot_general(a, b, (contract, ((), ())), preferred_element_type=F32)
+
+
+def split(a):
+    high = a.astype(BF16)
+    return high, (a - high.astype(F32)).astype(BF16)
+
+
+def fine(a, b, contract):
+    a_high, a_low = split(a)
+    b_high, b_low = split(b)
+    return dot(a_high, b_high, contract) + (dot(a_high, b_low, contract) + dot(a_low, b_high, contract))
 
 
 NN = ((1,), (0,))
@@ -41,18 +52,38 @@
     return pl.ds(pl.multiple_of(index * width, LANES), width)
 
 
-def forward_kernel(head_count, group_count, width, place, ids, table, in_w, in_b, w, keep, send, hidden_t, preact_out, chosen_t, held, hidden, sems):
+def product_loop(width, first, hidden, w, keep, send, held, sems):
     slots = held.shape[0]
+    blocks = keep.shape[1] // width
+    half = keep.shape[0]
+
+    def copy(index):
+        return pltpu.make_async_copy(w.at[:, span(first + index, width)], held.at[index % slots], sems.at[index % slots])
+
+    def start():
+        @pl.loop(0, slots)
+        def _(index):
+            copy(index).start()
+
+    def run():
+        @pl.loop(0, blocks)
+        def _(index):
+            copy(index).wait()
+            part = dot(hidden[...], held[index % slots], NN)
+            keep[:, span(index, width)] = part[:half]
+            send[:, span(index, width)] = part[half:].astype(BF16)
+
+            @pl.when(index + slots < blocks)
+            def _():
+                copy(index + slots).start()
+
+    return start, run
+
+
+def first_kernel(head_count, group_count, width, place, ids, table, in_w, in_b, w, keep, send, hidden, hidden_t, preact_out, chosen_t, held, sems):
+    start, run = product_loop(width, 0, hidden, w, keep, send, held, sems)
+    start()
     rows = keep.shape[0] * 2
-    blocks = w.shape[1] // width
-
-    def copy(index):
-        return pltpu.make_async_copy(w.at[:, span(index, width)], held.at[index % slots], sems.at[index % slots])
-
-    @pl.loop(0, slots)
-    def _(index):
-        copy(index).start()
-
     row = lax.broadcasted_iota(jnp.int32, (rows, rows), 0)
     column = lax.broadcasted_iota(jnp.int32, (rows, rows), 1)
     position = row // head_count
@@ -71,48 +102,59 @@
     hidden_t[...] = value.T.astype(BF16)
     chosen_t[...] = chosen.T.astype(BF16)
     preact_out[...] = preact
-
-    @pl.loop(0, blocks)
-    def _(index):
-        copy(index).wait()
-        part = dot(hidden[...], held[index % slots], NN)
-        keep[:, span(index, width)] = part[: rows // 2]
-        send[:, span(index, width)] = part[rows // 2 :].astype(BF16)
-
-        @pl.when(index + slots < blocks)
-        def _():
-            copy(index + slots).start()
-
-
-def forward(place, ids, table, in_w, in_b, w, head_count, group_count):
+    run()
+
+
+def next_kernel(width, first, hidden, w, keep, send, held, sems):
+    start, run = product_loop(width, first, hidden, w, keep, send, held, sems)
+    start()
+    run()
+
+
+def forward(place, ids, table, in_w, in_b, w, head_count, group_count, calls):
     rows = ids.shape[1]
     depth, columns = w.shape
-    width = min(1024, columns)
+    share = columns // calls
+    width = min(1024, share)
+    slots = min(6, share // width)
     whole = pl.BlockSpec(memory_space=pltpu.VMEM)
-    shapes = [
-        ((rows // 2, columns), F32),
-        ((rows // 2, columns), BF16),
-        ((depth, rows), BF16),
-        ((rows, depth), F32),
-        ((table.shape[1], rows), BF16),
-    ]
-    slots = min(6, columns // width)
-    return pl.pallas_call(
-        functools.partial(forward_kernel, head_count, group_count, width),
-        in_specs=[pl.BlockSpec(memory_space=pltpu.SMEM)] + [whole] * 4 + [pl.BlockSpec(memory_space=pltpu.HBM)],
-        out_specs=[whole] * len(shapes),
-        out_shape=[jax.ShapeDtypeStruct(*shape) for shape in shapes],
-        scratch_shapes=[pltpu.VMEM((slots, depth, width), BF16), pltpu.VMEM((rows, depth), BF16), pltpu.SemaphoreType.DMA((slots,))],
+    hbm = pl.BlockSpec(memory_space=pltpu.HBM)
+    shapes = [((rows // 2, share), F32), ((rows // 2, share), BF16)]
+    extra = [((rows, depth), BF16), ((depth, rows), BF16), ((rows, depth), F32), ((table.shape[1], rows), BF16)]
+    common = dict(
+        scratch_shapes=[pltpu.VMEM((slots, depth, width), BF16), pltpu.SemaphoreType.DMA((slots,))],
         compiler_params=pltpu.CompilerParams(vmem_limit_bytes=40 * 1024 * 1024),
-        cost_estimate=pl.CostEstimate(flops=32 * rows * depth * columns, bytes_accessed=2 * depth * columns, transcendentals=0),
+        cost_estimate=pl.CostEstimate(flops=32 * rows * depth * share, bytes_accessed=2 * depth * share, transcendentals=0),
         name="factors",
-    )(place, ids, table, in_w, in_b, w)
+    )
+    shaped = lambda items: [jax.ShapeDtypeStruct(*shape) for shape in items]
+    first = pl.pallas_call(
+        functools.partial(first_kernel, head_count, group_count, width),
+        in_specs=[pl.BlockSpec(memory_space=pltpu.SMEM)] + [pl.BlockSpec(value.shape) for value in (ids, table, in_w, in_b)] + [hbm],
+        out_specs=[whole] * 6,
+        out_shape=shaped(shapes + extra),
+        **common,
+    )
+    keep, send, hidden, hidden_t, preact, chosen_t = first(place, ids, table, in_w, in_b, w)
+    pairs = [(keep, send)]
+    for call in range(1, calls):
+        later = pl.pallas_call(
+            functools.partial(next_kernel, width, call * (share // width)),
+            in_specs=[whole, hbm],
+            out_specs=[whole] * 2,
+            out_shape=shaped(shapes),
+            **common,
+        )
+        pairs.append(later(hidden, w))
+    return pairs, hidden_t, preact, chosen_t
 
 
 def prepare_kernel(group_count, step, place, tokens, *refs):
-    byte_parts, out_parts = refs[:group_count], refs[group_count : 2 * group_count]
-    byte_full, out_full, byte_mixed, logit_gram, grams, normed_gram, inverse, squares = refs[2 * group_count :]
-    vocab, width = byte_parts[0].shape
+    near, far = refs[:group_count], refs[group_count : 3 * group_count]
+    byte_full, out_full, byte_mixed, logit_gram, grams, normed_gram, inverse, squares = refs[3 * group_count :]
+    vocab, width = near[0].shape
+    part = vocab // 2
+    turned = place[1] != 0
     depth = byte_full.shape[1]
     inner = width // step
     pair = min(2, step)
@@ -121,10 +163,19 @@
     cross = jnp.zeros((vocab, vocab), F32)
     own_gram = jnp.zeros((vocab, vocab), F32)
     for position in range(group_count):
-        start = jnp.bitwise_xor(place[0], offset_of(position, group_count))
-        byte_part, out_part = byte_parts[position][...], out_parts[position][...]
-        byte_full[:, pl.ds(pl.multiple_of(start * width, LANES), width)] = byte_part
-        out_full[:, pl.ds(pl.multiple_of(start * width, LANES), width)] = out_part
+        offset = offset_of(position, group_count)
+        start = jnp.bitwise_xor(place[0], offset)
+        where = span(start, width)
+        if offset < group_count // 2:
+            out_full[:, where] = near[2 * offset][...]
+            byte_full[:, where] = near[2 * offset + 1][...]
+        else:
+            out_low, byte_low, crossing, handed = (ref[...] for ref in far[4 * (offset - group_count // 2) :][:4])
+            out_full[:part, where] = out_low
+            byte_full[:part, where] = byte_low
+            out_full[part:, where] = jnp.where(turned, handed, crossing)
+            byte_full[part:, where] = jnp.where(turned, crossing, handed)
+        out_part, byte_part = out_full[:, where], byte_full[:, where]
         byte_gram += dot(byte_part, byte_part, NT)
         cross += dot(out_part, byte_part, NT)
         own_gram += dot(out_part, out_part, NT)
@@ -132,17 +183,17 @@
         mixer = jnp.concatenate([jnp.where(gap == first + k, 1.0, 0.0) for k in range(pair)], axis=1).astype(BF16)
         for position in range(group_count):
             start = jnp.bitwise_xor(place[0], offset_of(position, group_count))
-            mixed = dot(byte_parts[position][...], mixer, NN).astype(BF16)
+            mixed = dot(byte_full[:, span(start, width)], mixer, NN).astype(BF16)
             for k in range(pair):
                 at = pl.multiple_of((first + k) * (depth // step) + start * inner, LANES)
                 byte_mixed[:, pl.ds(at, inner)] = mixed[:, k * inner : (k + 1) * inner]
     count = tokens.shape[1]
     onehot = (lax.broadcasted_iota(jnp.int32, (vocab, count), 0) == tokens[...]).astype(F32)
-    logit = dot(cross, onehot, NN, HIGH)
+    logit = fine(cross, onehot, NN)
     logit_gram[...] = logit
-    half = dot(byte_gram, onehot, NN, HIGH)
+    half = fine(byte_gram, onehot, NN)
     total = jnp.sum(onehot * half, axis=0, keepdims=True)
-    both = dot(onehot, half, TN, HIGH)
+    both = fine(onehot, half, TN)
     scale = lax.rsqrt(total / depth + EPSILON)
     eye = lax.broadcasted_iota(jnp.int32, (count, count), 0) == lax.broadcasted_iota(jnp.int32, (count, count), 1)
     down = jnp.sum(jnp.where(eye, scale, 0.0), axis=1, keepdims=True)
@@ -155,9 +206,9 @@
     squares[...] = total
 
 
-def prepare(place, tokens, byte_parts, out_parts, step):
-    group_count = len(byte_parts)
-    vocab, width = byte_parts[0].shape
+def prepare(place, tokens, near, far, step):
+    group_count = len(near)
+    vocab, width = near[0].shape
     count = tokens.shape[1]
     depth = width * group_count
     whole = pl.BlockSpec(memory_space=pltpu.VMEM)
@@ -173,13 +224,13 @@
     ]
     return pl.pallas_call(
         functools.partial(prepare_kernel, group_count, step),
-        in_specs=[pl.BlockSpec(memory_space=pltpu.SMEM)] + [whole] * (1 + 2 * group_count),
+        in_specs=[pl.BlockSpec(memory_space=pltpu.SMEM)] + [whole] * (1 + 3 * group_count),
         out_specs=[whole] * len(shapes),
         out_shape=[jax.ShapeDtypeStruct(*shape) for shape in shapes],
         compiler_params=pltpu.CompilerParams(vmem_limit_bytes=16 * 1024 * 1024),
         cost_estimate=pl.CostEstimate(flops=2**31, bytes_accessed=2**23, transcendentals=0),
         name="prepare",
-    )(place, tokens, *byte_parts, *out_parts)
+    )(place, tokens, *near, *far)
 
 
 def train_kernel(
@@ -217,8 +268,8 @@
     out_b = dot(b, out_full[...], NT)
     byte_b = dot(b, byte_full[...], NT)
     gram_b = dot(b, b, NT)
-    low = dot(table_a, onehot, NN, HIGH) * scale
-    in_b = dot(byte_b, onehot, NN, HIGH)
+    low = fine(table_a, onehot, NN) * scale
+    in_b = fine(byte_b, onehot, NN)
     s = 1.0 / (depth * rank) ** 0.5
     c = 4.0 / depth**0.5
 
@@ -227,7 +278,7 @@
         low_gram = small(gram_b, low)
         mean = (squares[...] + jnp.sum(low * (2.0 * s * in_b + (s * s) * low_gram), axis=0, keepdims=True)) / depth
         r = lax.rsqrt(jnp.maximum(mean, 0.0) + EPSILON)
-        raw = logit_gram[...] + s * dot(out_b, low, TN, HIGH)
+        raw = logit_gram[...] + s * fine(out_b, low, TN)
         logits = raw * (c * r)
         top = jnp.max(logits, axis=0, keepdims=True)
         grown = jnp.exp(logits - top)
@@ -236,24 +287,24 @@
         error = grown / total - label
         k = (c / depth) * (r * r * r) * jnp.sum(error * raw, axis=0, keepdims=True)
         error = error * (c * r)
-        d_low = s * (dot(out_b, error, NN, HIGH) - k * (in_b + s * low_gram))
+        d_low = s * (fine(out_b, error, NN) - k * (in_b + s * low_gram))
         kept = k * low
-        on_both = rate * jnp.concatenate([-dot(low, error, NT, HIGH), kept], axis=1)
-        return loss, d_low, on_both, (rate * s) * dot(kept, low, NT, HIGH)
+        on_both = rate * jnp.concatenate([-fine(low, error, NT), kept], axis=1)
+        return loss, d_low, on_both, (rate * s) * fine(kept, low, NT)
 
     rate = learn_rate * s
     both_b = jnp.concatenate([out_b, in_b], axis=1)
     loss, d_low, on_both, more = one_step(low, both_b, gram_b)
-    low_1 = low - learn_rate * dot(d_low, normed_gram[...], NN, HIGH)
-    both_b1 = both_b + small(more, both_b) + dot(on_both, grams[...], NN, HIGH)
-    gram_1 = gram_b + small(more, gram_b) + dot(on_both, both_b, NT, HIGH)
-    gram_b1 = gram_1 + small(gram_1, more.T) + dot(both_b1, on_both, NT, HIGH)
+    low_1 = low - learn_rate * fine(d_low, normed_gram[...], NN)
+    both_b1 = both_b + small(more, both_b) + fine(on_both, grams[...], NN)
+    gram_1 = gram_b + small(more, gram_b) + fine(on_both, both_b, NT)
+    gram_b1 = gram_1 + small(gram_1, more.T) + fine(both_b1, on_both, NT)
     _, d_low1, on_both1, more1 = one_step(low_1, both_b1, gram_b1)
     total_b = more + more1 + small(more1, more)
     total_both = on_both + on_both1 + small(more1, on_both)
     total_out, total_in = total_both[:, :vocab], total_both[:, vocab:]
-    on_byte = dot(total_in, onehot, NT, HIGH)
-    on_a = dot((-learn_rate) * scale * (d_low + d_low1), onehot, NT, HIGH).astype(BF16)
+    on_byte = fine(total_in, onehot, NT)
+    on_a = fine((-learn_rate) * scale * (d_low + d_low1), onehot, NT).astype(BF16)
     pieces = [dot(on_a, byte_mixed[:, j * inner : (j + 1) * inner], NN) for j in range(step)]
     deltas[:rows, :] = jnp.concatenate(pieces, axis=0).T.astype(BF16)
     delta_b = dot(total_b.astype(BF16), b, NN) + dot(total_out.astype(BF16), out_full[...], NN) + dot(on_byte.astype(BF16), byte_full[...], NN)
@@ -351,22 +402,24 @@
 def grad(hidden_t, parts, calls):
     depth, rows = hidden_t.shape
     columns = parts[0].shape[1]
-    width = min(1024, columns // calls)
-    count = columns // width // calls
+    width = min(1024, columns // 4)
+    blocks = columns // width
+    edges = [blocks * call // calls for call in range(calls + 1)]
     whole = pl.BlockSpec(memory_space=pltpu.VMEM)
     anywhere = pl.BlockSpec(memory_space=pltpu.HBM)
     out = None
     for call in range(calls):
         later = call > 0
+        count = edges[call + 1] - edges[call]
         out = pl.pallas_call(
-            functools.partial(grad_kernel, width, call * count, count),
+            functools.partial(grad_kernel, width, edges[call], count),
             in_specs=[whole] * (1 + len(parts)) + [anywhere] * later,
             out_specs=anywhere,
             out_shape=jax.ShapeDtypeStruct((depth, columns), BF16),
             scratch_shapes=[pltpu.VMEM((min(4, count), depth, width), BF16), pltpu.SemaphoreType.DMA((min(4, count),))],
             input_output_aliases={1 + len(parts): 0} if later else {},
             compiler_params=pltpu.CompilerParams(vmem_limit_bytes=16 * 1024 * 1024),
-            cost_estimate=pl.CostEstimate(flops=16 * rows * depth * columns // calls, bytes_accessed=2 * depth * columns // calls, transcendentals=0),
+            cost_estimate=pl.CostEstimate(flops=16 * rows * depth * width * count, bytes_accessed=2 * depth * width * count, transcendentals=0),
             name="head_grad",
         )(hidden_t, *parts, *([out] if later else []))
     return out
@@ -403,32 +456,48 @@
     return parts
 
 
-def local(client_ids, client_table, in_weight, in_bias, head_weight, tokens, labels, byte_table, out_table):
+def steps(client_ids, client_table, in_weight, in_bias, head_weight, tokens, labels, byte_table, out_table):
     head_count = lax.axis_size("head")
     group_count = lax.axis_size("client")
     columns = head_weight.shape[1]
     depth = byte_table.shape[1] * group_count
     rank = columns * head_count // (2 * depth)
     slots = client_ids.shape[0]
-    place = lax.axis_index("client").astype(jnp.int32).reshape(1)
-    out_parts = gathered(out_table, "client")
-    byte_parts = gathered(byte_table, "client")
-    keep, send, hidden_t, preact, chosen_t = forward(
-        place, client_ids.reshape(1, slots), client_table, in_weight, in_bias.reshape(1, -1), head_weight, head_count, group_count
+    top = bits_of(group_count) - 1
+    side = lax.axis_index("head") & 1
+    place = jnp.stack([lax.axis_index("client"), side]).astype(jnp.int32)
+    part = out_table.shape[0] // 2
+    out_low, out_high, byte_low, byte_high = out_table[:part], out_table[part:], byte_table[:part], byte_table[part:]
+    crossing = swap(jnp.where(side == 0, out_high, byte_high), "client", top)
+    far = [swap(out_low, "client", top), swap(byte_low, "client", top)]
+    near = [out_table, byte_table]
+    for bit in range(top):
+        near = near + [swap(value, "client", bit) for value in near]
+    pairs, hidden_t, preact, chosen_t = forward(
+        place, client_ids.reshape(1, slots), client_table, in_weight, in_bias.reshape(1, -1), head_weight, head_count, group_count, 2
     )
-    prepared = prepare(place, tokens, byte_parts, out_parts, LANES // rank)
-    total = keep + swap(send, "client", 0).astype(F32)
-    for bit in range(1, bits_of(group_count)):
-        half = total.shape[0] // 2
-        total = total[:half] + swap(total[half:].astype(BF16), "client", bit).astype(F32)
-    own = total.astype(BF16).reshape(head_count, columns // LANES, LANES)
+    crossing, pairs[0] = lax.optimization_barrier((crossing, pairs[0]))
+    handed = swap(crossing, "head", 0)
+    far = far + [crossing, handed]
+    for bit in range(top):
+        far = far + [swap(value, "client", bit) for value in far]
+    prepared = prepare(place, tokens, near, far, LANES // rank)
+    halves = []
+    for keep, send in pairs:
+        total = keep + swap(send, "client", 0).astype(F32)
+        for bit in range(1, top + 1):
+            half = total.shape[0] // 2
+            got = swap(total[half:].astype(BF16), "client", bit)
+            total = total[:half] + got.astype(F32)
+        halves.append(total.astype(BF16).reshape(head_count, -1, LANES))
+    own = jnp.concatenate(halves, axis=1)
     own, prepared = lax.optimization_barrier((own, prepared))
     owned = lax.all_to_all(own, "head", split_axis=0, concat_axis=0, tiled=True)
     deltas, losses = train(rank, owned.reshape(-1, LANES), tokens, labels, prepared)
     returned = lax.all_to_all(deltas.reshape(own.shape), "head", split_axis=0, concat_axis=0, tiled=True)
     parts = gathered(returned.reshape(head_count, columns), "client")
     hidden_back = back(head_weight, parts)
-    head_grad = grad(hidden_t, parts, 4)
+    head_grad = grad(hidden_t, parts, 3)
     bits = bits_of(head_count)
     for bit in range(bits - 1):
         hidden_back = hidden_back + swap(hidden_back.astype(BF16), "head", bit).astype(F32)
@@ -450,7 +519,7 @@
         P(None, "client"),
     )
     return jax.shard_map(
-        local,
+        steps,
         mesh=mesh,
         in_specs=placed,
         out_specs=(P("client", "head"), P(None, "client"), P(("head", "client"))),

time: 121 us -> 127 us (1.050)
  waiting for transfers between devices: 20.9 us -> 25.7 us
  starting transfers between devices: 12.3 us -> 13.7 us
  other arithmetic: 0.22 us -> 1.58 us
    ppermute x14 -> x20, waiting for transfers between devices: 20.9 us -> 25.7 us  [swap(): return lax.ppermute(value, axis, [(i, i ^ 1 << bit) for i in range(size)])]
    pallas_call x1, Pallas kernels: 7.75 us -> 5.81 us  [train(): pl.pallas_call(functools.partial(train_kernel, rank), in_specs=[whole] *...]
    ppermute x14 -> x20, starting transfers between devices: 12.3 us -> 13.7 us  [swap(): return lax.ppermute(value, axis, [(i, i ^ 1 << bit) for i in range(size)])]
  transfers between devices with their start and end apart: 14 -> 20, of which waited for: 5 -> 7; matrix products, arithmetic and copies ran while one was open for 0% -> 0% of each run, Pallas kernels for 23% -> 23%
where the time goes in v2:
time: 127 us
  Pallas kernels  54.9 us (43%)
  blocking collectives  26.7 us (21%)
  waiting for transfers between devices  25.7 us (20%)
  starting transfers between devices  13.7 us (11%)
  local copies, waits for them, and re-layouts  3.48 us (3%)
  other arithmetic  1.58 us (1%)
    ppermute x20, waiting for transfers between devices, swap(): return lax.ppermute(value, axis, [(i, i ^ 1 << bit) for i in range(size)])  25.7 us
    pallas_call x3, Pallas kernels, grad(): pl.pallas_call(functools.partial(grad_kernel, width, edges[call], count),...  15 us
    all_to_all x1, blocking collectives, steps(): owned = lax.all_to_all(own, 'head', split_axis=0, concat_axis=0, tiled=True)  14.8 us
    ppermute x20, starting transfers between devices, swap(): return lax.ppermute(value, axis, [(i, i ^ 1 << bit) for i in range(size)])  13.7 us
    pallas_call x1, Pallas kernels, back(): pl.pallas_call(functools.partial(back_kernel, width), in_specs=[pl.BlockS...  13.3 us
    all_to_all x1, blocking collectives, steps(): lax.all_to_all(deltas.reshape(own.shape), 'head', split_axis=0, concat_ax...  12 us
    pallas_call x1, Pallas kernels, forward(): first(place, ids, table, in_w, in_b, w)  7.22 us
    pallas_call x1, Pallas kernels, forward(): pairs.append(later(hidden, w))  6.68 us
  transfers between devices with their start and end apart: 20, of which 7 were waited for; matrix products, arithmetic and copies ran while one was open for 0% of the time, Pallas kernels for 23%

profile of v2, /device:TPU:0, one launch (start us, length us, event | category | flops | bytes accessed | tf_op | source)
XLA Modules:
  0.0 127.0 jit_solution(18016271561759254898)
XLA Ops:
  0.6 1.3 fusion.6
  1.9 3.1 %collective-permute-start = (bf16[128,1024]{1,0:T(8,128)(2,1)S(1)}, bf16[128,1024]{1,0:T(8,128)(2,1)S(1)}, u32[]{:S(2)}, u32[]{:S(2)}) collective-permute-start(bf16[128,1024]{1,0:T(8,128)(2,1)S(1)} %get-tuple-element.66), channel_id=1, source_target_pairs={{0,2},{1,3},{2,0},{3,1},{4,6},{5,7},{6,4},{7,5},{8,10},{9,11},{10,... | collective-permute-start | bytes 786440 | tf_op jit(solution)/shard_map/ppermute | solution.py:449
  5.0 0.1 pad_add_fusion.place
  5.0 0.0 copy-start
  5.0 1.0 copy-done
  6.1 0.8 copy-done.3
  6.9 0.7 copy-done.4
  7.6 0.7 copy-done.7
  8.3 7.2 %factors.2 = (f32[16,8192]{1,0:T(8,128)S(1)}, bf16[16,8192]{1,0:T(8,128)(2,1)S(1)}, bf16[32,1024]{1,0:T(8,128)(2,1)S(1)}, bf16[1024,32]{1,0:T(8,128)(2,1)S(1)}, ...) custom-call(s32[2]{0:T(128)S(1)} %pad_add_fusion.place, s32[1,32]{1,0:T(1,128)S(1)} %bitcast.25, ...), custom_call_target="tpu_custom_call" | custom-call | flops 8589934592 | bytes 16777216 | tf_op jit(solution)/shard_map/factors/pallas_call | solution.py:138
  15.5 6.7 %factors.3 = (f32[16,8192]{1,0:T(8,128)S(1)}, bf16[16,8192]{1,0:T(8,128)(2,1)S(1)}) custom-call(bf16[32,1024]{1,0:T(8,128)(2,1)S(1)} %get-tuple-element.38.hidden, bf16[1024,16384]{1,0:T(8,128)(2,1)} %w.5), custom_call_target="tpu_custom_call" | custom-call | flops 8589934592 | bytes 16777216 | tf_op jit(solution)/shard_map/factors/pallas_call | solution.py:148
  22.2 0.1 collective-permute-start.3
  22.3 0.0 copy-done.1
  22.3 0.5 collective-permute-start.5
  22.8 0.0 collective-permute-start.7
  22.8 2.0 %collective-permute-start.8 = (bf16[128,1024]{1,0:T(8,128)(2,1)S(1)}, bf16[128,1024]{1,0:T(8,128)(2,1)S(1)}, u32[]{:S(2)}, u32[]{:S(2)}) collective-permute-start(bf16[128,1024]{1,0:T(8,128)(2,1)S(1)} %get-tuple-element.65), channel_id=1, source_target_pairs={{0,2},{1,3},{2,0},{3,1},{4,6},{5,7},{6,4},{7,5},{8,10},{9,11},{10,... | collective-permute-start | bytes 786440 | tf_op jit(solution)/shard_map/ppermute | solution.py:449
  24.8 0.0 collective-permute-done.refs_6_
  24.8 0.0 collective-permute-start.1
  24.8 0.0 collective-permute-done.3
  24.9 0.1 collective-permute-start.4
  25.0 1.4 %collective-permute-done.1 = bf16[16,8192]{1,0:T(8,128)(2,1)S(1)} collective-permute-done((bf16[16,8192]{1,0:T(8,128)(2,1)S(1)}, bf16[16,8192]{1,0:T(8,128)(2,1)S(1)}, u32[]{:S(2)}, u32[]{:S(2)}) %collective-permute-start.1) | collective-permute-done | bytes 262176 | tf_op jit(solution)/shard_map/ppermute | solution.py:449
  26.3 1.5 %collective-permute-start.9 = (bf16[128,1024]{1,0:T(8,128)(2,1)S(1)}, bf16[128,1024]{1,0:T(8,128)(2,1)S(1)}, u32[]{:S(2)}, u32[]{:S(2)}) collective-permute-start(bf16[128,1024]{1,0:T(8,128)(2,1)S(1)} %collective-permute-done.refs_6_), channel_id=1, source_target_pairs={{0,4},{4,0},{8,12},{12,8},{16,20},{20,16},{24,28},{28,24},{1,5},{5... | collective-permute-start | bytes 786440 | tf_op jit(solution)/shard_map/ppermute | solution.py:449
  27.8 0.1 convert_add_fusion.1
  27.9 4.0 %collective-permute-done.7.refs_4_ = bf16[128,1024]{1,0:T(8,128)(2,1)S(1)} collective-permute-done((bf16[128,1024]{1,0:T(8,128)(2,1)S(1)}, bf16[128,1024]{1,0:T(8,128)(2,1)S(1)}, u32[]{:S(2)}, u32[]{:S(2)}) %collective-permute-start.7) | collective-permute-done | bytes 262176 | tf_op jit(solution)/shard_map/ppermute | solution.py:449
  31.9 0.0 copy-done.2
  31.9 0.0 collective-permute-start.6
  31.9 7.5 %collective-permute-done.4 = bf16[8,8192]{1,0:T(8,128)(2,1)S(1)} collective-permute-done((bf16[8,8192]{1,0:T(8,128)(2,1)S(1)}, bf16[8,8192]{1,0:T(8,128)(2,1)S(1)}, u32[]{:S(2)}, u32[]{:S(2)}) %collective-permute-start.4) | collective-permute-done | bytes 131104 | tf_op jit(solution)/shard_map/ppermute | solution.py:449
  39.5 0.3 collective-permute-start.2
  39.8 0.0 collective-permute-done.8.refs_5_
  39.8 0.1 collective-permute-start.12
  39.9 0.0 collective-permute-done.5.refs_2_
  39.9 0.5 collective-permute-start.10
  40.4 0.0 collective-permute-done.9.refs_7_
  40.4 0.1 collective-permute-start.11
  40.5 3.9 %collective-permute-done.2 = bf16[8,8192]{1,0:T(8,128)(2,1)S(1)} collective-permute-done((bf16[8,8192]{1,0:T(8,128)(2,1)S(1)}, bf16[8,8192]{1,0:T(8,128)(2,1)S(1)}, u32[]{:S(2)}, u32[]{:S(2)}) %collective-permute-start.2) | collective-permute-done | bytes 131104 | tf_op jit(solution)/shard_map/ppermute | solution.py:449
  44.4 0.0 collective-permute-start.13
  44.5 0.0 collective-permute-done.6.refs_3_
  44.6 0.0 collective-permute-done.10.refs_8_
  44.6 0.0 collective-permute-done.11.refs_9_
  44.6 0.0 collective-permute-done.12.refs_10_
  44.6 1.4 %collective-permute-done.13.refs_11_ = bf16[128,1024]{1,0:T(8,128)(2,1)S(1)} collective-permute-done((bf16[128,1024]{1,0:T(8,128)(2,1)S(1)}, bf16[128,1024]{1,0:T(8,128)(2,1)S(1)}, u32[]{:S(2)}, u32[]{:S(2)}) %collective-permute-start.13) | collective-permute-done | bytes 262176 | tf_op jit(solution)/shard_map/ppermute | solution.py:449
  46.0 0.0 copy-done.5
  46.0 5.6 %prepare.1 = (bf16[256,4096]{1,0:T(8,128)(2,1)S(1)}, bf16[256,4096]{1,0:T(8,128)(2,1)S(1)}, bf16[256,4096]{1,0:T(8,128)(2,1)S(1)}, f32[256,256]{1,0:T(8,128)S(1)...) custom-call(s32[2]{0:T(128)S(1)} %pad_add_fusion.place, ...), custom_call_target="tpu_custom_call" | custom-call | flops 2147483648 | bytes 8388608 | tf_op jit(solution)/shard_map/prepare/pallas_call | solution.py:225
  51.5 14.8 %all_to_all.10 = bf16[8,128,128]{2,1,0:T(8,128)(2,1)S(1)} all-to-all(bf16[8,128,128]{2,1,0:T(8,128)(2,1)S(1)} %pad_maximum_fusion), channel_id=1, replica_groups=mesh['head'=8,'client'=4] {'head'}, dimensions={0} | all-to-all | bytes 524288 | tf_op jit(solution)/shard_map/all_to_all | solution.py:495
  66.3 0.0 copy-done.6
  66.3 5.8 %train.1 = (bf16[1024,128]{1,0:T(8,128)(2,1)S(1)}, f32[1,128]{1,0:T(1,128)}) custom-call(bf16[1024,128]{1,0:T(8,128)(2,1)S(1)} %bitcast.22, s32[1,256]{1,0:T(1,128)S(1)} %copy-done.5, s32[1,256]{1,0:T(1,128)S(1)} %copy-done.6, bf16[256,4096]{1,0:T(8,128)(2,1)S(1)} %get-tuple-element.51.byte_full, bf16[256,4096]{1,0:T(8,128)(2,1)S(1)} %get-tuple-element.52.out_full, ...), custom_call_target="tpu_custom_call" | custom-call | flops 2147483648 | bytes 8388608 | tf_op jit(solution)/shard_map/train/pallas_call | solution.py:319
  72.2 12.0 %all_to_all.11 = bf16[8,128,128]{2,1,0:T(8,128)(2,1)S(1)} all-to-all(bf16[8,128,128]{2,1,0:T(8,128)(2,1)S(1)} %bitcast.23), channel_id=1, replica_groups=mesh['head'=8,'client'=4] {'head'}, dimensions={0} | all-to-all | bytes 524288 | tf_op jit(solution)/shard_map/all_to_all | solution.py:497
  84.1 0.2 copy.21
  84.3 0.6 collective-permute-start.14
  84.9 0.0 collective-permute-start.15
  84.9 5.8 %collective-permute-done.14.refs_1_ = bf16[8,16384]{1,0:T(8,128)(2,1)S(1)} collective-permute-done((bf16[8,16384]{1,0:T(8,128)(2,1)S(1)}, bf16[8,16384]{1,0:T(8,128)(2,1)S(1)}, u32[]{:S(2)}, u32[]{:S(2)}) %collective-permute-start.14) | collective-permute-done | bytes 262176 | tf_op jit(solution)/shard_map/ppermute | solution.py:449
  90.7 0.0 collective-permute-start.16
  90.7 0.0 collective-permute-done.15.refs_2_
  90.7 1.5 %collective-permute-done.16.refs_3_ = bf16[8,16384]{1,0:T(8,128)(2,1)S(1)} collective-permute-done((bf16[8,16384]{1,0:T(8,128)(2,1)S(1)}, bf16[8,16384]{1,0:T(8,128)(2,1)S(1)}, u32[]{:S(2)}, u32[]{:S(2)}) %collective-permute-start.16) | collective-permute-done | bytes 262176 | tf_op jit(solution)/shard_map/ppermute | solution.py:449
  92.3 13.3 %hidden_back.1 = f32[32,1024]{1,0:T(8,128)S(1)} custom-call(bf16[1024,16384]{1,0:T(8,128)(2,1)} %w.5, bf16[8,16384]{1,0:T(8,128)(2,1)S(1)} %bitcast.18, bf16[8,16384]{1,0:T(8,128)(2,1)S(1)} %collective-permute-done.14.refs_1_, bf16[8,16384]{1,0:T(8,128)(2,1)S(1)} %collective-permute-done.15.refs_2_, bf16[8,16384]{1,0:T(8,128)(2,1)S(1)} %collective-permute-done.16.refs_3_), custom_call_target="tpu_custom_call" | custom-call | flops 8589934592 | bytes 33554432 | tf_op jit(solution)/shard_map/hidden_back/pallas_call | solution.py:366
  105.6 1.5 %collective-permute-start.17 = (bf16[32,1024]{1,0:T(8,128)(2,1)S(1)}, bf16[32,1024]{1,0:T(8,128)(2,1)S(1)}, u32[]{:S(2)}, u32[]{:S(2)}) collective-permute-start(bf16[32,1024]{1,0:T(8,128)(2,1)S(1)} %convert_element_type.41), channel_id=1, source_target_pairs={{0,4},{4,0},{8,12},{12,8},{16,20},{20,16},{24,28},{28,24},{1,5},{5... | collective-permute-start | bytes 196616 | tf_op jit(solution)/shard_map/ppermute | solution.py:449
  107.1 4.8 %head_grad.3.refs_4_ = bf16[1024,16384]{1,0:T(8,128)(2,1)} custom-call(bf16[1024,32]{1,0:T(8,128)(2,1)S(1)} %get-tuple-element.33.hidden_t, bf16[8,16384]{1,0:T(8,128)(2,1)S(1)} %bitcast.19, bf16[8,16384]{1,0:T(8,128)(2,1)S(1)} %collective-permute-done.14.refs_1_, bf16[8,16384]{1,0:T(8,128)(2,1)S(1)} %collective-permute-done.15.refs_2_, ...), custom_call_target="tpu_custom_call" | custom-call | flops 2684354560 | bytes 10485760 | tf_op jit(solution)/shard_map/head_grad/pallas_call | solution.py:414
  111.9 0.0 collective-permute-done.17
  111.9 0.1 collective-permute-start.18
  112.0 4.8 %head_grad.4.refs_4_ = bf16[1024,16384]{1,0:T(8,128)(2,1)} custom-call(bf16[1024,32]{1,0:T(8,128)(2,1)S(1)} %get-tuple-element.33.hidden_t, bf16[8,16384]{1,0:T(8,128)(2,1)S(1)} %bitcast.20, bf16[8,16384]{1,0:T(8,128)(2,1)S(1)} %collective-permute-done.14.refs_1_, ...), custom_call_target="tpu_custom_call", output_to_operand_aliasing={{}: (5, {})} | custom-call | flops 2684354560 | bytes 10485760 | tf_op jit(solution)/shard_map/head_grad/pallas_call | solution.py:414
  116.8 0.0 collective-permute-done.18
  116.8 3.3 %collective-permute-start.19 = (bf16[32,1024]{1,0:T(8,128)(2,1)S(1)}, bf16[32,1024]{1,0:T(8,128)(2,1)S(1)}, u32[]{:S(2)}, u32[]{:S(2)}) collective-permute-start(bf16[32,1024]{1,0:T(8,128)(2,1)S(1)} %get-tuple-element.63), channel_id=1, source_target_pairs={{0,16},{4,20},{8,24},{12,28},{16,0},{20,4},{24,8},{28,12},{1,17},{... | collective-permute-start | bytes 196616 | tf_op jit(solution)/shard_map/ppermute | solution.py:449
  120.1 5.4 %head_grad.5 = bf16[1024,16384]{1,0:T(8,128)(2,1)} custom-call(bf16[1024,32]{1,0:T(8,128)(2,1)S(1)} %get-tuple-element.33.hidden_t, bf16[8,16384]{1,0:T(8,128)(2,1)S(1)} %bitcast.21, bf16[8,16384]{1,0:T(8,128)(2,1)S(1)} %collective-permute-done.14.refs_1_, bf16[8,16384]{1,0:T(8,128)(2,1)S(1)} %collective-permute-done.15.refs_2_, ...), custom_call_target="tpu_custom_call", output_to_operand_aliasing={{}: (5, {})} | custom-call | flops 3221225472 | bytes 12582912 | tf_op jit(solution)/shard_map/head_grad/pallas_call | solution.py:414
  125.6 0.0 collective-permute-done.19.other
  125.6 1.4 %in_grad.1 = f32[256,1024]{1,0:T(8,128)} custom-call(bf16[256,32]{1,0:T(8,128)(2,1)S(1)} %get-tuple-element.60.chosen_t, f32[32,1024]{1,0:T(8,128)S(1)} %get-tuple-element.61.preact, f32[32,1024]{1,0:T(8,128)S(1)} %get-tuple-element.64.mine, bf16[32,1024]{1,0:T(8,128)(2,1)S(1)} %collective-permute-done.19.other), custom_call_target="tpu_custom_call" | custom-call | tf_op jit(solution)/shard_map/in_grad/pallas_call | solution.py:437
  (18 shorter events, 0.3 us)
Async XLA Ops:
  1.9 22.9 %collective-permute-start = (bf16[128,1024]{1,0:T(8,128)(2,1)S(1)}, bf16[128,1024]{1,0:T(8,128)(2,1)S(1)}, u32[]{:S(2)}, u32[]{:S(2)}) collective-permute-start(bf16[128,1024]{1,0:T(8,128)(2,1)S(1)} %get-tuple-element.66), channel_id=1, source_target_pairs={{0,2},{1,3},{2,0},{3,1},{4,6},{5,7},{6,4},{7,5},{8,10},{9,11},{10,... | collective-permute-start | bytes 786440 | tf_op jit(solution)/shard_map/ppermute | solution.py:449
  5.0 1.0 copy-start
  6.1 0.8 copy-start.3
  6.9 0.7 copy-start.4
  7.6 0.7 copy-start.7
  8.3 14.0 %copy-start.1 = (bf16[256,1024]{1,0:T(8,128)(2,1)S(1)}, bf16[256,1024]{1,0:T(8,128)(2,1)}, u32[]{:S(2)}) copy-start(bf16[256,1024]{1,0:T(8,128)(2,1)} %refs_0_.1) | copy-start | bytes 1572868
  8.3 23.7 %copy-start.2 = (bf16[256,1024]{1,0:T(8,128)(2,1)S(1)}, bf16[256,1024]{1,0:T(8,128)(2,1)}, u32[]{:S(2)}) copy-start(bf16[256,1024]{1,0:T(8,128)(2,1)} %refs_1_.1) | copy-start | bytes 1572868
  8.3 37.7 %copy-start.5 = (s32[1,256]{1,0:T(1,128)S(1)}, s32[1,256]{1,0:T(1,128)}, u32[]{:S(2)}) copy-start(s32[1,256]{1,0:T(1,128)} %tokens.3) | copy-start | bytes 3076
  8.3 58.1 %copy-start.6 = (s32[1,256]{1,0:T(1,128)S(1)}, s32[1,256]{1,0:T(1,128)}, u32[]{:S(2)}) copy-start(s32[1,256]{1,0:T(1,128)} %labels.1) | copy-start | bytes 3076
  22.2 2.6 %collective-permute-start.3 = (bf16[16,8192]{1,0:T(8,128)(2,1)S(1)}, bf16[16,8192]{1,0:T(8,128)(2,1)S(1)}, u32[]{:S(2)}, u32[]{:S(2)}) collective-permute-start(bf16[16,8192]{1,0:T(8,128)(2,1)S(1)} %get-tuple-element.40), channel_id=1, source_target_pairs={{0,1},{1,0},{2,3},{3,2},{4,5},{5,4},{6,7},{7,6},{8,9},{9,8},{10,11... | collective-permute-start | bytes 786440 | tf_op jit(solution)/shard_map/ppermute | solution.py:449
  22.3 17.7 %collective-permute-start.5 = (bf16[256,1024]{1,0:T(8,128)(2,1)S(1)}, bf16[256,1024]{1,0:T(8,128)(2,1)S(1)}, u32[]{:S(2)}, u32[]{:S(2)}) collective-permute-start(bf16[256,1024]{1,0:T(8,128)(2,1)S(1)} %copy-done.1), channel_id=1, source_target_pairs={{0,1},{1,0},{2,3},{3,2},{4,5},{5,4},{6,7},{7,6},{8,9},{9,8},{10,11... | collective-permute-start | bytes 1572872 | tf_op jit(solution)/shard_map/ppermute | solution.py:449
  22.8 9.2 %collective-permute-start.7 = (bf16[128,1024]{1,0:T(8,128)(2,1)S(1)}, bf16[128,1024]{1,0:T(8,128)(2,1)S(1)}, u32[]{:S(2)}, u32[]{:S(2)}) collective-permute-start(bf16[128,1024]{1,0:T(8,128)(2,1)S(1)} %get-tuple-element.67), channel_id=1, source_target_pairs={{0,2},{1,3},{2,0},{3,1},{4,6},{5,7},{6,4},{7,5},{8,10},{9,11},{10,... | collective-permute-start | bytes 786440 | tf_op jit(solution)/shard_map/ppermute | solution.py:449
  22.8 17.1 %collective-permute-start.8 = (bf16[128,1024]{1,0:T(8,128)(2,1)S(1)}, bf16[128,1024]{1,0:T(8,128)(2,1)S(1)}, u32[]{:S(2)}, u32[]{:S(2)}) collective-permute-start(bf16[128,1024]{1,0:T(8,128)(2,1)S(1)} %get-tuple-element.65), channel_id=1, source_target_pairs={{0,2},{1,3},{2,0},{3,1},{4,6},{5,7},{6,4},{7,5},{8,10},{9,11},{10,... | collective-permute-start | bytes 786440 | tf_op jit(solution)/shard_map/ppermute | solution.py:449
  24.8 1.5 %collective-permute-start.1 = (bf16[16,8192]{1,0:T(8,128)(2,1)S(1)}, bf16[16,8192]{1,0:T(8,128)(2,1)S(1)}, u32[]{:S(2)}, u32[]{:S(2)}) collective-permute-start(bf16[16,8192]{1,0:T(8,128)(2,1)S(1)} %get-tuple-element.37), channel_id=1, source_target_pairs={{0,1},{1,0},{2,3},{3,2},{4,5},{5,4},{6,7},{7,6},{8,9},{9,8},{10,11... | collective-permute-start | bytes 786440 | tf_op jit(solution)/shard_map/ppermute | solution.py:449
  24.9 14.6 %collective-permute-start.4 = (bf16[8,8192]{1,0:T(8,128)(2,1)S(1)}, bf16[8,8192]{1,0:T(8,128)(2,1)S(1)}, u32[]{:S(2)}, u32[]{:S(2)}) collective-permute-start(bf16[8,8192]{1,0:T(8,128)(2,1)S(1)} %slice.56), channel_id=1, source_target_pairs={{0,2},{1,3},{2,0},{3,1},{4,6},{5,7},{6,4},{7,5},{8,10},{9,11},{10,... | collective-permute-start | bytes 393224 | tf_op jit(solution)/shard_map/ppermute | solution.py:449
  26.3 14.1 %collective-permute-start.9 = (bf16[128,1024]{1,0:T(8,128)(2,1)S(1)}, bf16[128,1024]{1,0:T(8,128)(2,1)S(1)}, u32[]{:S(2)}, u32[]{:S(2)}) collective-permute-start(bf16[128,1024]{1,0:T(8,128)(2,1)S(1)} %collective-permute-done.refs_6_), channel_id=1, source_target_pairs={{0,4},{4,0},{8,12},{12,8},{16,20},{20,16},{24,28},{28,24},{1,5},{5... | collective-permute-start | bytes 786440 | tf_op jit(solution)/shard_map/ppermute | solution.py:449
  31.9 12.6 %collective-permute-start.6 = (bf16[256,1024]{1,0:T(8,128)(2,1)S(1)}, bf16[256,1024]{1,0:T(8,128)(2,1)S(1)}, u32[]{:S(2)}, u32[]{:S(2)}) collective-permute-start(bf16[256,1024]{1,0:T(8,128)(2,1)S(1)} %copy-done.2), channel_id=1, source_target_pairs={{0,1},{1,0},{2,3},{3,2},{4,5},{5,4},{6,7},{7,6},{8,9},{9,8},{10,11... | collective-permute-start | bytes 1572872 | tf_op jit(solution)/shard_map/ppermute | solution.py:449
  39.5 5.0 %collective-permute-start.2 = (bf16[8,8192]{1,0:T(8,128)(2,1)S(1)}, bf16[8,8192]{1,0:T(8,128)(2,1)S(1)}, u32[]{:S(2)}, u32[]{:S(2)}) collective-permute-start(bf16[8,8192]{1,0:T(8,128)(2,1)S(1)} %slice.57), channel_id=1, source_target_pairs={{0,2},{1,3},{2,0},{3,1},{4,6},{5,7},{6,4},{7,5},{8,10},{9,11},{10,... | collective-permute-start | bytes 393224 | tf_op jit(solution)/shard_map/ppermute | solution.py:449
  39.8 4.7 %collective-permute-start.12 = (bf16[128,1024]{1,0:T(8,128)(2,1)S(1)}, bf16[128,1024]{1,0:T(8,128)(2,1)S(1)}, u32[]{:S(2)}, u32[]{:S(2)}) collective-permute-start(bf16[128,1024]{1,0:T(8,128)(2,1)S(1)} %collective-permute-done.refs_6_), channel_id=1, source_target_pairs={{0,1},{1,0},{2,3},{3,2},{4,5},{5,4},{6,7},{7,6},{8,9},{9,8},{10,11... | collective-permute-start | bytes 786440 | tf_op jit(solution)/shard_map/ppermute | solution.py:449
  39.9 4.6 %collective-permute-start.10 = (bf16[128,1024]{1,0:T(8,128)(2,1)S(1)}, bf16[128,1024]{1,0:T(8,128)(2,1)S(1)}, u32[]{:S(2)}, u32[]{:S(2)}) collective-permute-start(bf16[128,1024]{1,0:T(8,128)(2,1)S(1)} %collective-permute-done.7.refs_4_), channel_id=1, source_target_pairs={{0,1},{1,0},{2,3},{3,2},{4,5},{5,4},{6,7},{7,6},{8,9},{9,8},{10,11... | collective-permute-start | bytes 786440 | tf_op jit(solution)/shard_map/ppermute | solution.py:449
  40.4 4.1 %collective-permute-start.11 = (bf16[128,1024]{1,0:T(8,128)(2,1)S(1)}, bf16[128,1024]{1,0:T(8,128)(2,1)S(1)}, u32[]{:S(2)}, u32[]{:S(2)}) collective-permute-start(bf16[128,1024]{1,0:T(8,128)(2,1)S(1)} %collective-permute-done.8.refs_5_), channel_id=1, source_target_pairs={{0,1},{1,0},{2,3},{3,2},{4,5},{5,4},{6,7},{7,6},{8,9},{9,8},{10,11... | collective-permute-start | bytes 786440 | tf_op jit(solution)/shard_map/ppermute | solution.py:449
  44.4 1.5 %collective-permute-start.13 = (bf16[128,1024]{1,0:T(8,128)(2,1)S(1)}, bf16[128,1024]{1,0:T(8,128)(2,1)S(1)}, u32[]{:S(2)}, u32[]{:S(2)}) collective-permute-start(bf16[128,1024]{1,0:T(8,128)(2,1)S(1)} %collective-permute-done.9.refs_7_), channel_id=1, source_target_pairs={{0,1},{1,0},{2,3},{3,2},{4,5},{5,4},{6,7},{7,6},{8,9},{9,8},{10,11... | collective-permute-start | bytes 786440 | tf_op jit(solution)/shard_map/ppermute | solution.py:449
  84.3 6.4 %collective-permute-start.14 = (bf16[8,16384]{1,0:T(8,128)(2,1)S(1)}, bf16[8,16384]{1,0:T(8,128)(2,1)S(1)}, u32[]{:S(2)}, u32[]{:S(2)}) collective-permute-start(bf16[8,16384]{1,0:T(8,128)(2,1)S(1)} %bitcast.16), channel_id=1, source_target_pairs={{0,2},{1,3},{2,0},{3,1},{4,6},{5,7},{6,4},{7,5},{8,10},{9,11},{10,... | collective-permute-start | bytes 786440 | tf_op jit(solution)/shard_map/ppermute | solution.py:449
  84.9 5.8 %collective-permute-start.15 = (bf16[8,16384]{1,0:T(8,128)(2,1)S(1)}, bf16[8,16384]{1,0:T(8,128)(2,1)S(1)}, u32[]{:S(2)}, u32[]{:S(2)}) collective-permute-start(bf16[8,16384]{1,0:T(8,128)(2,1)S(1)} %bitcast.17), channel_id=1, source_target_pairs={{0,1},{1,0},{2,3},{3,2},{4,5},{5,4},{6,7},{7,6},{8,9},{9,8},{10,11... | collective-permute-start | bytes 786440 | tf_op jit(solution)/shard_map/ppermute | solution.py:449
  90.7 1.5 %collective-permute-start.16 = (bf16[8,16384]{1,0:T(8,128)(2,1)S(1)}, bf16[8,16384]{1,0:T(8,128)(2,1)S(1)}, u32[]{:S(2)}, u32[]{:S(2)}) collective-permute-start(bf16[8,16384]{1,0:T(8,128)(2,1)S(1)} %collective-permute-done.14.refs_1_), channel_id=1, source_target_pairs={{0,1},{1,0},{2,3},{3,2},{4,5},{5,4},{6,7},{7,6},{8,9},{9,8},{10,11... | collective-permute-start | bytes 786440 | tf_op jit(solution)/shard_map/ppermute | solution.py:449
  105.6 6.3 %collective-permute-start.17 = (bf16[32,1024]{1,0:T(8,128)(2,1)S(1)}, bf16[32,1024]{1,0:T(8,128)(2,1)S(1)}, u32[]{:S(2)}, u32[]{:S(2)}) collective-permute-start(bf16[32,1024]{1,0:T(8,128)(2,1)S(1)} %convert_element_type.41), channel_id=1, source_target_pairs={{0,4},{4,0},{8,12},{12,8},{16,20},{20,16},{24,28},{28,24},{1,5},{5... | collective-permute-start | bytes 196616 | tf_op jit(solution)/shard_map/ppermute | solution.py:449
  111.9 4.9 %collective-permute-start.18 = (bf16[32,1024]{1,0:T(8,128)(2,1)S(1)}, bf16[32,1024]{1,0:T(8,128)(2,1)S(1)}, u32[]{:S(2)}, u32[]{:S(2)}) collective-permute-start(bf16[32,1024]{1,0:T(8,128)(2,1)S(1)} %fusion.4), channel_id=1, source_target_pairs={{0,8},{4,12},{8,0},{12,4},{16,24},{20,28},{24,16},{28,20},{1,9},{5... | collective-permute-start | bytes 196616 | tf_op jit(solution)/shard_map/ppermute | solution.py:449
  116.8 8.7 %collective-permute-start.19 = (bf16[32,1024]{1,0:T(8,128)(2,1)S(1)}, bf16[32,1024]{1,0:T(8,128)(2,1)S(1)}, u32[]{:S(2)}, u32[]{:S(2)}) collective-permute-start(bf16[32,1024]{1,0:T(8,128)(2,1)S(1)} %get-tuple-element.63), channel_id=1, source_target_pairs={{0,16},{4,20},{8,24},{12,28},{16,0},{20,4},{24,8},{28,12},{1,17},{... | collective-permute-start | bytes 196616 | tf_op jit(solution)/shard_map/ppermute | solution.py:449

commit v3 on v2

--- a/solution.py
+++ b/solution.py
@@ -30,6 +30,12 @@
     return dot(a_high, b_high, contract) + (dot(a_high, b_low, contract) + dot(a_low, b_high, contract))
 
 
+def exact(a, b, contract):
+    a_high, a_low = split(a)
+    picked = b.astype(BF16)
+    return dot(a_high, picked, contract) + dot(a_low, picked, contract)
+
+
 NN = ((1,), (0,))
 NT = ((1,), (1,))
 TN = ((0,), (0,))
@@ -37,11 +43,6 @@
 
 def bits_of(count):
     return count.bit_length() - 1
-
-
-def offset_of(position, count):
-    bits = bits_of(count)
-    return sum(((position >> (bits - 1 - bit)) & 1) << bit for bit in range(bits))
 
 
 def small(a, b):
@@ -80,10 +81,12 @@
     return start, run
 
 
-def first_kernel(head_count, group_count, width, place, ids, table, in_w, in_b, w, keep, send, hidden, hidden_t, preact_out, chosen_t, held, sems):
+def first_kernel(head_count, group_count, width, people, place, row_values, matrices, w, keep, send, hidden, hidden_t, preact_out, chosen_t, held, sems):
     start, run = product_loop(width, 0, hidden, w, keep, send, held, sems)
     start()
     rows = keep.shape[0] * 2
+    embed = chosen_t.shape[0]
+    depth = hidden.shape[1]
     row = lax.broadcasted_iota(jnp.int32, (rows, rows), 0)
     column = lax.broadcasted_iota(jnp.int32, (rows, rows), 1)
     position = row // head_count
@@ -92,11 +95,10 @@
     for bit in range(bits):
         offset = offset + (((position >> (bits - 1 - bit)) & 1) << bit)
     slot = (row % head_count) * group_count + jnp.bitwise_xor(offset, place[0])
-    picked = jnp.sum(jnp.where(column == slot, ids[...], 0), axis=1, keepdims=True)
-    people = table.shape[0]
+    picked = jnp.sum(jnp.where(column == slot, row_values[:, depth:], 0.0), axis=1, keepdims=True).astype(jnp.int32)
     onehot = (lax.broadcasted_iota(jnp.int32, (rows, people), 1) == picked).astype(F32).astype(BF16)
-    chosen = dot(onehot, table[...], NN)
-    preact = dot(chosen.astype(BF16), in_w[...], NN) + in_b[...]
+    chosen = dot(onehot, matrices[:people, depth:], NN)
+    preact = dot(chosen.astype(BF16), matrices[:embed, :depth], NN) + row_values[:, :depth]
     value = jnp.maximum(preact, 0.0)
     hidden[...] = value.astype(BF16)
     hidden_t[...] = value.T.astype(BF16)
@@ -112,7 +114,11 @@
 
 
 def forward(place, ids, table, in_w, in_b, w, head_count, group_count, calls):
-    rows = ids.shape[1]
+    rows = ids.shape[0]
+    people, embed = table.shape
+    row_values = jnp.concatenate([in_b, ids.astype(F32)]).reshape(1, -1)
+    tall = max(people, embed)
+    matrices = jnp.concatenate([jnp.pad(value, ((0, tall - value.shape[0]), (0, 0))) for value in (in_w, table)], axis=1)
     depth, columns = w.shape
     share = columns // calls
     width = min(1024, share)
@@ -120,7 +126,7 @@
     whole = pl.BlockSpec(memory_space=pltpu.VMEM)
     hbm = pl.BlockSpec(memory_space=pltpu.HBM)
     shapes = [((rows // 2, share), F32), ((rows // 2, share), BF16)]
-    extra = [((rows, depth), BF16), ((depth, rows), BF16), ((rows, depth), F32), ((table.shape[1], rows), BF16)]
+    extra = [((rows, depth), BF16), ((depth, rows), BF16), ((rows, depth), F32), ((embed, rows), BF16)]
     common = dict(
         scratch_shapes=[pltpu.VMEM((slots, depth, width), BF16), pltpu.SemaphoreType.DMA((slots,))],
         compiler_params=pltpu.CompilerParams(vmem_limit_bytes=40 * 1024 * 1024),
@@ -129,13 +135,13 @@
     )
     shaped = lambda items: [jax.ShapeDtypeStruct(*shape) for shape in items]
     first = pl.pallas_call(
-        functools.partial(first_kernel, head_count, group_count, width),
-        in_specs=[pl.BlockSpec(memory_space=pltpu.SMEM)] + [pl.BlockSpec(value.shape) for value in (ids, table, in_w, in_b)] + [hbm],
+        functools.partial(first_kernel, head_count, group_count, width, people),
+        in_specs=[pl.BlockSpec(memory_space=pltpu.SMEM)] + [whole] * 2 + [hbm],
         out_specs=[whole] * 6,
         out_shape=shaped(shapes + extra),
         **common,
     )
-    keep, send, hidden, hidden_t, preact, chosen_t = first(place, ids, table, in_w, in_b, w)
+    keep, send, hidden, hidden_t, preact, chosen_t = first(place, row_values, matrices, w)
     pairs = [(keep, send)]
     for call in range(1, calls):
         later = pl.pallas_call(
@@ -149,51 +155,78 @@
     return pairs, hidden_t, preact, chosen_t
 
 
+def products(out_part, byte_part):
+    return dot(byte_part, byte_part, NT), dot(out_part, byte_part, NT), dot(out_part, out_part, NT)
+
+
+def mixers(width, step):
+    inner = width // step
+    gap = lax.broadcasted_iota(jnp.int32, (width, inner), 0) - step * lax.broadcasted_iota(jnp.int32, (width, inner), 1)
+    pair = min(2, step)
+    return [
+        (first, jnp.concatenate([jnp.where(gap == first + k, 1.0, 0.0) for k in range(pair)], axis=1).astype(BF16))
+        for first in range(0, step, pair)
+    ]
+
+
+def near_kernel(step, *refs):
+    near, (byte_gram, cross, own_gram, mixed) = refs[:-4], refs[-4:]
+    width = near[0].shape[1]
+    inner = width // step
+    sums = [jnp.zeros(ref.shape, F32) for ref in (byte_gram, cross, own_gram)]
+    for index in range(len(near) // 2):
+        out_part, byte_part = near[2 * index][...], near[2 * index + 1][...]
+        sums = [total + value for total, value in zip(sums, products(out_part, byte_part))]
+        for first, mixer in mixers(width, step):
+            at = index * width + first * inner
+            mixed[:, at : at + mixer.shape[1]] = dot(byte_part, mixer, NN).astype(BF16)
+    byte_gram[...], cross[...], own_gram[...] = sums
+
+
 def prepare_kernel(group_count, step, place, tokens, *refs):
-    near, far = refs[:group_count], refs[group_count : 3 * group_count]
-    byte_full, out_full, byte_mixed, logit_gram, grams, normed_gram, inverse, squares = refs[3 * group_count :]
+    half = group_count // 2
+    near, far, known = refs[:group_count], refs[group_count : group_count + 3 * half], refs[group_count + 3 * half :][:4]
+    byte_full, out_full, byte_mixed, logit_gram, grams, normed_gram, inverse, squares = refs[group_count + 3 * half + 4 :]
     vocab, width = near[0].shape
     part = vocab // 2
     turned = place[1] != 0
     depth = byte_full.shape[1]
     inner = width // step
-    pair = min(2, step)
-    gap = lax.broadcasted_iota(jnp.int32, (width, inner), 0) - step * lax.broadcasted_iota(jnp.int32, (width, inner), 1)
-    byte_gram = jnp.zeros((vocab, vocab), F32)
-    cross = jnp.zeros((vocab, vocab), F32)
-    own_gram = jnp.zeros((vocab, vocab), F32)
-    for position in range(group_count):
-        offset = offset_of(position, group_count)
+    byte_gram, cross, own_gram = (ref[...] for ref in known[:3])
+    for offset in range(group_count):
         start = jnp.bitwise_xor(place[0], offset)
         where = span(start, width)
-        if offset < group_count // 2:
+
+        def mixed_at(j):
+            return pl.ds(pl.multiple_of(j * (depth // step) + start * inner, LANES), inner)
+
+        if offset < half:
             out_full[:, where] = near[2 * offset][...]
             byte_full[:, where] = near[2 * offset + 1][...]
-        else:
-            out_low, byte_low, crossing, handed = (ref[...] for ref in far[4 * (offset - group_count // 2) :][:4])
-            out_full[:part, where] = out_low
-            byte_full[:part, where] = byte_low
-            out_full[part:, where] = jnp.where(turned, handed, crossing)
-            byte_full[part:, where] = jnp.where(turned, crossing, handed)
+            for j in range(step):
+                at = offset * width + j * inner
+                byte_mixed[:, mixed_at(j)] = known[3][:, at : at + inner]
+            continue
+        lows, crossing, handed = (ref[...] for ref in far[3 * (offset - half) :][:3])
+        out_full[:part, where] = lows[:part]
+        byte_full[:part, where] = lows[part:]
+        out_full[part:, where] = jnp.where(turned, handed, crossing)
+        byte_full[part:, where] = jnp.where(turned, crossing, handed)
         out_part, byte_part = out_full[:, where], byte_full[:, where]
-        byte_gram += dot(byte_part, byte_part, NT)
-        cross += dot(out_part, byte_part, NT)
-        own_gram += dot(out_part, out_part, NT)
-    for first in range(0, step, pair):
-        mixer = jnp.concatenate([jnp.where(gap == first + k, 1.0, 0.0) for k in range(pair)], axis=1).astype(BF16)
-        for position in range(group_count):
-            start = jnp.bitwise_xor(place[0], offset_of(position, group_count))
-            mixed = dot(byte_full[:, span(start, width)], mixer, NN).astype(BF16)
-            for k in range(pair):
-                at = pl.multiple_of((first + k) * (depth // step) + start * inner, LANES)
-                byte_mixed[:, pl.ds(at, inner)] = mixed[:, k * inner : (k + 1) * inner]
+        values = products(out_part, byte_part)
+        byte_gram, cross, own_gram = byte_gram + values[0], cross + values[1], own_gram + values[2]
+        for first, mixer in mixers(width, step):
+            mixed = dot(byte_part, mixer, NN).astype(BF16)
+            for k in range(mixer.shape[1] // inner):
+                byte_mixed[:, mixed_at(first + k)] = mixed[:, k * inner : (k + 1) * inner]
     count = tokens.shape[1]
     onehot = (lax.broadcasted_iota(jnp.int32, (vocab, count), 0) == tokens[...]).astype(F32)
-    logit = fine(cross, onehot, NN)
+    logit = exact(cross, onehot, NN)
     logit_gram[...] = logit
-    half = fine(byte_gram, onehot, NN)
-    total = jnp.sum(onehot * half, axis=0, keepdims=True)
-    both = fine(onehot, half, TN)
+    picked = exact(byte_gram, onehot, NN)
+    total = jnp.sum(onehot * picked, axis=0, keepdims=True)
+    picked_high, picked_low = split(picked)
+    both = dot(onehot.astype(BF16), picked_high, TN) + dot(onehot.astype(BF16), picked_low, TN)
     scale = lax.rsqrt(total / depth + EPSILON)
     eye = lax.broadcasted_iota(jnp.int32, (count, count), 0) == lax.broadcasted_iota(jnp.int32, (count, count), 1)
     down = jnp.sum(jnp.where(eye, scale, 0.0), axis=1, keepdims=True)
@@ -212,6 +245,17 @@
     count = tokens.shape[1]
     depth = width * group_count
     whole = pl.BlockSpec(memory_space=pltpu.VMEM)
+    shaped = lambda shapes: [jax.ShapeDtypeStruct(*shape) for shape in shapes]
+    known_shapes = [((vocab, vocab), F32)] * 3 + [((vocab, depth // 2), BF16)]
+    known = pl.pallas_call(
+        functools.partial(near_kernel, step),
+        in_specs=[whole] * len(near),
+        out_specs=[whole] * 4,
+        out_shape=shaped(known_shapes),
+        compiler_params=pltpu.CompilerParams(vmem_limit_bytes=16 * 1024 * 1024),
+        cost_estimate=pl.CostEstimate(flops=2**30, bytes_accessed=2**22, transcendentals=0),
+        name="prepare_near",
+    )(*near)
     shapes = [
         ((vocab, depth), BF16),
         ((vocab, depth), BF16),
@@ -224,13 +268,13 @@
     ]
     return pl.pallas_call(
         functools.partial(prepare_kernel, group_count, step),
-        in_specs=[pl.BlockSpec(memory_space=pltpu.SMEM)] + [whole] * (1 + 3 * group_count),
+        in_specs=[pl.BlockSpec(memory_space=pltpu.SMEM)] + [whole] * (5 + len(near) + len(far)),
         out_specs=[whole] * len(shapes),
-        out_shape=[jax.ShapeDtypeStruct(*shape) for shape in shapes],
+        out_shape=shaped(shapes),
         compiler_params=pltpu.CompilerParams(vmem_limit_bytes=16 * 1024 * 1024),
-        cost_estimate=pl.CostEstimate(flops=2**31, bytes_accessed=2**23, transcendentals=0),
+        cost_estimate=pl.CostEstimate(flops=2**30, bytes_accessed=2**23, transcendentals=0),
         name="prepare",
-    )(place, tokens, *near, *far)
+    )(place, tokens, *near, *far, *known)
 
 
 def train_kernel(
@@ -268,8 +312,8 @@
     out_b = dot(b, out_full[...], NT)
     byte_b = dot(b, byte_full[...], NT)
     gram_b = dot(b, b, NT)
-    low = fine(table_a, onehot, NN) * scale
-    in_b = fine(byte_b, onehot, NN)
+    low = exact(table_a, onehot, NN) * scale
+    in_b = exact(byte_b, onehot, NN)
     s = 1.0 / (depth * rank) ** 0.5
     c = 4.0 / depth**0.5
 
@@ -303,8 +347,8 @@
     total_b = more + more1 + small(more1, more)
     total_both = on_both + on_both1 + small(more1, on_both)
     total_out, total_in = total_both[:, :vocab], total_both[:, vocab:]
-    on_byte = fine(total_in, onehot, NT)
-    on_a = fine((-learn_rate) * scale * (d_low + d_low1), onehot, NT).astype(BF16)
+    on_byte = exact(total_in, onehot, NT)
+    on_a = exact((-learn_rate) * scale * (d_low + d_low1), onehot, NT).astype(BF16)
     pieces = [dot(on_a, byte_mixed[:, j * inner : (j + 1) * inner], NN) for j in range(step)]
     deltas[:rows, :] = jnp.concatenate(pieces, axis=0).T.astype(BF16)
     delta_b = dot(total_b.astype(BF16), b, NN) + dot(total_out.astype(BF16), out_full[...], NN) + dot(on_byte.astype(BF16), byte_full[...], NN)
@@ -360,8 +404,8 @@
 def back(w, parts):
     depth, columns = w.shape
     rows = sum(part.shape[0] for part in parts)
-    width = min(1024, columns)
-    slots = min(6, columns // width)
+    width = min(2048, columns)
+    slots = min(4, columns // width)
     whole = pl.BlockSpec(memory_space=pltpu.VMEM)
     return pl.pallas_call(
         functools.partial(back_kernel, width),
@@ -462,29 +506,31 @@
     columns = head_weight.shape[1]
     depth = byte_table.shape[1] * group_count
     rank = columns * head_count // (2 * depth)
-    slots = client_ids.shape[0]
     top = bits_of(group_count) - 1
     side = lax.axis_index("head") & 1
     place = jnp.stack([lax.axis_index("client"), side]).astype(jnp.int32)
     part = out_table.shape[0] // 2
     out_low, out_high, byte_low, byte_high = out_table[:part], out_table[part:], byte_table[:part], byte_table[part:]
     crossing = swap(jnp.where(side == 0, out_high, byte_high), "client", top)
-    far = [swap(out_low, "client", top), swap(byte_low, "client", top)]
+    far = [swap(jnp.concatenate([out_low, byte_low]), "client", top)]
     near = [out_table, byte_table]
     for bit in range(top):
         near = near + [swap(value, "client", bit) for value in near]
     pairs, hidden_t, preact, chosen_t = forward(
-        place, client_ids.reshape(1, slots), client_table, in_weight, in_bias.reshape(1, -1), head_weight, head_count, group_count, 2
+        place, client_ids, client_table, in_weight, in_bias, head_weight, head_count, group_count, 2
     )
     crossing, pairs[0] = lax.optimization_barrier((crossing, pairs[0]))
     handed = swap(crossing, "head", 0)
-    far = far + [crossing, handed]
+    far, late = far + [crossing], [handed]
     for bit in range(top):
         far = far + [swap(value, "client", bit) for value in far]
+        late = late + [swap(value, "client", bit) for value in late]
+    far = [value for at in range(1 << top) for value in (*far[2 * at : 2 * at + 2], late[at])]
     prepared = prepare(place, tokens, near, far, LANES // rank)
     halves = []
     for keep, send in pairs:
-        total = keep + swap(send, "client", 0).astype(F32)
+        got = swap(send, "client", 0)
+        total = keep + got.astype(F32)
         for bit in range(1, top + 1):
             half = total.shape[0] // 2
             got = swap(total[half:].astype(BF16), "client", bit)

time: 127 us -> 122 us (0.961)
  waiting for transfers between devices: 25.7 us -> 21.5 us
  local copies, waits for them, and re-layouts: 3.48 us -> 0.28 us
  other arithmetic: 1.58 us -> 3.91 us
  blocking collectives: 26.7 us -> 25.3 us
    ppermute x20 -> x18, waiting for transfers between devices: 25.7 us -> 21.5 us  [swap(): return lax.ppermute(value, axis, [(i, i ^ 1 << bit) for i in range(size)])]
    unnamed x17 -> x11, local copies, waits for them, and re-layouts: 3.41 us -> 0.2 us
    pallas_call x1 -> x2, Pallas kernels: 7.22 us -> 9.34 us  [the longest x1 7.22 us: forward(): first(place, row_values, matrices, w)]
    pallas_call x1, Pallas kernels: 5.55 us -> 3.69 us  [prepare(): pl.pallas_call(functools.partial(prepare_kernel, group_count, step), in_s...]
    concatenate x0 -> x3, other arithmetic: none -> 1.61 us  [the longest x1 0.88 us: forward(): jnp.concatenate([jnp.pad(value, ((0, tall - value.shape[0]), (0, 0))) for...]
    ppermute x20 -> x18, starting transfers between devices: 13.7 us -> 14.8 us  [swap(): return lax.ppermute(value, axis, [(i, i ^ 1 << bit) for i in range(size)])]
  transfers between devices with their start and end apart: 20 -> 18, of which waited for: 7 -> 6; matrix products, arithmetic and copies ran while one was open for 0% -> 2% of each run, Pallas kernels for 23% -> 26%
where the time goes in v3:
time: 122 us
  Pallas kernels  55.1 us (45%)
  blocking collectives  25.3 us (21%)
  waiting for transfers between devices  21.5 us (18%)
  starting transfers between devices  14.8 us (12%)
  other arithmetic  3.91 us (3%)
    ppermute x18, waiting for transfers between devices, swap(): return lax.ppermute(value, axis, [(i, i ^ 1 << bit) for i in range(size)])  21.5 us
    pallas_call x3, Pallas kernels, grad(): pl.pallas_call(functools.partial(grad_kernel, width, edges[call], count),...  15 us
    ppermute x18, starting transfers between devices, swap(): return lax.ppermute(value, axis, [(i, i ^ 1 << bit) for i in range(size)])  14.8 us
    all_to_all x1, blocking collectives, steps(): owned = lax.all_to_all(own, 'head', split_axis=0, concat_axis=0, tiled=True)  13.8 us
    pallas_call x1, Pallas kernels, back(): pl.pallas_call(functools.partial(back_kernel, width), in_specs=[pl.BlockS...  12.9 us
    all_to_all x1, blocking collectives, steps(): lax.all_to_all(deltas.reshape(own.shape), 'head', split_axis=0, concat_ax...  11.5 us
    pallas_call x1, Pallas kernels, forward(): first(place, row_values, matrices, w)  7.22 us
    pallas_call x1, Pallas kernels, forward(): pairs.append(later(hidden, w))  6.76 us
  transfers between devices with their start and end apart: 18, of which 6 were waited for; matrix products, arithmetic and copies ran while one was open for 2% of the time, Pallas kernels for 26%

profile of v3, /device:TPU:0, one launch (start us, length us, event | category | flops | bytes accessed | tf_op | source)
XLA Modules:
  0.0 121.7 jit_solution(10884921877843201504)
XLA Ops:
  0.6 0.0 copy-start.4
  0.6 1.3 %fusion.8 = (bf16[128,1024]{1,0:T(8,128)(2,1)S(1)}, bf16[128,1024]{1,0:T(8,128)(2,1)S(1)}, bf16[128,1024]{1,0:T(8,128)(2,1)S(1)}) fusion(bf16[256,1024]{1,0:T(8,128)(2,1)} %refs_0_.3, bf16[256,1024]{1,0:T(8,128)(2,1)} %refs_1_.3, pred[]{:T(512)S(6)} %eq.3), kind=kLoop, calls=%fused_computation.23 | loop fusion | flops 131072 | bytes 1835009 | tf_op jit(solution)/shard_map/slice | solution.py:513
  2.0 3.1 %collective-permute-start = (bf16[128,1024]{1,0:T(8,128)(2,1)S(1)}, bf16[128,1024]{1,0:T(8,128)(2,1)S(1)}, u32[]{:S(2)}, u32[]{:S(2)}) collective-permute-start(bf16[128,1024]{1,0:T(8,128)(2,1)S(1)} %get-tuple-element.74), channel_id=1, source_target_pairs={{0,2},{1,3},{2,0},{3,1},{4,6},{5,7},{6,4},{7,5},{8,10},{9,11},{10,... | collective-permute-start | bytes 786440 | tf_op jit(solution)/shard_map/ppermute | solution.py:493
  5.0 0.7 convert_element_type.40
  5.7 0.7 pad_maximum_fusion.2
  6.4 0.1 pad_add_fusion.place
  6.4 0.0 copy-done.4
  6.4 0.9 fusion.1.matrices
  7.3 7.2 %factors.2 = (f32[16,8192]{1,0:T(8,128)S(1)}, bf16[16,8192]{1,0:T(8,128)(2,1)S(1)}, bf16[32,1024]{1,0:T(8,128)(2,1)S(1)}, bf16[1024,32]{1,0:T(8,128)(2,1)S(1)}, ...) custom-call(s32[2]{0:T(128)S(1)} %pad_add_fusion.place, f32[1,1056]{1,0:T(1,128)S(1)} %reshape.24.row_values, ...), custom_call_target="tpu_custom_call" | custom-call | flops 8589934592 | bytes 16777216 | tf_op jit(solution)/shard_map/factors/pallas_call | solution.py:144
  14.6 0.0 copy-start
  14.6 0.0 copy-start.1
  14.6 6.8 %factors.3 = (f32[16,8192]{1,0:T(8,128)S(1)}, bf16[16,8192]{1,0:T(8,128)(2,1)S(1)}) custom-call(bf16[32,1024]{1,0:T(8,128)(2,1)S(1)} %get-tuple-element.42.hidden, bf16[1024,16384]{1,0:T(8,128)(2,1)} %w.5), custom_call_target="tpu_custom_call" | custom-call | flops 8589934592 | bytes 16777216 | tf_op jit(solution)/shard_map/factors/pallas_call | solution.py:154
  21.4 0.1 collective-permute-start.3
  21.4 0.0 copy-done
  21.4 0.5 collective-permute-start.5
  21.9 0.1 collective-permute-start.6
  22.1 0.1 collective-permute-start.7
  22.1 0.0 collective-permute-done.refs_5_
  22.2 0.5 collective-permute-start.1
  22.6 0.3 collective-permute-done.3
  23.0 0.1 convert_add_fusion
  23.0 1.4 %collective-permute-start.4 = (bf16[8,8192]{1,0:T(8,128)(2,1)S(1)}, bf16[8,8192]{1,0:T(8,128)(2,1)S(1)}, u32[]{:S(2)}, u32[]{:S(2)}) collective-permute-start(bf16[8,8192]{1,0:T(8,128)(2,1)S(1)} %slice.56), channel_id=1, source_target_pairs={{0,2},{1,3},{2,0},{3,1},{4,6},{5,7},{6,4},{7,5},{8,10},{9,11},{10,... | collective-permute-start | bytes 393224 | tf_op jit(solution)/shard_map/ppermute | solution.py:493
  24.5 0.4 collective-permute-done.1
  24.8 1.5 %collective-permute-start.8 = (bf16[128,1024]{1,0:T(8,128)(2,1)S(1)}, bf16[128,1024]{1,0:T(8,128)(2,1)S(1)}, u32[]{:S(2)}, u32[]{:S(2)}) collective-permute-start(bf16[128,1024]{1,0:T(8,128)(2,1)S(1)} %collective-permute-done.refs_5_), channel_id=1, source_target_pairs={{0,4},{4,0},{8,12},{12,8},{16,20},{20,16},{24,28},{28,24},{1,5},{5... | collective-permute-start | bytes 786440 | tf_op jit(solution)/shard_map/ppermute | solution.py:493
  26.3 0.1 convert_add_fusion.1
  26.4 12.8 %collective-permute-done.4 = bf16[8,8192]{1,0:T(8,128)(2,1)S(1)} collective-permute-done((bf16[8,8192]{1,0:T(8,128)(2,1)S(1)}, bf16[8,8192]{1,0:T(8,128)(2,1)S(1)}, u32[]{:S(2)}, u32[]{:S(2)}) %collective-permute-start.4) | collective-permute-done | bytes 131104 | tf_op jit(solution)/shard_map/ppermute | solution.py:493
  39.2 0.3 collective-permute-start.2
  39.5 0.0 collective-permute-done.7.refs_4_
  39.5 0.0 collective-permute-start.9
  39.5 0.0 copy-start.2
  39.6 0.0 collective-permute-done.5.refs_2_
  39.6 0.6 collective-permute-start.10
  40.1 0.0 collective-permute-done.8.refs_6_
  40.1 0.1 collective-permute-start.11
  40.2 0.0 collective-permute-done.6.refs_3_
  40.2 2.1 %prepare_near.1 = (f32[256,256]{1,0:T(8,128)S(1)}, f32[256,256]{1,0:T(8,128)S(1)}, f32[256,256]{1,0:T(8,128)S(1)}, bf16[256,2048]{1,0:T(8,128)(2,1)S(1)}) custom-call(bf16[256,1024]{1,0:T(8,128)(2,1)S(1)} %copy-done, bf16[256,1024]{1,0:T(8,128)(2,1)S(1)} %copy-done.1, bf16[256,1024]{1,0:T(8,128)(2,1)S(1)} %collective-permute-done.5.refs_2_, ...), custom_call_target="tpu_custom_call" | custom-call | flops 1073741824 | bytes 4194304 | tf_op jit(solution)/shard_map/prepare_near/pallas_call | solution.py:250
  42.4 1.8 %collective-permute-done.2 = bf16[8,8192]{1,0:T(8,128)(2,1)S(1)} collective-permute-done((bf16[8,8192]{1,0:T(8,128)(2,1)S(1)}, bf16[8,8192]{1,0:T(8,128)(2,1)S(1)}, u32[]{:S(2)}, u32[]{:S(2)}) %collective-permute-start.2) | collective-permute-done | bytes 131104 | tf_op jit(solution)/shard_map/ppermute | solution.py:493
  44.3 0.0 collective-permute-done.10.refs_8_
  44.3 0.0 collective-permute-done.11.refs_9_
  44.3 0.0 collective-permute-done.9.refs_7_
  44.3 0.0 copy-done.2
  44.3 0.0 copy-start.3
  44.3 3.7 %prepare.1 = (bf16[256,4096]{1,0:T(8,128)(2,1)S(1)}, bf16[256,4096]{1,0:T(8,128)(2,1)S(1)}, bf16[256,4096]{1,0:T(8,128)(2,1)S(1)}, f32[256,256]{1,0:T(8,128)S(1)...) custom-call(s32[2]{0:T(128)S(1)} %pad_add_fusion.place, ...), custom_call_target="tpu_custom_call" | custom-call | flops 1073741824 | bytes 8388608 | tf_op jit(solution)/shard_map/prepare/pallas_call | solution.py:269
  48.0 13.8 %all_to_all.10 = bf16[8,128,128]{2,1,0:T(8,128)(2,1)S(1)} all-to-all(bf16[8,128,128]{2,1,0:T(8,128)(2,1)S(1)} %pad_maximum_fusion.1), channel_id=1, replica_groups=mesh['head'=8,'client'=4] {'head'}, dimensions={0} | all-to-all | bytes 524288 | tf_op jit(solution)/shard_map/all_to_all | solution.py:541
  61.8 6.0 %train.1 = (bf16[1024,128]{1,0:T(8,128)(2,1)S(1)}, f32[1,128]{1,0:T(1,128)}) custom-call(bf16[1024,128]{1,0:T(8,128)(2,1)S(1)} %bitcast.20, s32[1,256]{1,0:T(1,128)S(1)} %copy-done.2, s32[1,256]{1,0:T(1,128)S(1)} %copy-done.3, bf16[256,4096]{1,0:T(8,128)(2,1)S(1)} %get-tuple-element.59.byte_full, bf16[256,4096]{1,0:T(8,128)(2,1)S(1)} %get-tuple-element.60.out_full, ...), custom_call_target="tpu_custom_call" | custom-call | flops 2147483648 | bytes 8388608 | tf_op jit(solution)/shard_map/train/pallas_call | solution.py:363
  67.8 11.5 %all_to_all.11 = bf16[8,128,128]{2,1,0:T(8,128)(2,1)S(1)} all-to-all(bf16[8,128,128]{2,1,0:T(8,128)(2,1)S(1)} %bitcast.21), channel_id=1, replica_groups=mesh['head'=8,'client'=4] {'head'}, dimensions={0} | all-to-all | bytes 524288 | tf_op jit(solution)/shard_map/all_to_all | solution.py:543
  79.3 0.2 copy.21
  79.5 1.8 %collective-permute-start.12 = (bf16[8,16384]{1,0:T(8,128)(2,1)S(1)}, bf16[8,16384]{1,0:T(8,128)(2,1)S(1)}, u32[]{:S(2)}, u32[]{:S(2)}) collective-permute-start(bf16[8,16384]{1,0:T(8,128)(2,1)S(1)} %bitcast.14), channel_id=1, source_target_pairs={{0,2},{1,3},{2,0},{3,1},{4,6},{5,7},{6,4},{7,5},{8,10},{9,11},{10,... | collective-permute-start | bytes 786440 | tf_op jit(solution)/shard_map/ppermute | solution.py:493
  81.3 0.0 collective-permute-start.13
  81.3 4.7 %collective-permute-done.12.refs_1_ = bf16[8,16384]{1,0:T(8,128)(2,1)S(1)} collective-permute-done((bf16[8,16384]{1,0:T(8,128)(2,1)S(1)}, bf16[8,16384]{1,0:T(8,128)(2,1)S(1)}, u32[]{:S(2)}, u32[]{:S(2)}) %collective-permute-start.12) | collective-permute-done | bytes 262176 | tf_op jit(solution)/shard_map/ppermute | solution.py:493
  85.9 0.0 collective-permute-start.14
  85.9 0.0 collective-permute-done.13.refs_2_
  85.9 1.5 %collective-permute-done.14.refs_3_ = bf16[8,16384]{1,0:T(8,128)(2,1)S(1)} collective-permute-done((bf16[8,16384]{1,0:T(8,128)(2,1)S(1)}, bf16[8,16384]{1,0:T(8,128)(2,1)S(1)}, u32[]{:S(2)}, u32[]{:S(2)}) %collective-permute-start.14) | collective-permute-done | bytes 262176 | tf_op jit(solution)/shard_map/ppermute | solution.py:493
  87.5 12.9 %hidden_back.1 = f32[32,1024]{1,0:T(8,128)S(1)} custom-call(bf16[1024,16384]{1,0:T(8,128)(2,1)} %w.5, bf16[8,16384]{1,0:T(8,128)(2,1)S(1)} %bitcast.16, bf16[8,16384]{1,0:T(8,128)(2,1)S(1)} %collective-permute-done.12.refs_1_, bf16[8,16384]{1,0:T(8,128)(2,1)S(1)} %collective-permute-done.13.refs_2_, bf16[8,16384]{1,0:T(8,128)(2,1)S(1)} %collective-permute-done.14.refs_3_), custom_call_target="tpu_custom_call" | custom-call | flops 8589934592 | bytes 33554432 | tf_op jit(solution)/shard_map/hidden_back/pallas_call | solution.py:410
  100.4 1.4 %collective-permute-start.15 = (bf16[32,1024]{1,0:T(8,128)(2,1)S(1)}, bf16[32,1024]{1,0:T(8,128)(2,1)S(1)}, u32[]{:S(2)}, u32[]{:S(2)}) collective-permute-start(bf16[32,1024]{1,0:T(8,128)(2,1)S(1)} %convert_element_type.47), channel_id=1, source_target_pairs={{0,4},{4,0},{8,12},{12,8},{16,20},{20,16},{24,28},{28,24},{1,5},{5... | collective-permute-start | bytes 196616 | tf_op jit(solution)/shard_map/ppermute | solution.py:493
  101.8 4.8 %head_grad.3.refs_4_ = bf16[1024,16384]{1,0:T(8,128)(2,1)} custom-call(bf16[1024,32]{1,0:T(8,128)(2,1)S(1)} %get-tuple-element.37.hidden_t, bf16[8,16384]{1,0:T(8,128)(2,1)S(1)} %bitcast.17, bf16[8,16384]{1,0:T(8,128)(2,1)S(1)} %collective-permute-done.12.refs_1_, bf16[8,16384]{1,0:T(8,128)(2,1)S(1)} %collective-permute-done.13.refs_2_, ...), custom_call_target="tpu_custom_call" | custom-call | flops 2684354560 | bytes 10485760 | tf_op jit(solution)/shard_map/head_grad/pallas_call | solution.py:458
  106.5 0.0 collective-permute-done.15
  106.6 0.1 collective-permute-start.16
  106.7 4.8 %head_grad.4.refs_4_ = bf16[1024,16384]{1,0:T(8,128)(2,1)} custom-call(bf16[1024,32]{1,0:T(8,128)(2,1)S(1)} %get-tuple-element.37.hidden_t, bf16[8,16384]{1,0:T(8,128)(2,1)S(1)} %bitcast.18, bf16[8,16384]{1,0:T(8,128)(2,1)S(1)} %collective-permute-done.12.refs_1_, ...), custom_call_target="tpu_custom_call", output_to_operand_aliasing={{}: (5, {})} | custom-call | flops 2684354560 | bytes 10485760 | tf_op jit(solution)/shard_map/head_grad/pallas_call | solution.py:458
  111.5 0.0 collective-permute-done.16
  111.5 3.4 %collective-permute-start.17 = (bf16[32,1024]{1,0:T(8,128)(2,1)S(1)}, bf16[32,1024]{1,0:T(8,128)(2,1)S(1)}, u32[]{:S(2)}, u32[]{:S(2)}) collective-permute-start(bf16[32,1024]{1,0:T(8,128)(2,1)S(1)} %get-tuple-element.71), channel_id=1, source_target_pairs={{0,16},{4,20},{8,24},{12,28},{16,0},{20,4},{24,8},{28,12},{1,17},{... | collective-permute-start | bytes 196616 | tf_op jit(solution)/shard_map/ppermute | solution.py:493
  114.9 5.4 %head_grad.5 = bf16[1024,16384]{1,0:T(8,128)(2,1)} custom-call(bf16[1024,32]{1,0:T(8,128)(2,1)S(1)} %get-tuple-element.37.hidden_t, bf16[8,16384]{1,0:T(8,128)(2,1)S(1)} %bitcast.19, bf16[8,16384]{1,0:T(8,128)(2,1)S(1)} %collective-permute-done.12.refs_1_, bf16[8,16384]{1,0:T(8,128)(2,1)S(1)} %collective-permute-done.13.refs_2_, ...), custom_call_target="tpu_custom_call", output_to_operand_aliasing={{}: (5, {})} | custom-call | flops 3221225472 | bytes 12582912 | tf_op jit(solution)/shard_map/head_grad/pallas_call | solution.py:458
  120.3 0.0 collective-permute-done.17.other
  120.3 1.4 %in_grad.1 = f32[256,1024]{1,0:T(8,128)} custom-call(bf16[256,32]{1,0:T(8,128)(2,1)S(1)} %get-tuple-element.68.chosen_t, f32[32,1024]{1,0:T(8,128)S(1)} %get-tuple-element.69.preact, f32[32,1024]{1,0:T(8,128)S(1)} %get-tuple-element.72.mine, bf16[32,1024]{1,0:T(8,128)(2,1)S(1)} %collective-permute-done.17.other), custom_call_target="tpu_custom_call" | custom-call | tf_op jit(solution)/shard_map/in_grad/pallas_call | solution.py:481
  (14 shorter events, 0.3 us)
Async XLA Ops:
  0.6 5.8 %copy-start.4 = (bf16[256,1024]{1,0:T(8,128)(2,1)S(1)}, bf16[256,1024]{1,0:T(8,128)(2,1)}, u32[]{:S(2)}) copy-start(bf16[256,1024]{1,0:T(8,128)(2,1)} %param.11) | copy-start | bytes 1572868
  2.0 20.2 %collective-permute-start = (bf16[128,1024]{1,0:T(8,128)(2,1)S(1)}, bf16[128,1024]{1,0:T(8,128)(2,1)S(1)}, u32[]{:S(2)}, u32[]{:S(2)}) collective-permute-start(bf16[128,1024]{1,0:T(8,128)(2,1)S(1)} %get-tuple-element.74), channel_id=1, source_target_pairs={{0,2},{1,3},{2,0},{3,1},{4,6},{5,7},{6,4},{7,5},{8,10},{9,11},{10,... | collective-permute-start | bytes 786440 | tf_op jit(solution)/shard_map/ppermute | solution.py:493
  14.6 6.9 %copy-start = (bf16[256,1024]{1,0:T(8,128)(2,1)S(1)}, bf16[256,1024]{1,0:T(8,128)(2,1)}, u32[]{:S(2)}) copy-start(bf16[256,1024]{1,0:T(8,128)(2,1)} %refs_0_.3) | copy-start | bytes 1572868
  14.6 7.4 %copy-start.1 = (bf16[256,1024]{1,0:T(8,128)(2,1)S(1)}, bf16[256,1024]{1,0:T(8,128)(2,1)}, u32[]{:S(2)}) copy-start(bf16[256,1024]{1,0:T(8,128)(2,1)} %refs_1_.3) | copy-start | bytes 1572868
  21.4 1.6 %collective-permute-start.3 = (bf16[16,8192]{1,0:T(8,128)(2,1)S(1)}, bf16[16,8192]{1,0:T(8,128)(2,1)S(1)}, u32[]{:S(2)}, u32[]{:S(2)}) collective-permute-start(bf16[16,8192]{1,0:T(8,128)(2,1)S(1)} %get-tuple-element.44), channel_id=1, source_target_pairs={{0,1},{1,0},{2,3},{3,2},{4,5},{5,4},{6,7},{7,6},{8,9},{9,8},{10,11... | collective-permute-start | bytes 786440 | tf_op jit(solution)/shard_map/ppermute | solution.py:493
  21.4 18.1 %collective-permute-start.5 = (bf16[256,1024]{1,0:T(8,128)(2,1)S(1)}, bf16[256,1024]{1,0:T(8,128)(2,1)S(1)}, u32[]{:S(2)}, u32[]{:S(2)}) collective-permute-start(bf16[256,1024]{1,0:T(8,128)(2,1)S(1)} %copy-done), channel_id=1, source_target_pairs={{0,1},{1,0},{2,3},{3,2},{4,5},{5,4},{6,7},{7,6},{8,9},{9,8},{10,11... | collective-permute-start | bytes 1572872 | tf_op jit(solution)/shard_map/ppermute | solution.py:493
  21.9 18.3 %collective-permute-start.6 = (bf16[256,1024]{1,0:T(8,128)(2,1)S(1)}, bf16[256,1024]{1,0:T(8,128)(2,1)S(1)}, u32[]{:S(2)}, u32[]{:S(2)}) collective-permute-start(bf16[256,1024]{1,0:T(8,128)(2,1)S(1)} %copy-done.1), channel_id=1, source_target_pairs={{0,1},{1,0},{2,3},{3,2},{4,5},{5,4},{6,7},{7,6},{8,9},{9,8},{10,11... | collective-permute-start | bytes 1572872 | tf_op jit(solution)/shard_map/ppermute | solution.py:493
  22.1 17.4 %collective-permute-start.7 = (bf16[256,1024]{1,0:T(8,128)(2,1)S(1)}, bf16[256,1024]{1,0:T(8,128)(2,1)S(1)}, u32[]{:S(2)}, u32[]{:S(2)}) collective-permute-start(bf16[256,1024]{1,0:T(8,128)(2,1)S(1)} %pad_maximum_fusion), channel_id=1, source_target_pairs={{0,2},{1,3},{2,0},{3,1},{4,6},{5,7},{6,4},{7,5},{8,10},{9,11},{10,... | collective-permute-start | bytes 1572872 | tf_op jit(solution)/shard_map/ppermute | solution.py:493
  22.2 2.7 %collective-permute-start.1 = (bf16[16,8192]{1,0:T(8,128)(2,1)S(1)}, bf16[16,8192]{1,0:T(8,128)(2,1)S(1)}, u32[]{:S(2)}, u32[]{:S(2)}) collective-permute-start(bf16[16,8192]{1,0:T(8,128)(2,1)S(1)} %get-tuple-element.41), channel_id=1, source_target_pairs={{0,1},{1,0},{2,3},{3,2},{4,5},{5,4},{6,7},{7,6},{8,9},{9,8},{10,11... | collective-permute-start | bytes 786440 | tf_op jit(solution)/shard_map/ppermute | solution.py:493
  23.0 16.1 %collective-permute-start.4 = (bf16[8,8192]{1,0:T(8,128)(2,1)S(1)}, bf16[8,8192]{1,0:T(8,128)(2,1)S(1)}, u32[]{:S(2)}, u32[]{:S(2)}) collective-permute-start(bf16[8,8192]{1,0:T(8,128)(2,1)S(1)} %slice.56), channel_id=1, source_target_pairs={{0,2},{1,3},{2,0},{3,1},{4,6},{5,7},{6,4},{7,5},{8,10},{9,11},{10,... | collective-permute-start | bytes 393224 | tf_op jit(solution)/shard_map/ppermute | solution.py:493
  24.8 15.3 %collective-permute-start.8 = (bf16[128,1024]{1,0:T(8,128)(2,1)S(1)}, bf16[128,1024]{1,0:T(8,128)(2,1)S(1)}, u32[]{:S(2)}, u32[]{:S(2)}) collective-permute-start(bf16[128,1024]{1,0:T(8,128)(2,1)S(1)} %collective-permute-done.refs_5_), channel_id=1, source_target_pairs={{0,4},{4,0},{8,12},{12,8},{16,20},{20,16},{24,28},{28,24},{1,5},{5... | collective-permute-start | bytes 786440 | tf_op jit(solution)/shard_map/ppermute | solution.py:493
  39.2 5.0 %collective-permute-start.2 = (bf16[8,8192]{1,0:T(8,128)(2,1)S(1)}, bf16[8,8192]{1,0:T(8,128)(2,1)S(1)}, u32[]{:S(2)}, u32[]{:S(2)}) collective-permute-start(bf16[8,8192]{1,0:T(8,128)(2,1)S(1)} %slice.57), channel_id=1, source_target_pairs={{0,2},{1,3},{2,0},{3,1},{4,6},{5,7},{6,4},{7,5},{8,10},{9,11},{10,... | collective-permute-start | bytes 393224 | tf_op jit(solution)/shard_map/ppermute | solution.py:493
  39.5 4.8 %collective-permute-start.9 = (bf16[256,1024]{1,0:T(8,128)(2,1)S(1)}, bf16[256,1024]{1,0:T(8,128)(2,1)S(1)}, u32[]{:S(2)}, u32[]{:S(2)}) collective-permute-start(bf16[256,1024]{1,0:T(8,128)(2,1)S(1)} %collective-permute-done.7.refs_4_), channel_id=1, source_target_pairs={{0,1},{1,0},{2,3},{3,2},{4,5},{5,4},{6,7},{7,6},{8,9},{9,8},{10,11... | collective-permute-start | bytes 1572872 | tf_op jit(solution)/shard_map/ppermute | solution.py:493
  39.5 4.7 %copy-start.2 = (s32[1,256]{1,0:T(1,128)S(1)}, s32[1,256]{1,0:T(1,128)}, u32[]{:S(2)}) copy-start(s32[1,256]{1,0:T(1,128)} %tokens.3) | copy-start | bytes 3076
  39.6 4.7 %collective-permute-start.10 = (bf16[128,1024]{1,0:T(8,128)(2,1)S(1)}, bf16[128,1024]{1,0:T(8,128)(2,1)S(1)}, u32[]{:S(2)}, u32[]{:S(2)}) collective-permute-start(bf16[128,1024]{1,0:T(8,128)(2,1)S(1)} %collective-permute-done.refs_5_), channel_id=1, source_target_pairs={{0,1},{1,0},{2,3},{3,2},{4,5},{5,4},{6,7},{7,6},{8,9},{9,8},{10,11... | collective-permute-start | bytes 786440 | tf_op jit(solution)/shard_map/ppermute | solution.py:493
  40.1 4.1 %collective-permute-start.11 = (bf16[128,1024]{1,0:T(8,128)(2,1)S(1)}, bf16[128,1024]{1,0:T(8,128)(2,1)S(1)}, u32[]{:S(2)}, u32[]{:S(2)}) collective-permute-start(bf16[128,1024]{1,0:T(8,128)(2,1)S(1)} %collective-permute-done.8.refs_6_), channel_id=1, source_target_pairs={{0,1},{1,0},{2,3},{3,2},{4,5},{5,4},{6,7},{7,6},{8,9},{9,8},{10,11... | collective-permute-start | bytes 786440 | tf_op jit(solution)/shard_map/ppermute | solution.py:493
  44.3 17.5 %copy-start.3 = (s32[1,256]{1,0:T(1,128)S(1)}, s32[1,256]{1,0:T(1,128)}, u32[]{:S(2)}) copy-start(s32[1,256]{1,0:T(1,128)} %labels.1) | copy-start | bytes 3076
  79.5 6.4 %collective-permute-start.12 = (bf16[8,16384]{1,0:T(8,128)(2,1)S(1)}, bf16[8,16384]{1,0:T(8,128)(2,1)S(1)}, u32[]{:S(2)}, u32[]{:S(2)}) collective-permute-start(bf16[8,16384]{1,0:T(8,128)(2,1)S(1)} %bitcast.14), channel_id=1, source_target_pairs={{0,2},{1,3},{2,0},{3,1},{4,6},{5,7},{6,4},{7,5},{8,10},{9,11},{10,... | collective-permute-start | bytes 786440 | tf_op jit(solution)/shard_map/ppermute | solution.py:493
  81.3 4.7 %collective-permute-start.13 = (bf16[8,16384]{1,0:T(8,128)(2,1)S(1)}, bf16[8,16384]{1,0:T(8,128)(2,1)S(1)}, u32[]{:S(2)}, u32[]{:S(2)}) collective-permute-start(bf16[8,16384]{1,0:T(8,128)(2,1)S(1)} %bitcast.15), channel_id=1, source_target_pairs={{0,1},{1,0},{2,3},{3,2},{4,5},{5,4},{6,7},{7,6},{8,9},{9,8},{10,11... | collective-permute-start | bytes 786440 | tf_op jit(solution)/shard_map/ppermute | solution.py:493
  85.9 1.5 %collective-permute-start.14 = (bf16[8,16384]{1,0:T(8,128)(2,1)S(1)}, bf16[8,16384]{1,0:T(8,128)(2,1)S(1)}, u32[]{:S(2)}, u32[]{:S(2)}) collective-permute-start(bf16[8,16384]{1,0:T(8,128)(2,1)S(1)} %collective-permute-done.12.refs_1_), channel_id=1, source_target_pairs={{0,1},{1,0},{2,3},{3,2},{4,5},{5,4},{6,7},{7,6},{8,9},{9,8},{10,11... | collective-permute-start | bytes 786440 | tf_op jit(solution)/shard_map/ppermute | solution.py:493
  100.4 6.1 %collective-permute-start.15 = (bf16[32,1024]{1,0:T(8,128)(2,1)S(1)}, bf16[32,1024]{1,0:T(8,128)(2,1)S(1)}, u32[]{:S(2)}, u32[]{:S(2)}) collective-permute-start(bf16[32,1024]{1,0:T(8,128)(2,1)S(1)} %convert_element_type.47), channel_id=1, source_target_pairs={{0,4},{4,0},{8,12},{12,8},{16,20},{20,16},{24,28},{28,24},{1,5},{5... | collective-permute-start | bytes 196616 | tf_op jit(solution)/shard_map/ppermute | solution.py:493
  106.6 4.9 %collective-permute-start.16 = (bf16[32,1024]{1,0:T(8,128)(2,1)S(1)}, bf16[32,1024]{1,0:T(8,128)(2,1)S(1)}, u32[]{:S(2)}, u32[]{:S(2)}) collective-permute-start(bf16[32,1024]{1,0:T(8,128)(2,1)S(1)} %fusion.6), channel_id=1, source_target_pairs={{0,8},{4,12},{8,0},{12,4},{16,24},{20,28},{24,16},{28,20},{1,9},{5... | collective-permute-start | bytes 196616 | tf_op jit(solution)/shard_map/ppermute | solution.py:493
  111.5 8.8 %collective-permute-start.17 = (bf16[32,1024]{1,0:T(8,128)(2,1)S(1)}, bf16[32,1024]{1,0:T(8,128)(2,1)S(1)}, u32[]{:S(2)}, u32[]{:S(2)}) collective-permute-start(bf16[32,1024]{1,0:T(8,128)(2,1)S(1)} %get-tuple-element.71), channel_id=1, source_target_pairs={{0,16},{4,20},{8,24},{12,28},{16,0},{20,4},{24,8},{28,12},{1,17},{... | collective-permute-start | bytes 196616 | tf_op jit(solution)/shard_map/ppermute | solution.py:493

commit v4 on v3

--- a/solution.py
+++ b/solution.py
@@ -422,25 +422,32 @@
 def grad_kernel(width, first, count, hidden_t, *refs):
     parts = refs[:-3] if first == 0 else refs[:-4]
     out, held, sems = refs[-3:]
-    slots = held.shape[0]
-
-    def copy(index):
-        slot = index % slots
-        return pltpu.make_async_copy(held.at[slot], out.at[:, span(first + index, width)], sems.at[slot])
+    slots, depth, _ = held.shape
+    bands = sems.shape[1]
+    tall = depth // bands
+
+    def copy(index, band):
+        slot, rows = index % slots, pl.ds(band * tall, tall)
+        return pltpu.make_async_copy(held.at[slot, rows], out.at[rows, span(first + index, width)], sems.at[slot, band])
 
     @pl.loop(0, count)
     def _(index):
+        piece = stacked([part.at[:, span(first + index, width)] for part in parts])
+
         @pl.when(index >= slots)
         def _():
-            copy(index - slots).wait()
-
-        piece = stacked([part.at[:, span(first + index, width)] for part in parts])
-        held[index % slots] = dot(hidden_t[...], piece, NN).astype(BF16)
-        copy(index).start()
+            for band in range(bands):
+                copy(index - slots, band).wait()
+
+        for band in range(bands):
+            rows = pl.ds(band * tall, tall)
+            held[index % slots, rows, :] = dot(hidden_t[rows, :], piece, NN).astype(BF16)
+            copy(index, band).start()
 
     @pl.loop(max(0, count - slots), count)
     def _(index):
-        copy(index).wait()
+        for band in range(bands):
+            copy(index, band).wait()
 
 
 def grad(hidden_t, parts, calls):
@@ -460,7 +467,7 @@
             in_specs=[whole] * (1 + len(parts)) + [anywhere] * later,
             out_specs=anywhere,
             out_shape=jax.ShapeDtypeStruct((depth, columns), BF16),
-            scratch_shapes=[pltpu.VMEM((min(4, count), depth, width), BF16), pltpu.SemaphoreType.DMA((min(4, count),))],
+            scratch_shapes=[pltpu.VMEM((min(4, count), depth, width), BF16), pltpu.SemaphoreType.DMA((min(4, count), 2))],
             input_output_aliases={1 + len(parts): 0} if later else {},
             compiler_params=pltpu.CompilerParams(vmem_limit_bytes=16 * 1024 * 1024),
             cost_estimate=pl.CostEstimate(flops=16 * rows * depth * width * count, bytes_accessed=2 * depth * width * count, transcendentals=0),

time: 122 us -> 121 us (level)
  transfers between devices with their start and end apart: 18 -> 18, of which waited for: 6 -> 6; matrix products, arithmetic and copies ran while one was open for 2% -> 2% of each run, Pallas kernels for 26% -> 25%
where the time goes in v4:
time: 121 us
  Pallas kernels  54.2 us (45%)
  blocking collectives  25.3 us (21%)
  waiting for transfers between devices  21.5 us (18%)
  starting transfers between devices  14.8 us (12%)
  other arithmetic  3.91 us (3%)
    ppermute x18, waiting for transfers between devices, swap(): return lax.ppermute(value, axis, [(i, i ^ 1 << bit) for i in range(size)])  21.5 us
    ppermute x18, starting transfers between devices, swap(): return lax.ppermute(value, axis, [(i, i ^ 1 << bit) for i in range(size)])  14.8 us
    pallas_call x3, Pallas kernels, grad(): pl.pallas_call(functools.partial(grad_kernel, width, edges[call], count),...  14.1 us
    all_to_all x1, blocking collectives, steps(): owned = lax.all_to_all(own, 'head', split_axis=0, concat_axis=0, tiled=True)  13.8 us
    pallas_call x1, Pallas kernels, back(): pl.pallas_call(functools.partial(back_kernel, width), in_specs=[pl.BlockS...  12.9 us
    all_to_all x1, blocking collectives, steps(): lax.all_to_all(deltas.reshape(own.shape), 'head', split_axis=0, concat_ax...  11.5 us
    pallas_call x1, Pallas kernels, forward(): first(place, row_values, matrices, w)  7.22 us
    pallas_call x1, Pallas kernels, forward(): pairs.append(later(hidden, w))  6.76 us
  transfers between devices with their start and end apart: 18, of which 6 were waited for; matrix products, arithmetic and copies ran while one was open for 2% of the time, Pallas kernels for 25%

profile of v4, /device:TPU:0, one launch (start us, length us, event | category | flops | bytes accessed | tf_op | source)
XLA Modules:
  0.0 120.9 jit_solution(4445742727946770249)
XLA Ops:
  0.6 0.0 copy-start.4
  0.6 1.3 %fusion.8 = (bf16[128,1024]{1,0:T(8,128)(2,1)S(1)}, bf16[128,1024]{1,0:T(8,128)(2,1)S(1)}, bf16[128,1024]{1,0:T(8,128)(2,1)S(1)}) fusion(bf16[256,1024]{1,0:T(8,128)(2,1)} %refs_0_.3, bf16[256,1024]{1,0:T(8,128)(2,1)} %refs_1_.3, pred[]{:T(512)S(6)} %eq.3), kind=kLoop, calls=%fused_computation.23 | loop fusion | flops 131072 | bytes 1835009 | tf_op jit(solution)/shard_map/slice | solution.py:520
  2.0 3.1 %collective-permute-start = (bf16[128,1024]{1,0:T(8,128)(2,1)S(1)}, bf16[128,1024]{1,0:T(8,128)(2,1)S(1)}, u32[]{:S(2)}, u32[]{:S(2)}) collective-permute-start(bf16[128,1024]{1,0:T(8,128)(2,1)S(1)} %get-tuple-element.74), channel_id=1, source_target_pairs={{0,2},{1,3},{2,0},{3,1},{4,6},{5,7},{6,4},{7,5},{8,10},{9,11},{10,... | collective-permute-start | bytes 786440 | tf_op jit(solution)/shard_map/ppermute | solution.py:500
  5.0 0.7 convert_element_type.40
  5.7 0.7 pad_maximum_fusion.2
  6.4 0.1 pad_add_fusion.place
  6.4 0.0 copy-done.4
  6.4 0.9 fusion.1.matrices
  7.3 7.2 %factors.2 = (f32[16,8192]{1,0:T(8,128)S(1)}, bf16[16,8192]{1,0:T(8,128)(2,1)S(1)}, bf16[32,1024]{1,0:T(8,128)(2,1)S(1)}, bf16[1024,32]{1,0:T(8,128)(2,1)S(1)}, ...) custom-call(s32[2]{0:T(128)S(1)} %pad_add_fusion.place, f32[1,1056]{1,0:T(1,128)S(1)} %reshape.24.row_values, ...), custom_call_target="tpu_custom_call" | custom-call | flops 8589934592 | bytes 16777216 | tf_op jit(solution)/shard_map/factors/pallas_call | solution.py:144
  14.6 0.0 copy-start
  14.6 0.0 copy-start.1
  14.6 6.8 %factors.3 = (f32[16,8192]{1,0:T(8,128)S(1)}, bf16[16,8192]{1,0:T(8,128)(2,1)S(1)}) custom-call(bf16[32,1024]{1,0:T(8,128)(2,1)S(1)} %get-tuple-element.42.hidden, bf16[1024,16384]{1,0:T(8,128)(2,1)} %w.5), custom_call_target="tpu_custom_call" | custom-call | flops 8589934592 | bytes 16777216 | tf_op jit(solution)/shard_map/factors/pallas_call | solution.py:154
  21.4 0.1 collective-permute-start.3
  21.4 0.0 copy-done
  21.4 0.5 collective-permute-start.5
  21.9 0.1 collective-permute-start.6
  22.1 0.1 collective-permute-start.7
  22.1 0.0 collective-permute-done.refs_5_
  22.2 0.5 collective-permute-start.1
  22.6 0.3 collective-permute-done.3
  23.0 0.1 convert_add_fusion
  23.0 1.4 %collective-permute-start.4 = (bf16[8,8192]{1,0:T(8,128)(2,1)S(1)}, bf16[8,8192]{1,0:T(8,128)(2,1)S(1)}, u32[]{:S(2)}, u32[]{:S(2)}) collective-permute-start(bf16[8,8192]{1,0:T(8,128)(2,1)S(1)} %slice.56), channel_id=1, source_target_pairs={{0,2},{1,3},{2,0},{3,1},{4,6},{5,7},{6,4},{7,5},{8,10},{9,11},{10,... | collective-permute-start | bytes 393224 | tf_op jit(solution)/shard_map/ppermute | solution.py:500
  24.5 0.4 collective-permute-done.1
  24.8 1.5 %collective-permute-start.8 = (bf16[128,1024]{1,0:T(8,128)(2,1)S(1)}, bf16[128,1024]{1,0:T(8,128)(2,1)S(1)}, u32[]{:S(2)}, u32[]{:S(2)}) collective-permute-start(bf16[128,1024]{1,0:T(8,128)(2,1)S(1)} %collective-permute-done.refs_5_), channel_id=1, source_target_pairs={{0,4},{4,0},{8,12},{12,8},{16,20},{20,16},{24,28},{28,24},{1,5},{5... | collective-permute-start | bytes 786440 | tf_op jit(solution)/shard_map/ppermute | solution.py:500
  26.3 0.1 convert_add_fusion.1
  26.4 12.8 %collective-permute-done.4 = bf16[8,8192]{1,0:T(8,128)(2,1)S(1)} collective-permute-done((bf16[8,8192]{1,0:T(8,128)(2,1)S(1)}, bf16[8,8192]{1,0:T(8,128)(2,1)S(1)}, u32[]{:S(2)}, u32[]{:S(2)}) %collective-permute-start.4) | collective-permute-done | bytes 131104 | tf_op jit(solution)/shard_map/ppermute | solution.py:500
  39.2 0.3 collective-permute-start.2
  39.5 0.0 collective-permute-done.7.refs_4_
  39.5 0.0 collective-permute-start.9
  39.5 0.0 copy-start.2
  39.6 0.0 collective-permute-done.5.refs_2_
  39.6 0.6 collective-permute-start.10
  40.1 0.0 collective-permute-done.8.refs_6_
  40.1 0.1 collective-permute-start.11
  40.2 0.0 collective-permute-done.6.refs_3_
  40.2 2.1 %prepare_near.1 = (f32[256,256]{1,0:T(8,128)S(1)}, f32[256,256]{1,0:T(8,128)S(1)}, f32[256,256]{1,0:T(8,128)S(1)}, bf16[256,2048]{1,0:T(8,128)(2,1)S(1)}) custom-call(bf16[256,1024]{1,0:T(8,128)(2,1)S(1)} %copy-done, bf16[256,1024]{1,0:T(8,128)(2,1)S(1)} %copy-done.1, bf16[256,1024]{1,0:T(8,128)(2,1)S(1)} %collective-permute-done.5.refs_2_, ...), custom_call_target="tpu_custom_call" | custom-call | flops 1073741824 | bytes 4194304 | tf_op jit(solution)/shard_map/prepare_near/pallas_call | solution.py:250
  42.4 1.8 %collective-permute-done.2 = bf16[8,8192]{1,0:T(8,128)(2,1)S(1)} collective-permute-done((bf16[8,8192]{1,0:T(8,128)(2,1)S(1)}, bf16[8,8192]{1,0:T(8,128)(2,1)S(1)}, u32[]{:S(2)}, u32[]{:S(2)}) %collective-permute-start.2) | collective-permute-done | bytes 131104 | tf_op jit(solution)/shard_map/ppermute | solution.py:500
  44.3 0.0 collective-permute-done.10.refs_8_
  44.3 0.0 collective-permute-done.11.refs_9_
  44.3 0.0 collective-permute-done.9.refs_7_
  44.3 0.0 copy-done.2
  44.3 0.0 copy-start.3
  44.3 3.7 %prepare.1 = (bf16[256,4096]{1,0:T(8,128)(2,1)S(1)}, bf16[256,4096]{1,0:T(8,128)(2,1)S(1)}, bf16[256,4096]{1,0:T(8,128)(2,1)S(1)}, f32[256,256]{1,0:T(8,128)S(1)...) custom-call(s32[2]{0:T(128)S(1)} %pad_add_fusion.place, ...), custom_call_target="tpu_custom_call" | custom-call | flops 1073741824 | bytes 8388608 | tf_op jit(solution)/shard_map/prepare/pallas_call | solution.py:269
  48.0 13.8 %all_to_all.10 = bf16[8,128,128]{2,1,0:T(8,128)(2,1)S(1)} all-to-all(bf16[8,128,128]{2,1,0:T(8,128)(2,1)S(1)} %pad_maximum_fusion.1), channel_id=1, replica_groups=mesh['head'=8,'client'=4] {'head'}, dimensions={0} | all-to-all | bytes 524288 | tf_op jit(solution)/shard_map/all_to_all | solution.py:548
  61.8 6.0 %train.1 = (bf16[1024,128]{1,0:T(8,128)(2,1)S(1)}, f32[1,128]{1,0:T(1,128)}) custom-call(bf16[1024,128]{1,0:T(8,128)(2,1)S(1)} %bitcast.20, s32[1,256]{1,0:T(1,128)S(1)} %copy-done.2, s32[1,256]{1,0:T(1,128)S(1)} %copy-done.3, bf16[256,4096]{1,0:T(8,128)(2,1)S(1)} %get-tuple-element.59.byte_full, bf16[256,4096]{1,0:T(8,128)(2,1)S(1)} %get-tuple-element.60.out_full, ...), custom_call_target="tpu_custom_call" | custom-call | flops 2147483648 | bytes 8388608 | tf_op jit(solution)/shard_map/train/pallas_call | solution.py:363
  67.8 11.5 %all_to_all.11 = bf16[8,128,128]{2,1,0:T(8,128)(2,1)S(1)} all-to-all(bf16[8,128,128]{2,1,0:T(8,128)(2,1)S(1)} %bitcast.21), channel_id=1, replica_groups=mesh['head'=8,'client'=4] {'head'}, dimensions={0} | all-to-all | bytes 524288 | tf_op jit(solution)/shard_map/all_to_all | solution.py:550
  79.3 0.2 copy.21
  79.5 1.8 %collective-permute-start.12 = (bf16[8,16384]{1,0:T(8,128)(2,1)S(1)}, bf16[8,16384]{1,0:T(8,128)(2,1)S(1)}, u32[]{:S(2)}, u32[]{:S(2)}) collective-permute-start(bf16[8,16384]{1,0:T(8,128)(2,1)S(1)} %bitcast.14), channel_id=1, source_target_pairs={{0,2},{1,3},{2,0},{3,1},{4,6},{5,7},{6,4},{7,5},{8,10},{9,11},{10,... | collective-permute-start | bytes 786440 | tf_op jit(solution)/shard_map/ppermute | solution.py:500
  81.3 0.0 collective-permute-start.13
  81.3 4.7 %collective-permute-done.12.refs_1_ = bf16[8,16384]{1,0:T(8,128)(2,1)S(1)} collective-permute-done((bf16[8,16384]{1,0:T(8,128)(2,1)S(1)}, bf16[8,16384]{1,0:T(8,128)(2,1)S(1)}, u32[]{:S(2)}, u32[]{:S(2)}) %collective-permute-start.12) | collective-permute-done | bytes 262176 | tf_op jit(solution)/shard_map/ppermute | solution.py:500
  85.9 0.0 collective-permute-start.14
  85.9 0.0 collective-permute-done.13.refs_2_
  85.9 1.5 %collective-permute-done.14.refs_3_ = bf16[8,16384]{1,0:T(8,128)(2,1)S(1)} collective-permute-done((bf16[8,16384]{1,0:T(8,128)(2,1)S(1)}, bf16[8,16384]{1,0:T(8,128)(2,1)S(1)}, u32[]{:S(2)}, u32[]{:S(2)}) %collective-permute-start.14) | collective-permute-done | bytes 262176 | tf_op jit(solution)/shard_map/ppermute | solution.py:500
  87.5 12.9 %hidden_back.1 = f32[32,1024]{1,0:T(8,128)S(1)} custom-call(bf16[1024,16384]{1,0:T(8,128)(2,1)} %w.5, bf16[8,16384]{1,0:T(8,128)(2,1)S(1)} %bitcast.16, bf16[8,16384]{1,0:T(8,128)(2,1)S(1)} %collective-permute-done.12.refs_1_, bf16[8,16384]{1,0:T(8,128)(2,1)S(1)} %collective-permute-done.13.refs_2_, bf16[8,16384]{1,0:T(8,128)(2,1)S(1)} %collective-permute-done.14.refs_3_), custom_call_target="tpu_custom_call" | custom-call | flops 8589934592 | bytes 33554432 | tf_op jit(solution)/shard_map/hidden_back/pallas_call | solution.py:410
  100.4 1.4 %collective-permute-start.15 = (bf16[32,1024]{1,0:T(8,128)(2,1)S(1)}, bf16[32,1024]{1,0:T(8,128)(2,1)S(1)}, u32[]{:S(2)}, u32[]{:S(2)}) collective-permute-start(bf16[32,1024]{1,0:T(8,128)(2,1)S(1)} %convert_element_type.47), channel_id=1, source_target_pairs={{0,4},{4,0},{8,12},{12,8},{16,20},{20,16},{24,28},{28,24},{1,5},{5... | collective-permute-start | bytes 196616 | tf_op jit(solution)/shard_map/ppermute | solution.py:500
  101.8 4.5 %head_grad.3.refs_4_ = bf16[1024,16384]{1,0:T(8,128)(2,1)} custom-call(bf16[1024,32]{1,0:T(8,128)(2,1)S(1)} %get-tuple-element.37.hidden_t, bf16[8,16384]{1,0:T(8,128)(2,1)S(1)} %bitcast.17, bf16[8,16384]{1,0:T(8,128)(2,1)S(1)} %collective-permute-done.12.refs_1_, bf16[8,16384]{1,0:T(8,128)(2,1)S(1)} %collective-permute-done.13.refs_2_, ...), custom_call_target="tpu_custom_call" | custom-call | flops 2684354560 | bytes 10485760 | tf_op jit(solution)/shard_map/head_grad/pallas_call | solution.py:465
  106.3 0.0 collective-permute-done.15
  106.3 0.1 collective-permute-start.16
  106.4 4.5 %head_grad.4.refs_4_ = bf16[1024,16384]{1,0:T(8,128)(2,1)} custom-call(bf16[1024,32]{1,0:T(8,128)(2,1)S(1)} %get-tuple-element.37.hidden_t, bf16[8,16384]{1,0:T(8,128)(2,1)S(1)} %bitcast.18, bf16[8,16384]{1,0:T(8,128)(2,1)S(1)} %collective-permute-done.12.refs_1_, ...), custom_call_target="tpu_custom_call", output_to_operand_aliasing={{}: (5, {})} | custom-call | flops 2684354560 | bytes 10485760 | tf_op jit(solution)/shard_map/head_grad/pallas_call | solution.py:465
  110.9 0.0 collective-permute-done.16
  111.0 3.4 %collective-permute-start.17 = (bf16[32,1024]{1,0:T(8,128)(2,1)S(1)}, bf16[32,1024]{1,0:T(8,128)(2,1)S(1)}, u32[]{:S(2)}, u32[]{:S(2)}) collective-permute-start(bf16[32,1024]{1,0:T(8,128)(2,1)S(1)} %get-tuple-element.71), channel_id=1, source_target_pairs={{0,16},{4,20},{8,24},{12,28},{16,0},{20,4},{24,8},{28,12},{1,17},{... | collective-permute-start | bytes 196616 | tf_op jit(solution)/shard_map/ppermute | solution.py:500
  114.3 5.2 %head_grad.5 = bf16[1024,16384]{1,0:T(8,128)(2,1)} custom-call(bf16[1024,32]{1,0:T(8,128)(2,1)S(1)} %get-tuple-element.37.hidden_t, bf16[8,16384]{1,0:T(8,128)(2,1)S(1)} %bitcast.19, bf16[8,16384]{1,0:T(8,128)(2,1)S(1)} %collective-permute-done.12.refs_1_, bf16[8,16384]{1,0:T(8,128)(2,1)S(1)} %collective-permute-done.13.refs_2_, ...), custom_call_target="tpu_custom_call", output_to_operand_aliasing={{}: (5, {})} | custom-call | flops 3221225472 | bytes 12582912 | tf_op jit(solution)/shard_map/head_grad/pallas_call | solution.py:465
  119.5 0.0 collective-permute-done.17.other
  119.5 1.4 %in_grad.1 = f32[256,1024]{1,0:T(8,128)} custom-call(bf16[256,32]{1,0:T(8,128)(2,1)S(1)} %get-tuple-element.68.chosen_t, f32[32,1024]{1,0:T(8,128)S(1)} %get-tuple-element.69.preact, f32[32,1024]{1,0:T(8,128)S(1)} %get-tuple-element.72.mine, bf16[32,1024]{1,0:T(8,128)(2,1)S(1)} %collective-permute-done.17.other), custom_call_target="tpu_custom_call" | custom-call | tf_op jit(solution)/shard_map/in_grad/pallas_call | solution.py:488
  (14 shorter events, 0.3 us)
Async XLA Ops:
  0.6 5.8 %copy-start.4 = (bf16[256,1024]{1,0:T(8,128)(2,1)S(1)}, bf16[256,1024]{1,0:T(8,128)(2,1)}, u32[]{:S(2)}) copy-start(bf16[256,1024]{1,0:T(8,128)(2,1)} %param.11) | copy-start | bytes 1572868
  2.0 20.2 %collective-permute-start = (bf16[128,1024]{1,0:T(8,128)(2,1)S(1)}, bf16[128,1024]{1,0:T(8,128)(2,1)S(1)}, u32[]{:S(2)}, u32[]{:S(2)}) collective-permute-start(bf16[128,1024]{1,0:T(8,128)(2,1)S(1)} %get-tuple-element.74), channel_id=1, source_target_pairs={{0,2},{1,3},{2,0},{3,1},{4,6},{5,7},{6,4},{7,5},{8,10},{9,11},{10,... | collective-permute-start | bytes 786440 | tf_op jit(solution)/shard_map/ppermute | solution.py:500
  14.6 6.9 %copy-start = (bf16[256,1024]{1,0:T(8,128)(2,1)S(1)}, bf16[256,1024]{1,0:T(8,128)(2,1)}, u32[]{:S(2)}) copy-start(bf16[256,1024]{1,0:T(8,128)(2,1)} %refs_0_.3) | copy-start | bytes 1572868
  14.6 7.4 %copy-start.1 = (bf16[256,1024]{1,0:T(8,128)(2,1)S(1)}, bf16[256,1024]{1,0:T(8,128)(2,1)}, u32[]{:S(2)}) copy-start(bf16[256,1024]{1,0:T(8,128)(2,1)} %refs_1_.3) | copy-start | bytes 1572868
  21.4 1.6 %collective-permute-start.3 = (bf16[16,8192]{1,0:T(8,128)(2,1)S(1)}, bf16[16,8192]{1,0:T(8,128)(2,1)S(1)}, u32[]{:S(2)}, u32[]{:S(2)}) collective-permute-start(bf16[16,8192]{1,0:T(8,128)(2,1)S(1)} %get-tuple-element.44), channel_id=1, source_target_pairs={{0,1},{1,0},{2,3},{3,2},{4,5},{5,4},{6,7},{7,6},{8,9},{9,8},{10,11... | collective-permute-start | bytes 786440 | tf_op jit(solution)/shard_map/ppermute | solution.py:500
  21.4 18.1 %collective-permute-start.5 = (bf16[256,1024]{1,0:T(8,128)(2,1)S(1)}, bf16[256,1024]{1,0:T(8,128)(2,1)S(1)}, u32[]{:S(2)}, u32[]{:S(2)}) collective-permute-start(bf16[256,1024]{1,0:T(8,128)(2,1)S(1)} %copy-done), channel_id=1, source_target_pairs={{0,1},{1,0},{2,3},{3,2},{4,5},{5,4},{6,7},{7,6},{8,9},{9,8},{10,11... | collective-permute-start | bytes 1572872 | tf_op jit(solution)/shard_map/ppermute | solution.py:500
  21.9 18.3 %collective-permute-start.6 = (bf16[256,1024]{1,0:T(8,128)(2,1)S(1)}, bf16[256,1024]{1,0:T(8,128)(2,1)S(1)}, u32[]{:S(2)}, u32[]{:S(2)}) collective-permute-start(bf16[256,1024]{1,0:T(8,128)(2,1)S(1)} %copy-done.1), channel_id=1, source_target_pairs={{0,1},{1,0},{2,3},{3,2},{4,5},{5,4},{6,7},{7,6},{8,9},{9,8},{10,11... | collective-permute-start | bytes 1572872 | tf_op jit(solution)/shard_map/ppermute | solution.py:500
  22.1 17.4 %collective-permute-start.7 = (bf16[256,1024]{1,0:T(8,128)(2,1)S(1)}, bf16[256,1024]{1,0:T(8,128)(2,1)S(1)}, u32[]{:S(2)}, u32[]{:S(2)}) collective-permute-start(bf16[256,1024]{1,0:T(8,128)(2,1)S(1)} %pad_maximum_fusion), channel_id=1, source_target_pairs={{0,2},{1,3},{2,0},{3,1},{4,6},{5,7},{6,4},{7,5},{8,10},{9,11},{10,... | collective-permute-start | bytes 1572872 | tf_op jit(solution)/shard_map/ppermute | solution.py:500
  22.2 2.7 %collective-permute-start.1 = (bf16[16,8192]{1,0:T(8,128)(2,1)S(1)}, bf16[16,8192]{1,0:T(8,128)(2,1)S(1)}, u32[]{:S(2)}, u32[]{:S(2)}) collective-permute-start(bf16[16,8192]{1,0:T(8,128)(2,1)S(1)} %get-tuple-element.41), channel_id=1, source_target_pairs={{0,1},{1,0},{2,3},{3,2},{4,5},{5,4},{6,7},{7,6},{8,9},{9,8},{10,11... | collective-permute-start | bytes 786440 | tf_op jit(solution)/shard_map/ppermute | solution.py:500
  23.0 16.1 %collective-permute-start.4 = (bf16[8,8192]{1,0:T(8,128)(2,1)S(1)}, bf16[8,8192]{1,0:T(8,128)(2,1)S(1)}, u32[]{:S(2)}, u32[]{:S(2)}) collective-permute-start(bf16[8,8192]{1,0:T(8,128)(2,1)S(1)} %slice.56), channel_id=1, source_target_pairs={{0,2},{1,3},{2,0},{3,1},{4,6},{5,7},{6,4},{7,5},{8,10},{9,11},{10,... | collective-permute-start | bytes 393224 | tf_op jit(solution)/shard_map/ppermute | solution.py:500
  24.8 15.3 %collective-permute-start.8 = (bf16[128,1024]{1,0:T(8,128)(2,1)S(1)}, bf16[128,1024]{1,0:T(8,128)(2,1)S(1)}, u32[]{:S(2)}, u32[]{:S(2)}) collective-permute-start(bf16[128,1024]{1,0:T(8,128)(2,1)S(1)} %collective-permute-done.refs_5_), channel_id=1, source_target_pairs={{0,4},{4,0},{8,12},{12,8},{16,20},{20,16},{24,28},{28,24},{1,5},{5... | collective-permute-start | bytes 786440 | tf_op jit(solution)/shard_map/ppermute | solution.py:500
  39.2 5.0 %collective-permute-start.2 = (bf16[8,8192]{1,0:T(8,128)(2,1)S(1)}, bf16[8,8192]{1,0:T(8,128)(2,1)S(1)}, u32[]{:S(2)}, u32[]{:S(2)}) collective-permute-start(bf16[8,8192]{1,0:T(8,128)(2,1)S(1)} %slice.57), channel_id=1, source_target_pairs={{0,2},{1,3},{2,0},{3,1},{4,6},{5,7},{6,4},{7,5},{8,10},{9,11},{10,... | collective-permute-start | bytes 393224 | tf_op jit(solution)/shard_map/ppermute | solution.py:500
  39.5 4.8 %collective-permute-start.9 = (bf16[256,1024]{1,0:T(8,128)(2,1)S(1)}, bf16[256,1024]{1,0:T(8,128)(2,1)S(1)}, u32[]{:S(2)}, u32[]{:S(2)}) collective-permute-start(bf16[256,1024]{1,0:T(8,128)(2,1)S(1)} %collective-permute-done.7.refs_4_), channel_id=1, source_target_pairs={{0,1},{1,0},{2,3},{3,2},{4,5},{5,4},{6,7},{7,6},{8,9},{9,8},{10,11... | collective-permute-start | bytes 1572872 | tf_op jit(solution)/shard_map/ppermute | solution.py:500
  39.5 4.7 %copy-start.2 = (s32[1,256]{1,0:T(1,128)S(1)}, s32[1,256]{1,0:T(1,128)}, u32[]{:S(2)}) copy-start(s32[1,256]{1,0:T(1,128)} %tokens.3) | copy-start | bytes 3076
  39.6 4.7 %collective-permute-start.10 = (bf16[128,1024]{1,0:T(8,128)(2,1)S(1)}, bf16[128,1024]{1,0:T(8,128)(2,1)S(1)}, u32[]{:S(2)}, u32[]{:S(2)}) collective-permute-start(bf16[128,1024]{1,0:T(8,128)(2,1)S(1)} %collective-permute-done.refs_5_), channel_id=1, source_target_pairs={{0,1},{1,0},{2,3},{3,2},{4,5},{5,4},{6,7},{7,6},{8,9},{9,8},{10,11... | collective-permute-start | bytes 786440 | tf_op jit(solution)/shard_map/ppermute | solution.py:500
  40.1 4.1 %collective-permute-start.11 = (bf16[128,1024]{1,0:T(8,128)(2,1)S(1)}, bf16[128,1024]{1,0:T(8,128)(2,1)S(1)}, u32[]{:S(2)}, u32[]{:S(2)}) collective-permute-start(bf16[128,1024]{1,0:T(8,128)(2,1)S(1)} %collective-permute-done.8.refs_6_), channel_id=1, source_target_pairs={{0,1},{1,0},{2,3},{3,2},{4,5},{5,4},{6,7},{7,6},{8,9},{9,8},{10,11... | collective-permute-start | bytes 786440 | tf_op jit(solution)/shard_map/ppermute | solution.py:500
  44.3 17.5 %copy-start.3 = (s32[1,256]{1,0:T(1,128)S(1)}, s32[1,256]{1,0:T(1,128)}, u32[]{:S(2)}) copy-start(s32[1,256]{1,0:T(1,128)} %labels.1) | copy-start | bytes 3076
  79.5 6.4 %collective-permute-start.12 = (bf16[8,16384]{1,0:T(8,128)(2,1)S(1)}, bf16[8,16384]{1,0:T(8,128)(2,1)S(1)}, u32[]{:S(2)}, u32[]{:S(2)}) collective-permute-start(bf16[8,16384]{1,0:T(8,128)(2,1)S(1)} %bitcast.14), channel_id=1, source_target_pairs={{0,2},{1,3},{2,0},{3,1},{4,6},{5,7},{6,4},{7,5},{8,10},{9,11},{10,... | collective-permute-start | bytes 786440 | tf_op jit(solution)/shard_map/ppermute | solution.py:500
  81.3 4.7 %collective-permute-start.13 = (bf16[8,16384]{1,0:T(8,128)(2,1)S(1)}, bf16[8,16384]{1,0:T(8,128)(2,1)S(1)}, u32[]{:S(2)}, u32[]{:S(2)}) collective-permute-start(bf16[8,16384]{1,0:T(8,128)(2,1)S(1)} %bitcast.15), channel_id=1, source_target_pairs={{0,1},{1,0},{2,3},{3,2},{4,5},{5,4},{6,7},{7,6},{8,9},{9,8},{10,11... | collective-permute-start | bytes 786440 | tf_op jit(solution)/shard_map/ppermute | solution.py:500
  85.9 1.5 %collective-permute-start.14 = (bf16[8,16384]{1,0:T(8,128)(2,1)S(1)}, bf16[8,16384]{1,0:T(8,128)(2,1)S(1)}, u32[]{:S(2)}, u32[]{:S(2)}) collective-permute-start(bf16[8,16384]{1,0:T(8,128)(2,1)S(1)} %collective-permute-done.12.refs_1_), channel_id=1, source_target_pairs={{0,1},{1,0},{2,3},{3,2},{4,5},{5,4},{6,7},{7,6},{8,9},{9,8},{10,11... | collective-permute-start | bytes 786440 | tf_op jit(solution)/shard_map/ppermute | solution.py:500
  100.4 5.9 %collective-permute-start.15 = (bf16[32,1024]{1,0:T(8,128)(2,1)S(1)}, bf16[32,1024]{1,0:T(8,128)(2,1)S(1)}, u32[]{:S(2)}, u32[]{:S(2)}) collective-permute-start(bf16[32,1024]{1,0:T(8,128)(2,1)S(1)} %convert_element_type.47), channel_id=1, source_target_pairs={{0,4},{4,0},{8,12},{12,8},{16,20},{20,16},{24,28},{28,24},{1,5},{5... | collective-permute-start | bytes 196616 | tf_op jit(solution)/shard_map/ppermute | solution.py:500
  106.3 4.6 %collective-permute-start.16 = (bf16[32,1024]{1,0:T(8,128)(2,1)S(1)}, bf16[32,1024]{1,0:T(8,128)(2,1)S(1)}, u32[]{:S(2)}, u32[]{:S(2)}) collective-permute-start(bf16[32,1024]{1,0:T(8,128)(2,1)S(1)} %fusion.6), channel_id=1, source_target_pairs={{0,8},{4,12},{8,0},{12,4},{16,24},{20,28},{24,16},{28,20},{1,9},{5... | collective-permute-start | bytes 196616 | tf_op jit(solution)/shard_map/ppermute | solution.py:500
  111.0 8.5 %collective-permute-start.17 = (bf16[32,1024]{1,0:T(8,128)(2,1)S(1)}, bf16[32,1024]{1,0:T(8,128)(2,1)S(1)}, u32[]{:S(2)}, u32[]{:S(2)}) collective-permute-start(bf16[32,1024]{1,0:T(8,128)(2,1)S(1)} %get-tuple-element.71), channel_id=1, source_target_pairs={{0,16},{4,20},{8,24},{12,28},{16,0},{20,4},{24,8},{28,12},{1,17},{... | collective-permute-start | bytes 196616 | tf_op jit(solution)/shard_map/ppermute | solution.py:500
